TPU v7x, 32 devices: a whole 2x2x4 slice. The times are simulated.
32 devices in a mesh: dom: 8 (over z, x), en: 4 (over y, core).
Axes of the slice: x: 2, y: 2, z: 4, core: 2. Of those that a mesh axis runs over, the one named last changes fastest.
Arguments:
- single_site: bfloat16 [4, 2048, 1024], P('en', 'dom'), may hold values from -1 to 1
- coupling: bfloat16 [16, 4, 4225], P('dom'), may hold values from -0.75 to 0.75
- angular: bfloat16 [4, 1024], replicated, may hold values from -1 to 1
- phases: float32 [4, 4], P('en'), may hold values from 0.22 to 0.38
- contour: float32 [4], P('en'), may hold values from 1 to 4
- radial: bfloat16 [4, 1024, 3136], P('en'), may hold values from -0.1875 to 0.1875
- neighbours: int32 [8, 2, 65], replicated, may hold values from 0 to 2047, as said below
- owner_row: int32 [2048], replicated, may hold values from 0 to 2047, as said below
- old_potential: float32 [16, 3136], P('dom'), may hold values from -1 to 1
Outputs:
- potential: float32 [16, 3136], P('dom')
Inputs may be any that keep to these rules, and one draw needn't show every extreme that they name: `neighbours`: each zone lists distinct atoms; no atom appears twice among the 130 entries of one domain's zones. Atom a lies in row owner_row[a], which belongs to domain owner_row[a] // 256; every zone's central atom belongs to the zone's own domain, and every listed atom to a domain within 2 of it along dom, counted cyclically. At most 48 entries of one domain's zones belong to any one domain; the domain itself holds exactly 48 of them, and so does one other domain. `owner_row`: A permutation of the atoms.
All inputs are finite; a program needn't handle non-finite values.
Results may differ from a plain program's by a relative error of at most 0.0029.
Values may be sent and summed in bfloat16 or wider, within the bound.
No kernel may reach another device: no remote copies, remote signals or barrier semaphores. Data moves between devices by JAX's collectives and lax.ppermute only.
A program may use at most 64 MiB of HBM per device.

v0:
```python
import jax
import jax.numpy as jnp
from jax import lax
from jax.sharding import PartitionSpec as P

BLK = 32
ZA = 65
TERMS = 4
ZONES_DEV = 2
REACH = 2
ITERS = 2
CAP = 48


def shifted(block, axis, distance):
    devices = range(lax.axis_size(axis))
    route = [((i - distance) % len(devices), i) for i in devices]
    return lax.ppermute(block, axis, route)


def mixed_potential(previous, density):
    return 0.5 * previous + 0.5 * density * lax.rsqrt(1.0 + density * density)


def shards(
    single_site, coupling, angular, phases, contour, radial, neighbours, owner_row, old_potential
):
    owned_blocks = single_site[0]
    owned_count = owned_blocks.shape[0]
    domain = lax.axis_index("dom")
    domain_count = lax.axis_size("dom")
    entry_total = ZA * ZONES_DEV
    own_lists = lax.dynamic_index_in_dim(neighbours, domain, 0, keepdims=False).reshape(entry_total)
    entry_rows = owner_row[own_lists]
    owners = entry_rows // owned_count
    source_offset = (domain - owners + REACH) % domain_count - REACH
    positions = jnp.arange(entry_total, dtype=jnp.int32)
    earlier = (owners[:, None] == owners[None, :]) & (positions[None, :] < positions[:, None])
    entry_rank = jnp.sum(earlier.astype(jnp.int32), axis=1)
    slot_ids = jnp.arange(CAP, dtype=jnp.int32)
    packs = {}
    for offset in range(-REACH, REACH + 1):
        target = (domain + offset) % domain_count
        target_lists = lax.dynamic_index_in_dim(neighbours, target, 0, keepdims=False).reshape(
            entry_total
        )
        target_rows = owner_row[target_lists]
        is_mine = target_rows // owned_count == domain
        slot_order = jnp.cumsum(is_mine.astype(jnp.int32)) - 1
        chosen = is_mine[None, :] & (slot_order[None, :] == slot_ids[:, None])
        local_index = jnp.sum(
            jnp.where(chosen, target_rows[None, :] - domain * owned_count, 0), axis=1
        )
        filled = jnp.any(chosen, axis=1)
        packs[offset] = jnp.where(
            filled[:, None], owned_blocks[local_index], jnp.zeros((), owned_blocks.dtype)
        )
    pieces = {0: packs[0]}
    for offset in range(-REACH, REACH + 1):
        if offset != 0:
            pieces[offset] = shifted(packs[offset], "dom", offset)
    near_table = jnp.concatenate([pieces[offset] for offset in range(-REACH, REACH + 1)], axis=0)
    entry_index = (source_offset + REACH) * CAP + entry_rank
    site_blocks = near_table[entry_index].reshape(ZONES_DEV, ZA, BLK, BLK)
    scaled = phases[0][None, :, None, None] * coupling.reshape(ZONES_DEV, TERMS, ZA, ZA).astype(
        jnp.float32
    )
    scaled = scaled.transpose(0, 2, 1, 3).astype(jnp.bfloat16).reshape(ZONES_DEV, ZA, TERMS * ZA)
    tables = angular.reshape(TERMS, BLK, BLK)
    start = (
        jnp.zeros((ZONES_DEV, ZA, BLK, BLK), jnp.float32)
        .at[:, 0]
        .set(site_blocks[:, 0].astype(jnp.float32))
    )
    iterate = start
    for repeat in range(ITERS):
        sweep_in = iterate.astype(jnp.bfloat16)
        spread = jnp.einsum(
            "qab,zjbc->zqjac", tables, sweep_in, preferred_element_type=jnp.float32
        ).astype(jnp.bfloat16)
        spread = spread.reshape(ZONES_DEV, TERMS * ZA, BLK * BLK)
        field_sum = jnp.einsum("zik,zkm->zim", scaled, spread, preferred_element_type=jnp.float32)
        field_half = field_sum.astype(jnp.bfloat16).reshape(ZONES_DEV, ZA, BLK, BLK)
        iterate = start + jnp.einsum(
            "ziab,zibc->ziac", site_blocks, field_half, preferred_element_type=jnp.float32
        )
    central = iterate[:, 0].astype(jnp.bfloat16).reshape(ZONES_DEV, BLK * BLK)
    energy_part = contour[0] * jnp.dot(central, radial[0], preferred_element_type=jnp.float32)
    density = lax.psum(energy_part, "en")
    return mixed_potential(old_potential, density)


def solution(mesh):
    return jax.shard_map(
        shards,
        mesh=mesh,
        in_specs=(
            P("en", "dom", None),
            P("dom", None, None),
            P(),
            P("en", None),
            P("en"),
            P("en", None, None),
            P(),
            P(),
            P("dom", None),
        ),
        out_specs=P("dom", None),
        check_vma=False,
    )
```

profile of v0, /device:TPU:0, one launch (start us, length us, event | category | flops | bytes accessed | tf_op | source)
XLA Modules:
  0.0 83.8 jit_solution(823018158614392358)
XLA Ops:
  0.0 0.8 constant_dynamic-slice_fusion
  1.0 1.9 %gather_fusion = s32[130]{0:T(256)S(1)} fusion(s32[2048]{0:T(1024)} %param.18, s32[1024]{0:T(1024)S(1)} %pad_clamp_fusion.11), kind=kCustom, calls=%fused_computation | custom fusion | bytes 1560 | tf_op jit(solution)/shard_map/gather | solution.py:47
  3.0 1.4 %gather_fusion.2 = s32[130]{0:T(256)S(1)} fusion(s32[2048]{0:T(1024)S(1)} %copy-done.1, s32[1024]{0:T(1024)S(1)} %pad_clamp_fusion.9), kind=kCustom, calls=%fused_computation.2 | custom fusion | bytes 1560 | tf_op jit(solution)/shard_map/gather | solution.py:47
  4.5 0.3 reduce-window.41
  5.4 0.7 gather_fusion.1
  6.1 5.1 %collective-permute-start = (bf16[48,1024]{1,0:T(8,128)(2,1)S(1)}, bf16[48,1024]{1,0:T(8,128)(2,1)S(1)}, u32[]{:S(2)}, u32[]{:S(2)}) collective-permute-start(bf16[48,1024]{1,0:T(8,128)(2,1)S(1)} %broadcast_select_fusion.4), channel_id=1, source_target_pairs={{8,0},{12,4},{16,8},{20,12},{24,16},{28,20},{0,24},{4,28},{9,1},{1... | collective-permute-start | bytes 294920 | tf_op jit(solution)/shard_map/ppermute | solution.py:18
  11.2 0.3 reduce-window.45
  12.1 0.7 gather_fusion.3
  12.9 1.4 %collective-permute-start.1 = (bf16[48,1024]{1,0:T(8,128)(2,1)S(1)}, bf16[48,1024]{1,0:T(8,128)(2,1)S(1)}, u32[]{:S(2)}, u32[]{:S(2)}) collective-permute-start(bf16[48,1024]{1,0:T(8,128)(2,1)S(1)} %broadcast_select_fusion.3), channel_id=1, source_target_pairs={{4,0},{8,4},{12,8},{16,12},{20,16},{24,20},{28,24},{0,28},{5,1},{9... | collective-permute-start | bytes 294920 | tf_op jit(solution)/shard_map/ppermute | solution.py:18
  14.4 1.4 %gather_fusion.6 = s32[130]{0:T(256)S(1)} fusion(s32[2048]{0:T(1024)S(1)} %copy-done.1, s32[1024]{0:T(1024)S(1)} %pad_clamp_fusion.5), kind=kCustom, calls=%fused_computation.6 | custom fusion | bytes 1560 | tf_op jit(solution)/shard_map/gather | solution.py:47
  16.0 1.4 %gather_fusion.8 = s32[130]{0:T(256)S(1)} fusion(s32[2048]{0:T(1024)S(1)} %copy-done.1, s32[1024]{0:T(1024)S(1)} %pad_clamp_fusion.3), kind=kCustom, calls=%fused_computation.8 | custom fusion | bytes 1560 | tf_op jit(solution)/shard_map/gather | solution.py:47
  17.4 0.3 reduce-window.61
  18.3 0.7 gather_fusion.7
  19.1 0.7 collective-permute-start.2
  19.8 0.3 reduce-window.63
  20.7 0.7 gather_fusion.9
  21.5 1.2 %collective-permute-start.3 = (bf16[48,1024]{1,0:T(8,128)(2,1)S(1)}, bf16[48,1024]{1,0:T(8,128)(2,1)S(1)}, u32[]{:S(2)}, u32[]{:S(2)}) collective-permute-start(bf16[48,1024]{1,0:T(8,128)(2,1)S(1)} %broadcast_select_fusion.1), channel_id=1, source_target_pairs={{24,0},{28,4},{0,8},{4,12},{8,16},{12,20},{16,24},{20,28},{25,1},{... | collective-permute-start | bytes 294920 | tf_op jit(solution)/shard_map/ppermute | solution.py:18
  22.7 1.4 %gather_fusion.10 = s32[130]{0:T(256)S(1)} fusion(s32[2048]{0:T(1024)S(1)} %copy-done.1, s32[1024]{0:T(1024)S(1)} %pad_clamp_fusion.1), kind=kCustom, calls=%fused_computation.10 | custom fusion | bytes 1560 | tf_op jit(solution)/shard_map/gather | solution.py:34
  24.2 0.2 convert_reduce_fusion
  24.5 1.4 %gather_fusion.4 = s32[130]{0:T(256)S(1)} fusion(s32[2048]{0:T(1024)S(1)} %copy-done.1, s32[1024]{0:T(1024)S(1)} %pad_clamp_fusion.7), kind=kCustom, calls=%fused_computation.4 | custom fusion | bytes 1560 | tf_op jit(solution)/shard_map/gather | solution.py:47
  26.0 0.3 reduce-window.49
  26.9 0.7 gather_fusion.5
  29.1 0.9 %gather_fusion.11 = bf16[130,1024]{1,0:T(8,128)(2,1)S(1)} fusion(bf16[240,1024]{1,0:T(8,128)(2,1)S(1)} %constant_dynamic-update-slice_fusion, s32[1024]{0:T(1024)S(1)} %pad_clamp_fusion), kind=kCustom, calls=%fused_computation.11 | custom fusion | bytes 533000 | tf_op jit(solution)/shard_map/gather | solution.py:64
  29.9 0.2 copy.67
  30.1 0.3 reshape.660
  30.4 1.1 %copy.84 = bf16[2,65,32,32]{3,2,1,0:T(8,128)(2,1)S(1)} copy(bf16[2,65,32,32]{1,0,3,2:T(2,128)(2,1)S(1)} %reshape.660) | data formatting | bytes 532480 | tf_op jit(solution)/shard_map/reshape | solution.py:64
  31.5 0.4 fusion.6
  32.0 1.0 %convert_bitcast_fusion.1 = bf16[2,4,65,32,32]{2,3,1,4,0:T(8,128)(2,1)S(1)} fusion(bf16[2,65,32,32,1]{1,0,3,2,4:T(2,128)(2,1)S(1)} %fusion.6, bf16[4,32,32,1,1]{2,1,0,3,4:T(8,128)(2,1)S(1)} %reshape.770), kind=kOutput, calls=%fused_computation.16 | convolution fusion | flops 34611200 | bytes 1339392 | tf_op jit(solution)/shard_map/qab,zjbc->zqjac/dot_general | solution.py:78
  33.0 2.4 %copy.70 = bf16[2,4,65,32,32]{2,1,4,3,0:T(4,128)(2,1)} copy(bf16[2,4,65,32,32]{2,3,1,4,0:T(8,128)(2,1)S(1)} %convert_bitcast_fusion.1) | data formatting | bytes 2129920 | tf_op jit(solution)/shard_map/convert_element_type | solution.py:80
  35.4 4.3 %reshape.663 = bf16[2,260,1024]{1,2,0:T(8,128)(2,1)} reshape(bf16[2,4,65,32,32]{2,1,4,3,0:T(4,128)(2,1)} %copy.70) | data formatting | bytes 2129920 | tf_op jit(solution)/shard_map/reshape | solution.py:81
  39.8 2.0 %convolution_convert_fusion.1 = bf16[2,65,1024]{2,1,0:T(8,128)(2,1)S(1)} fusion(bf16[2,65,260]{2,1,0:T(8,128)(2,1)S(1)} %reshape.773, bf16[2,260,1024]{1,2,0:T(8,128)(2,1)} %reshape.663), kind=kOutput, calls=%fused_computation.20 | convolution fusion | flops 69355520 | bytes 1398800 | tf_op jit(solution)/shard_map/zik,zkm->zim/dot_general | solution.py:82
  41.8 1.0 %copy.73 = bf16[2,65,1024]{1,2,0:T(8,128)(2,1)} copy(bf16[2,65,1024]{2,1,0:T(8,128)(2,1)S(1)} %convolution_convert_fusion.1) | data formatting | bytes 532480 | tf_op jit(solution)/shard_map/convert_element_type | solution.py:83
  42.8 2.8 %copy.75 = bf16[2,65,32,32]{3,2,1,0:T(8,128)(2,1)S(1)} copy(bf16[2,65,32,32]{1,3,2,0:T(8,128)(2,1)} %bitcast.98) | data formatting | bytes 532480 | tf_op jit(solution)/shard_map/reshape | solution.py:83
  45.6 1.8 %fusion.42 = f32[2,65,32,32]{3,2,1,0:T(8,128)} fusion(bf16[2,65,32,32]{3,2,1,0:T(8,128)(2,1)S(1)} %copy.84, bf16[2,65,32,32]{3,2,1,0:T(8,128)(2,1)S(1)} %copy.75), kind=kOutput, calls=%fused_computation.169 | convolution fusion | flops 8519680 | bytes 1064960 | tf_op jit(solution)/shard_map/ziab,zibc->ziac/dot_general | solution.py:84
  47.4 2.4 %copy.78 = f32[2,65,32,32]{1,3,2,0:T(8,128)S(1)} copy(f32[2,65,32,32]{3,2,1,0:T(8,128)} %fusion.42) | data formatting | bytes 1064960 | tf_op jit(solution)/shard_map/ziab,zibc->ziac/dot_general | solution.py:84
  49.8 1.1 %convert_add_fusion.1 = f32[2,1,32,32]{1,3,2,0:T(8,128)} fusion(f32[2,65,32,32]{1,3,2,0:T(8,128)S(1)} %copy.78, bf16[2,1,32,32]{1,0,3,2:T(2,128)(2,1)S(1)} %bitcast.96), kind=kLoop, calls=%fused_computation.18 | loop fusion | flops 4096 | bytes 20480 | tf_op jit(solution)/shard_map/scatter | solution.py:73
  51.0 2.8 %add.306 = f32[2,65,32,32]{1,3,2,0:T(8,128)S(1)} dynamic-update-slice(f32[2,65,32,32]{1,3,2,0:T(8,128)S(1)} %copy.78, f32[2,1,32,32]{1,3,2,0:T(8,128)} %convert_add_fusion.1, s32[]{:T(128)} %constant.162.clone.1, s32[]{:T(128)} %constant.162.clone.1, s32[]{:T(128)} %constant.162.clone.1, s32[]{:T(128)} %constant.162.clone.1) | dynamic-update-slice | bytes 16388 | tf_op jit(solution)/shard_map/add | solution.py:84
  53.9 0.7 convert_bitcast_fusion
  54.6 2.4 %copy.80 = bf16[2,4,65,32,32]{2,1,4,3,0:T(4,128)(2,1)} copy(bf16[2,4,65,32,32]{2,3,1,4,0:T(8,128)(2,1)S(1)} %convert_bitcast_fusion) | data formatting | bytes 2129920 | tf_op jit(solution)/shard_map/convert_element_type | solution.py:80
  57.0 4.3 %reshape.665 = bf16[2,260,1024]{1,2,0:T(8,128)(2,1)} reshape(bf16[2,4,65,32,32]{2,1,4,3,0:T(4,128)(2,1)} %copy.80) | data formatting | bytes 2129920 | tf_op jit(solution)/shard_map/reshape | solution.py:81
  61.4 2.0 %convolution_convert_fusion = bf16[2,65,1024]{2,1,0:T(8,128)(2,1)S(1)} fusion(bf16[2,65,260]{2,1,0:T(8,128)(2,1)S(1)} %reshape.773, bf16[2,260,1024]{1,2,0:T(8,128)(2,1)} %reshape.665), kind=kOutput, calls=%fused_computation.19 | convolution fusion | flops 69355520 | bytes 1398800 | tf_op jit(solution)/shard_map/zik,zkm->zim/dot_general | solution.py:82
  63.4 1.0 %copy.83 = bf16[2,65,1024]{1,2,0:T(8,128)(2,1)} copy(bf16[2,65,1024]{2,1,0:T(8,128)(2,1)S(1)} %convolution_convert_fusion) | data formatting | bytes 532480 | tf_op jit(solution)/shard_map/convert_element_type | solution.py:83
  64.4 2.8 %copy.85 = bf16[2,65,32,32]{3,2,1,0:T(8,128)(2,1)S(1)} copy(bf16[2,65,32,32]{1,3,2,0:T(8,128)(2,1)} %bitcast.99) | data formatting | bytes 532480 | tf_op jit(solution)/shard_map/reshape | solution.py:83
  67.3 0.5 copy.99
  67.8 0.4 fusion.7
  68.3 4.6 %fusion.2 = f32[2,3136]{1,0:T(2,128)S(1)} fusion(bf16[2,1024]{1,0:T(2,128)(2,1)S(1)} %convert_element_type.67, bf16[1,1024,3136]{1,2,0:T(8,128)(2,1)} %param.16, f32[]{:T(128)} %bitcast.90), kind=kOutput, calls=%fused_computation.14 | convolution fusion | flops 12851328 | bytes 6451716 | tf_op jit(solution)/shard_map/dot_general | solution.py:88
  72.9 10.3 %psum.7 = f32[2,3136]{1,0:T(2,128)S(1)} all-reduce(f32[2,3136]{1,0:T(2,128)S(1)} %fusion.2), channel_id=1, replica_groups=mesh['dom'=8,'en'=4] {'en'}, use_global_device_ids=true, to_apply=%region_21.22 | all-reduce | flops 6272 | bytes 50176 | tf_op jit(solution)/shard_map/psum | solution.py:89
  83.2 0.6 multiply_add_fusion
  (111 shorter events, 4.8 us)
Async XLA Ops:
  0.0 5.3 %copy-start = (bf16[1,256,1024]{2,1,0:T(8,128)(2,1)S(1)}, bf16[1,256,1024]{2,1,0:T(8,128)(2,1)}, u32[]{:S(2)}) copy-start(bf16[1,256,1024]{2,1,0:T(8,128)(2,1)} %param.11) | copy-start | bytes 1572868
  0.0 3.0 %copy-start.1 = (s32[2048]{0:T(1024)S(1)}, s32[2048]{0:T(1024)}, u32[]{:S(2)}) copy-start(s32[2048]{0:T(1024)} %param.18) | copy-start | bytes 24580
  6.1 22.8 %collective-permute-start = (bf16[48,1024]{1,0:T(8,128)(2,1)S(1)}, bf16[48,1024]{1,0:T(8,128)(2,1)S(1)}, u32[]{:S(2)}, u32[]{:S(2)}) collective-permute-start(bf16[48,1024]{1,0:T(8,128)(2,1)S(1)} %broadcast_select_fusion.4), channel_id=1, source_target_pairs={{8,0},{12,4},{16,8},{20,12},{24,16},{28,20},{0,24},{4,28},{9,1},{1... | collective-permute-start | bytes 294920 | tf_op jit(solution)/shard_map/ppermute | solution.py:18
  12.9 16.0 %collective-permute-start.1 = (bf16[48,1024]{1,0:T(8,128)(2,1)S(1)}, bf16[48,1024]{1,0:T(8,128)(2,1)S(1)}, u32[]{:S(2)}, u32[]{:S(2)}) collective-permute-start(bf16[48,1024]{1,0:T(8,128)(2,1)S(1)} %broadcast_select_fusion.3), channel_id=1, source_target_pairs={{4,0},{8,4},{12,8},{16,12},{20,16},{24,20},{28,24},{0,28},{5,1},{9... | collective-permute-start | bytes 294920 | tf_op jit(solution)/shard_map/ppermute | solution.py:18
  19.1 9.9 %collective-permute-start.2 = (bf16[48,1024]{1,0:T(8,128)(2,1)S(1)}, bf16[48,1024]{1,0:T(8,128)(2,1)S(1)}, u32[]{:S(2)}, u32[]{:S(2)}) collective-permute-start(bf16[48,1024]{1,0:T(8,128)(2,1)S(1)} %broadcast_select_fusion.2), channel_id=1, source_target_pairs={{28,0},{0,4},{4,8},{8,12},{12,16},{16,20},{20,24},{24,28},{29,1},{... | collective-permute-start | bytes 294920 | tf_op jit(solution)/shard_map/ppermute | solution.py:18
  21.4 6.1 %copy-start.4 = (bf16[4,1024]{1,0:T(4,128)(2,1)S(1)}, bf16[4,1024]{1,0:T(4,128)(2,1)}, u32[]{:S(2)}) copy-start(bf16[4,1024]{1,0:T(4,128)(2,1)} %param.13) | copy-start | bytes 24580
  21.4 6.2 %copy-start.2 = (bf16[2,4,4225]{2,1,0:T(4,128)(2,1)S(1)}, bf16[2,4,4225]{2,1,0:T(4,128)(2,1)}, u32[]{:S(2)}) copy-start(bf16[2,4,4225]{2,1,0:T(4,128)(2,1)} %param.12) | copy-start | bytes 202804
  21.5 7.6 %collective-permute-start.3 = (bf16[48,1024]{1,0:T(8,128)(2,1)S(1)}, bf16[48,1024]{1,0:T(8,128)(2,1)S(1)}, u32[]{:S(2)}, u32[]{:S(2)}) collective-permute-start(bf16[48,1024]{1,0:T(8,128)(2,1)S(1)} %broadcast_select_fusion.1), channel_id=1, source_target_pairs={{24,0},{28,4},{0,8},{4,12},{8,16},{12,20},{16,24},{20,28},{25,1},{... | collective-permute-start | bytes 294920 | tf_op jit(solution)/shard_map/ppermute | solution.py:18
  22.7 5.1 %copy-start.6 = (f32[1,4]{1,0:T(1,128)S(1)}, f32[1,4]{1,0:T(1,128)}, u32[]{:S(2)}) copy-start(f32[1,4]{1,0:T(1,128)} %param.14) | copy-start | bytes 52
  29.9 1.6 %copy-start.5 = (pred[65]{0:T(512)(128)(4,1)S(1)}, pred[65]{0:T(512)(128)(4,1)}, u32[]{:S(2)}) copy-start(pred[65]{0:T(512)(128)(4,1)} %constant.175.clone.1) | copy-start | bytes 199
  68.3 14.9 %copy-start.3 = (f32[2,3136]{1,0:T(2,128)S(1)}, f32[2,3136]{1,0:T(2,128)}, u32[]{:S(2)}) copy-start(f32[2,3136]{1,0:T(2,128)} %param.19) | copy-start | bytes 75268
where the time goes:
time: 84.3 us; the launch traced here: 83.8 us
  local copies, waits for them, and re-layouts  44.7 us (53%)
  matrix products  12.2 us (14%)
  blocking collectives  10.3 us (12%)
  starting transfers between devices  8.44 us (10%)
  other arithmetic  6.99 us (8%)
  between operations  1.15 us (1%)
    psum x1, blocking collectives, shards(): density = lax.psum(energy_part, 'en')  10.3 us
    reshape x2, local copies, waits for them, and re-layouts, shards(): spread = spread.reshape(ZONES_DEV, TERMS * ZA, BLK * BLK)  8.67 us
    ppermute x4, starting transfers between devices, shifted(): return lax.ppermute(block, axis, route)  8.44 us
    gather x5, local copies, waits for them, and re-layouts, shards(): target_rows = owner_row[target_lists]  7.69 us
    reshape x2, local copies, waits for them, and re-layouts, shards(): field_half = field_sum.astype(jnp.bfloat16).reshape(ZONES_DEV, ZA, BLK, BLK)  5.52 us
    convert_element_type x2, local copies, waits for them, and re-layouts, shards(): spread = jnp.einsum('qab,zjbc->zqjac', tables, sweep_in, preferred_elemen...  4.87 us
    dot_general x1, matrix products, shards(): jnp.dot(central, radial[0], preferred_element_type=jnp.float32)  4.59 us
    dot_general x2, matrix products, shards(): jnp.einsum('zik,zkm->zim', scaled, spread, preferred_element_type=jnp.flo...  4.03 us
  transfers between devices with their start and end apart: 4, of which 0 were waited for; matrix products, arithmetic and copies ran while one was open for 16% of the time, Pallas kernels for 0%

commit v1 on v0

v1 whole, which is shorter than its diff:
```python
import functools
import math

import jax
import jax.numpy as jnp
from jax import lax
from jax.experimental import pallas as pl
from jax.experimental.pallas import tpu as pltpu
from jax.sharding import PartitionSpec as P

REACH = 2
CAP = 48
LANES = 128
SUBS = 8
OFFSETS = tuple(offset for offset in range(-REACH, REACH + 1) if offset != 0)
F32 = jnp.float32
BF16 = jnp.bfloat16


def matmul(a, b, dims=((1,), (0,))):
    return lax.dot_general(a, b, (dims, ((), ())), preferred_element_type=F32)


def iota(shape, axis):
    return lax.broadcasted_iota(jnp.int32, shape, axis)


def ones_where(mask):
    return jnp.where(mask, 1.0, 0.0).astype(BF16)


def split(x):
    high = x.astype(BF16)
    return high, (x - high.astype(F32)).astype(BF16)


def load_lists(nbr_ref, pad_ref, targets):
    zones, places = nbr_ref.shape[1:]
    pad_ref[...] = jnp.full(pad_ref.shape, -1, jnp.int32)
    for k, target in enumerate(targets):
        pad_ref[k * zones : (k + 1) * zones, 0:places] = nbr_ref[target]
    return jnp.concatenate(
        [pad_ref[r : r + 1, :] for r in range(len(targets) * zones)], axis=1
    )


def resolve(atoms, table_ref, owned):
    table = table_ref[...]
    if owned & (owned - 1) == 0:
        shift = owned.bit_length() - 1
        domain, local = table >> shift, table & (owned - 1)
    else:
        domain, local = table // owned, table % owned
    both = jnp.concatenate([domain, local], axis=1).astype(F32).astype(BF16)
    width = atoms.shape[1]
    row_hot = ones_where(iota((table.shape[0], width), 0) == (atoms >> 7))
    picked = matmul(both, row_hot, ((0,), (0,)))
    lane_hot = iota((LANES, width), 0) == (atoms & (LANES - 1))
    found = [
        jnp.sum(jnp.where(lane_hot, picked[i * LANES : (i + 1) * LANES], 0.0), axis=0, keepdims=True)
        for i in range(2)
    ]
    return jnp.where(atoms < 0, -1.0, found[0]), found[1]


def slot_hot(masks):
    width = masks[0].shape[1]
    rows = jnp.concatenate(
        [jnp.where(mask, 1.0, 0.0) for mask in masks]
        + [jnp.zeros((SUBS - len(masks), width), F32)],
        axis=0,
    ).astype(BF16)
    earlier = ones_where(iota((width, width), 0) < iota((width, width), 1))
    rank = matmul(rows, earlier)
    slots = iota((CAP, width), 0).astype(F32)
    return [
        ones_where((rank[k : k + 1] == slots) & mask) for k, mask in enumerate(masks)
    ]


def pack_kernel(axis, nbr_ref, table_ref, site_ref, *refs):
    pack_refs, pad_ref = refs[:-1], refs[-1]
    count = nbr_ref.shape[0]
    owned = site_ref.shape[0]
    me = lax.axis_index(axis)
    atoms = load_lists(nbr_ref, pad_ref, [lax.rem(me + o + count, count) for o in OFFSETS])
    domain, local = resolve(atoms, table_ref, owned)
    width = atoms.shape[1] // len(OFFSETS)
    mine = domain == me.astype(F32)
    spans = [slice(k * width, (k + 1) * width) for k in range(len(OFFSETS))]
    hots = slot_hot([mine[:, s] for s in spans])
    rows = iota((owned, width), 0).astype(F32)
    chosen = [
        matmul(hot, ones_where(local[:, s] == rows), ((1,), (1,))).astype(BF16)
        for hot, s in zip(hots, spans)
    ]
    packed = matmul(jnp.concatenate(chosen, axis=0), site_ref[...]).astype(BF16)
    for k, pack_ref in enumerate(pack_refs):
        pack_ref[...] = packed[k * CAP : (k + 1) * CAP]


def fold_matrix():
    return ones_where(
        (iota((LANES, LANES), 0) % 32) == (iota((LANES, LANES), 1) % 32)
    )


def block_mask():
    return (iota((LANES, LANES), 0) // 32) == (iota((LANES, LANES), 1) // 32)


def prepare_kernel(
    axis,
    nbr_ref, table_ref, site_ref, first_ref, last_ref, phase_ref, angular_ref,
    slot_ref, own_ref, chain_ref, spread_ref, start_ref, centre_ref,
    pad_ref, scaled_ref, grid_ref,
):
    count, zones, places = nbr_ref.shape
    owned = site_ref.shape[0]
    terms = angular_ref.shape[0]
    groups = angular_ref.shape[1] // LANES
    me = lax.axis_index(axis)
    atoms = load_lists(nbr_ref, pad_ref, [me])
    domain, local = resolve(atoms, table_ref, owned)
    width = atoms.shape[1]
    hots = slot_hot(
        [domain == lax.rem(me - o + count, count).astype(F32) for o in OFFSETS]
    )
    scaled_ref[...] = jnp.zeros(scaled_ref.shape, F32)
    for z in range(zones):
        for q in range(terms):
            phase = phase_ref[0, q]
            for half, ref in enumerate((first_ref, last_ref)):
                row = (phase * ref[z, q : q + 1, :].astype(F32)).astype(BF16)
                at = half * zones * SUBS + z * SUBS + q
                scaled_ref[at : at + 1, 0:places] = row.astype(F32)
    coefs = []
    for z in range(zones):
        to_first = scaled_ref[z * SUBS : (z + 1) * SUBS, :]
        at = (zones + z) * SUBS
        rows = jnp.concatenate(
            [scaled_ref[at + p : at + p + 1, :] * to_first for p in range(terms)], axis=0
        )
        blank = jnp.zeros(rows.shape, F32)
        coefs.append(
            jnp.concatenate([rows if y == z else blank for y in range(zones)], axis=1)
        )
    high, low = split(jnp.concatenate(coefs, axis=0))
    size = high.shape[0]
    both = jnp.concatenate([high, low], axis=0)
    slot_ref[...] = matmul(both, jnp.concatenate(hots, axis=0), ((1,), (1,))).astype(BF16)
    centres = ones_where(
        iota((2 * SUBS, width), 1) == iota((2 * SUBS, width), 0) * LANES
    )
    own_hot = ones_where(
        (local == iota((owned, width), 0).astype(F32)) & (domain == me.astype(F32))
    )
    own_coefs = matmul(jnp.concatenate([both, centres], axis=0), own_hot, ((1,), (1,)))
    own = matmul(own_coefs.astype(BF16), site_ref[...])
    own_ref[...] = own[:size] + own[size : 2 * size]
    centre = own[2 * size : 2 * size + zones]

    for g in range(groups):
        at = slice(g * LANES, (g + 1) * LANES)
        for q in range(terms):
            grid_ref[g : g + 1, q * LANES : (q + 1) * LANES] = angular_ref[q : q + 1, at].astype(F32)
        for z in range(zones):
            m = terms + z
            grid_ref[g : g + 1, m * LANES : (m + 1) * LANES] = centre[z : z + 1, at]
    grid = grid_ref[...]
    for z in range(zones):
        m = terms + z
        centre_ref[z * groups : (z + 1) * groups, :] = grid[:, m * LANES : (m + 1) * LANES]
        start_ref[z * groups * SUBS : (z + 1) * groups * SUBS, :] = jnp.concatenate(
            [
                scaled_ref[z * SUBS : (z + 1) * SUBS, 0:1] * grid[g : g + 1, m * LANES : (m + 1) * LANES]
                for g in range(groups)
            ],
            axis=0,
        )
    repeat = ones_where(iota((32, groups), 0) // 4 == iota((32, groups), 1))
    tall = matmul(repeat, grid.astype(BF16))
    keep = iota((32, LANES), 0) % 4 == iota((32, LANES), 1) // 32
    masked = jnp.concatenate(
        [
            jnp.where(keep, tall[:, m * LANES : (m + 1) * LANES], 0.0)
            for m in range(terms + zones)
        ],
        axis=0,
    ).astype(BF16)
    tiled = matmul(masked, fold_matrix())
    diagonal = block_mask()
    tables = tiled[: terms * 32]
    first_only = jnp.where(iota(tables.shape, 1) < 32, tables, 0.0).astype(BF16)
    for z in range(zones):
        m = terms + z
        block = tiled[m * 32 : (m + 1) * 32].astype(BF16)
        product = matmul(first_only, jnp.concatenate([block] * 4, axis=0))
        for p in range(terms):
            piece = product[p * 32 : (p + 1) * 32]
            at = (z * terms + p) * LANES
            chain_ref[at : at + LANES, :] = jnp.where(
                diagonal, jnp.concatenate([piece] * 4, axis=0), 0.0
            ).astype(BF16)
    lane_term = iota((32, LANES), 1) // 32
    side = sum(
        jnp.where(lane_term == q, tables[q * 32 : (q + 1) * 32], 0.0) for q in range(terms)
    ).astype(BF16)
    row = iota((LANES, LANES), 0)
    column = iota((LANES, LANES), 1) % 64
    for low_row in range(4):
        move = ones_where(
            (row % 4 == low_row) & (column == ((row % 32) // 4) * SUBS + row // 32)
        )
        spread_ref[low_row * 32 : (low_row + 1) * 32, :] = matmul(side, move).astype(BF16)


def finish_kernel(
    piece_refs_count,
    *refs,
):
    pieces = refs[:piece_refs_count]
    (slot_ref, own_ref, chain_ref, spread_ref, start_ref, centre_ref, contour_ref, radial_hbm,
     out_ref, flat_ref, radial_ref, sem) = refs[piece_refs_count:]
    copy = pltpu.make_async_copy(radial_hbm, radial_ref, sem)
    copy.start()
    zones = out_ref.shape[0]
    near = jnp.concatenate([ref[...] for ref in pieces], axis=0)
    far = matmul(slot_ref[...], near)
    size = own_ref.shape[0]
    weights = own_ref[...] + far[:size] + far[size:]
    per_zone = size // zones
    terms = per_zone // SUBS
    groups = weights.shape[1] // LANES
    diagonal = block_mask()
    fold = fold_matrix()
    flat_ref[...] = jnp.zeros(flat_ref.shape, F32)
    for z in range(zones):
        base = z * per_zone
        lhs = jnp.concatenate(
            [
                jnp.concatenate(
                    [
                        weights[base + p * SUBS : base + (p + 1) * SUBS, g * LANES : (g + 1) * LANES]
                        for p in range(terms)
                    ],
                    axis=1,
                )
                for g in range(groups)
            ],
            axis=0,
        )
        rows = groups * SUBS
        both = matmul(
            jnp.concatenate(split(lhs), axis=0),
            chain_ref[z * terms * LANES : (z + 1) * terms * LANES, :],
        )
        sums = both[:rows] + both[rows:] + start_ref[z * rows : (z + 1) * rows, :]
        field = matmul(spread_ref[...], jnp.concatenate(split(sums), axis=0))
        field = jnp.where(diagonal, field, 0.0)
        field = field[0:32] + field[32:64] + field[64:96] + field[96:128]
        both = matmul(jnp.concatenate(split(field), axis=0), fold)
        field = (both[:32] + both[32:]).astype(BF16).astype(F32)
        block = jnp.where(diagonal, jnp.concatenate([field] * 4, axis=0), 0.0).astype(BF16)
        centre = centre_ref[z * groups : (z + 1) * groups, :]
        central = centre + matmul(centre.astype(BF16), block)
        for g in range(groups):
            flat_ref[z : z + 1, g * LANES : (g + 1) * LANES] = central[g : g + 1]
    central = flat_ref[...].astype(BF16)
    copy.wait()
    out_ref[...] = contour_ref[0] * matmul(central, radial_ref[...])[:zones]


def vmem():
    return pl.BlockSpec(memory_space=pltpu.VMEM)


def smem():
    return pl.BlockSpec(memory_space=pltpu.SMEM)


def sum_over(value, axis):
    size = lax.axis_size(axis)
    if size & (size - 1):
        return lax.psum(value, axis)
    stride = 1
    while stride < size:
        radix = min(4, size // stride)
        parts = [value] + [
            lax.ppermute(value, axis, [(i, i ^ (stride * k)) for i in range(size)])
            for k in range(1, radix)
        ]
        value = (parts[0] + parts[1]) + (parts[2] + parts[3]) if radix == 4 else parts[0] + parts[1]
        stride *= radix
    return value


def shards(
    single_site, coupling, angular, phases, contour, radial, neighbours, owner_row, old_potential
):
    site = single_site[0]
    owned, width = site.shape
    count, zones, places = neighbours.shape
    terms = angular.shape[0]
    atoms = owner_row.shape[0]
    assert owned <= 256 and count <= 256 and places <= LANES and zones == 2
    assert width == 1024 and terms == 4 and atoms % LANES == 0
    table = owner_row.reshape(atoms // LANES, LANES)
    packs = pl.pallas_call(
        functools.partial(pack_kernel, "dom"),
        out_shape=[jax.ShapeDtypeStruct((CAP, width), BF16)] * len(OFFSETS),
        in_specs=[vmem()] * 3,
        out_specs=[vmem()] * len(OFFSETS),
        scratch_shapes=[pltpu.VMEM((len(OFFSETS) * zones, LANES), jnp.int32)],
        name="pack",
    )(neighbours, table, site)
    pieces = [
        lax.ppermute(pack, "dom", [((i - offset) % count, i) for i in range(count)])
        for pack, offset in zip(packs, OFFSETS)
    ]
    first = coupling[:, :, :places]
    last = coupling.reshape(zones, terms, places, places)[:, :, :, 0]
    size = zones * terms * SUBS
    groups = width // LANES
    prepared = pl.pallas_call(
        functools.partial(prepare_kernel, "dom"),
        out_shape=[
            jax.ShapeDtypeStruct((2 * size, CAP * len(OFFSETS)), BF16),
            jax.ShapeDtypeStruct((size, width), F32),
            jax.ShapeDtypeStruct((zones * terms * LANES, LANES), BF16),
            jax.ShapeDtypeStruct((LANES, LANES), BF16),
            jax.ShapeDtypeStruct((zones * groups * SUBS, LANES), F32),
            jax.ShapeDtypeStruct((zones * groups, LANES), F32),
        ],
        in_specs=[vmem()] * 5 + [smem(), vmem()],
        out_specs=[vmem()] * 6,
        scratch_shapes=[
            pltpu.VMEM((zones, LANES), jnp.int32),
            pltpu.VMEM((2 * zones * SUBS, LANES), F32),
            pltpu.VMEM((groups, (terms + zones) * LANES), F32),
        ],
        name="prepare",
    )(neighbours, table, site, first, last, phases, angular)
    part = pl.pallas_call(
        functools.partial(finish_kernel, len(pieces)),
        out_shape=jax.ShapeDtypeStruct((zones, radial.shape[2]), F32),
        in_specs=[vmem()] * (len(pieces) + 6) + [smem(), pl.BlockSpec(memory_space=pltpu.HBM)],
        out_specs=vmem(),
        scratch_shapes=[
            pltpu.VMEM((SUBS, width), F32),
            pltpu.VMEM(radial.shape[1:], BF16),
            pltpu.SemaphoreType.DMA,
        ],
        name="finish",
    )(*pieces, *prepared, contour, radial[0])
    density = sum_over(part, "en")
    return 0.5 * old_potential + 0.5 * density * lax.rsqrt(1.0 + density * density)


def solution(mesh):
    return jax.shard_map(
        shards,
        mesh=mesh,
        in_specs=(
            P("en", "dom", None),
            P("dom", None, None),
            P(),
            P("en", None),
            P("en"),
            P("en", None, None),
            P(),
            P(),
            P("dom", None),
        ),
        out_specs=P("dom", None),
        check_vma=False,
    )
```

time: 84.3 us -> 39.5 us (0.47)
  local copies, waits for them, and re-layouts: 44.7 us -> 13.2 us
  matrix products: 12.2 us -> 0 us
  Pallas kernels: 0 us -> 11.3 us
  blocking collectives: 10.3 us -> 0 us
  other arithmetic: 6.99 us -> 1.39 us
  waiting for transfers between devices: 0.01 us -> 2.32 us
  starting transfers between devices: 8.44 us -> 9.96 us
    reshape x15 -> x1, local copies, waits for them, and re-layouts: 16.3 us -> 1.07 us  [shards(): last = coupling.reshape(zones, terms, places, places)[:, :, :, 0]]
    gather x13 -> x0, local copies, waits for them, and re-layouts: 13.6 us -> none  [the longest x5 7.69 us: shards(): target_rows = owner_row[target_lists]]
    dot_general x7 -> x0, matrix products: 12.2 us -> none  [the longest x1 4.59 us: shards(): jnp.dot(central, radial[0], preferred_element_type=jnp.float32)]
    pallas_call x0 -> x3, Pallas kernels: none -> 11.3 us  [the longest x1 5.69 us: shards(): pl.pallas_call(functools.partial(finish_kernel, len(pieces)), out_shape=j...]
    unnamed x18 -> x12, local copies, waits for them, and re-layouts: 0.52 us -> 10.9 us
    psum x1 -> x0, blocking collectives: 10.3 us -> none  [shards(): density = lax.psum(energy_part, 'en')]
    convert_element_type x6 -> x0, local copies, waits for them, and re-layouts: 7.2 us -> none  [the longest x2 4.87 us: shards(): spread = jnp.einsum('qab,zjbc->zqjac', tables, sweep_in, preferred_elemen...]
    add x1 -> x0, local copies, waits for them, and re-layouts: 2.84 us -> none  [shards(): start + jnp.einsum('ziab,zibc->ziac', site_blocks, field_half, preferred_...]
  transfers between devices with their start and end apart: 4 -> 7, of which waited for: 0 -> 2; matrix products, arithmetic and copies ran while one was open for 16% -> 32% of each run, Pallas kernels for 0% -> 7%
where the time goes in v1:
time: 39.5 us; the launch traced here: 39 us
  local copies, waits for them, and re-layouts  13.2 us (33%)
  Pallas kernels  11.3 us (29%)
  starting transfers between devices  9.96 us (25%)
  waiting for transfers between devices  2.32 us (6%)
  other arithmetic  1.39 us (4%)
  between operations  0.74 us (2%)
    unnamed x12, local copies, waits for them, and re-layouts  10.9 us
    ppermute x4, starting transfers between devices, shards(): lax.ppermute(pack, 'dom', [((i - offset) % count, i) for i in range(count)])  8.03 us
    pallas_call x1, Pallas kernels, shards(): pl.pallas_call(functools.partial(finish_kernel, len(pieces)), out_shape=j...  5.69 us
    pallas_call x1, Pallas kernels, shards(): pl.pallas_call(functools.partial(prepare_kernel, 'dom'), out_shape=[jax.S...  2.91 us
    pallas_call x1, Pallas kernels, shards(): pl.pallas_call(functools.partial(pack_kernel, 'dom'), out_shape=[jax.Shap...  2.72 us
    ppermute x3, waiting for transfers between devices, sum_over(): lax.ppermute(value, axis, [(i, i ^ stride * k) for i in range(size)])  2.31 us
    ppermute x3, starting transfers between devices, sum_over(): lax.ppermute(value, axis, [(i, i ^ stride * k) for i in range(size)])  1.93 us
    add x1, other arithmetic, shards(): 0.5 * old_potential + 0.5 * density * lax.rsqrt(1.0 + density * density)  1.39 us
  transfers between devices with their start and end apart: 7, of which 2 were waited for; matrix products, arithmetic and copies ran while one was open for 32% of the time, Pallas kernels for 7%

profile of v1, /device:TPU:0, one launch (start us, length us, event | category | flops | bytes accessed | tf_op | source)
XLA Modules:
  0.0 39.0 jit_solution(10043811384983608527)
XLA Ops:
  0.0 2.7 %pack.1 = (bf16[48,1024]{1,0:T(8,128)(2,1)}, bf16[48,1024]{1,0:T(8,128)(2,1)}, bf16[48,1024]{1,0:T(8,128)(2,1)}, bf16[48,1024]{1,0:T(8,128)(2,1)}) custom-call(s32[8,2,65]{2,1,0:T(2,128)} %nbr_ref.3, s32[16,128]{1,0:T(8,128)} %bitcast.9, bf16[256,1024]{1,0:T(8,128)(2,1)} %bitcast.6), custom_call_target="tpu_custom_call" | custom-call | tf_op jit(solution)/shard_map/pack/pallas_call | solution.py:309
  2.7 5.1 %collective-permute-start = (bf16[48,1024]{1,0:T(8,128)(2,1)}, bf16[48,1024]{1,0:T(8,128)(2,1)S(1)}, u32[]{:S(2)}, u32[]{:S(2)}) collective-permute-start(bf16[48,1024]{1,0:T(8,128)(2,1)} %get-tuple-element.15), channel_id=1, source_target_pairs={{8,0},{12,4},{16,8},{20,12},{24,16},{28,20},{0,24},{4,28},{9,1},{1... | collective-permute-start | bytes 294920 | tf_op jit(solution)/shard_map/ppermute | solution.py:318
  7.8 1.4 %collective-permute-start.1 = (bf16[48,1024]{1,0:T(8,128)(2,1)}, bf16[48,1024]{1,0:T(8,128)(2,1)S(1)}, u32[]{:S(2)}, u32[]{:S(2)}) collective-permute-start(bf16[48,1024]{1,0:T(8,128)(2,1)} %get-tuple-element.16), channel_id=1, source_target_pairs={{4,0},{8,4},{12,8},{16,12},{20,16},{24,20},{28,24},{0,28},{5,1},{9... | collective-permute-start | bytes 294920 | tf_op jit(solution)/shard_map/ppermute | solution.py:318
  9.2 0.7 %collective-permute-start.2 = (bf16[48,1024]{1,0:T(8,128)(2,1)}, bf16[48,1024]{1,0:T(8,128)(2,1)S(1)}, u32[]{:S(2)}, u32[]{:S(2)}) collective-permute-start(bf16[48,1024]{1,0:T(8,128)(2,1)} %get-tuple-element.17), channel_id=1, source_target_pairs={{28,0},{0,4},{4,8},{8,12},{12,16},{16,20},{20,24},{24,28},{29,1},{... | collective-permute-start | bytes 294920 | tf_op jit(solution)/shard_map/ppermute | solution.py:318
  9.8 0.9 %collective-permute-start.3 = (bf16[48,1024]{1,0:T(8,128)(2,1)}, bf16[48,1024]{1,0:T(8,128)(2,1)S(1)}, u32[]{:S(2)}, u32[]{:S(2)}) collective-permute-start(bf16[48,1024]{1,0:T(8,128)(2,1)} %get-tuple-element.18), channel_id=1, source_target_pairs={{24,0},{28,4},{0,8},{4,12},{8,16},{12,20},{16,24},{20,28},{25,1},{... | collective-permute-start | bytes 294920 | tf_op jit(solution)/shard_map/ppermute | solution.py:318
  10.8 1.3 %slice.6.first_ref = bf16[2,4,65]{2,1,0:T(4,128)(2,1)} slice(bf16[2,4,4225]{2,1,0:T(4,128)(2,1)} %param.10), slice={[0:2], [0:4], [0:65]} | slice | bytes 2080 | tf_op jit(solution)/shard_map/slice | solution.py:321
  12.0 1.1 %reshape.7 = bf16[2,4,65,65]{3,2,1,0:T(8,128)(2,1)S(1)} reshape(bf16[2,4,4225]{2,1,0:T(4,128)(2,1)} %param.10) | data formatting | bytes 135200 | tf_op jit(solution)/shard_map/reshape | solution.py:322
  13.8 0.7 %copy.13 = bf16[2,4,65,1]{2,1,0,3:T(4,128)(2,1)} copy(bf16[2,4,65,1]{3,2,1,0:T(8,128)(2,1)S(1)} %bitcast.8) | data formatting | bytes 2080
  14.5 9.5 %copy.12 = bf16[1,1024,3136]{2,1,0:T(8,128)(2,1)} copy(bf16[1,1024,3136]{1,2,0:T(8,128)(2,1)} %param.14) | data formatting | bytes 12845056 | tf_op args[5]
  23.9 0.0 copy-start.4
  23.9 2.9 %prepare.1 = (bf16[128,192]{1,0:T(8,128)(2,1)}, f32[64,1024]{1,0:T(8,128)}, bf16[1024,128]{1,0:T(8,128)(2,1)}, bf16[128,128]{1,0:T(8,128)(2,1)}, f32[128,128]{1,0:T(8,128)}, /*index=5*/f32[16,128]{1,0:T(8,128)}) custom-call(s32[8,2,65]{2,1,0:T(2,128)} %nbr_ref.3, s32[16,128]{1,0:T(8,128)} %bitcast.10, bf16[256,1024]{1,0:T(8,128)(2,1)} %bitcast.7, ...), custom_call_target="tpu_custom_call" | custom-call | tf_op jit(solution)/shard_map/prepare/pallas_call | solution.py:325
  26.9 0.0 collective-permute-done.refs_0_
  26.9 0.0 copy-start
  26.9 0.0 collective-permute-done.1.refs_1_
  26.9 0.0 copy-start.1
  26.9 0.0 collective-permute-done.2.refs_2_
  26.9 0.0 copy-start.2
  26.9 0.0 collective-permute-done.3.refs_3_
  26.9 0.0 copy-start.3
  26.9 0.6 %copy-done = bf16[48,1024]{1,0:T(8,128)(2,1)} copy-done((bf16[48,1024]{1,0:T(8,128)(2,1)}, bf16[48,1024]{1,0:T(8,128)(2,1)S(1)}, u32[]{:S(2)}) %copy-start) | copy-done | bytes 98328
  27.5 0.0 copy-done.1
  27.5 0.0 copy-done.2
  27.6 0.1 copy-done.3
  27.6 5.7 %finish.1 = f32[2,3136]{1,0:T(2,128)} custom-call(bf16[48,1024]{1,0:T(8,128)(2,1)} %copy-done, bf16[48,1024]{1,0:T(8,128)(2,1)} %copy-done.1, bf16[48,1024]{1,0:T(8,128)(2,1)} %copy-done.2, bf16[48,1024]{1,0:T(8,128)(2,1)} %copy-done.3, bf16[128,192]{1,0:T(8,128)(2,1)} %get-tuple-element.19.refs_4_, f32[64,1024]{1,0:T(8,128)} %get-tuple-element.20.refs_5_, ...), custom_call_target="tpu_custom_call" | custom-call | tf_op jit(solution)/shard_map/finish/pallas_call | solution.py:344
  33.3 0.2 collective-permute-start.6
  33.5 1.5 %collective-permute-start.5 = (f32[2,3136]{1,0:T(2,128)}, f32[2,3136]{1,0:T(2,128)S(1)}, u32[]{:S(2)}, u32[]{:S(2)}) collective-permute-start(f32[2,3136]{1,0:T(2,128)} %finish.1), channel_id=1, source_target_pairs={{0,2},{1,3},{2,0},{3,1},{4,6},{5,7},{6,4},{7,5},{8,10},{9,11},{10,... | collective-permute-start | bytes 75272 | tf_op jit(solution)/shard_map/ppermute | solution.py:290
  35.0 0.3 collective-permute-start.4
  35.3 1.8 %collective-permute-done.6 = f32[2,3136]{1,0:T(2,128)S(1)} collective-permute-done((f32[2,3136]{1,0:T(2,128)}, f32[2,3136]{1,0:T(2,128)S(1)}, u32[]{:S(2)}, u32[]{:S(2)}) %collective-permute-start.6) | collective-permute-done | bytes 25120 | tf_op jit(solution)/shard_map/ppermute | solution.py:290
  37.1 0.5 %collective-permute-done.5 = f32[2,3136]{1,0:T(2,128)S(1)} collective-permute-done((f32[2,3136]{1,0:T(2,128)}, f32[2,3136]{1,0:T(2,128)S(1)}, u32[]{:S(2)}, u32[]{:S(2)}) %collective-permute-start.5) | collective-permute-done | bytes 25120 | tf_op jit(solution)/shard_map/ppermute | solution.py:290
  37.6 0.0 collective-permute-done.4
  37.6 0.0 copy-done.4
  37.6 1.4 %multiply_add_fusion = f32[2,3136]{1,0:T(2,128)} fusion(f32[2,3136]{1,0:T(2,128)S(1)} %collective-permute-done.5, f32[2,3136]{1,0:T(2,128)S(1)} %collective-permute-done.6, f32[2,3136]{1,0:T(2,128)} %finish.1, f32[2,3136]{1,0:T(2,128)S(1)} %collective-permute-done.4, f32[2,3136]{1,0:T(2,128)S(1)} %copy-done.4), kind=kLoop, calls=%fused_computation | loop fusion | flops 56448 | bytes 150528 | tf_op jit(solution)/shard_map/add | solution.py:357
Async XLA Ops:
  2.7 24.1 %collective-permute-start = (bf16[48,1024]{1,0:T(8,128)(2,1)}, bf16[48,1024]{1,0:T(8,128)(2,1)S(1)}, u32[]{:S(2)}, u32[]{:S(2)}) collective-permute-start(bf16[48,1024]{1,0:T(8,128)(2,1)} %get-tuple-element.15), channel_id=1, source_target_pairs={{8,0},{12,4},{16,8},{20,12},{24,16},{28,20},{0,24},{4,28},{9,1},{1... | collective-permute-start | bytes 294920 | tf_op jit(solution)/shard_map/ppermute | solution.py:318
  7.8 19.1 %collective-permute-start.1 = (bf16[48,1024]{1,0:T(8,128)(2,1)}, bf16[48,1024]{1,0:T(8,128)(2,1)S(1)}, u32[]{:S(2)}, u32[]{:S(2)}) collective-permute-start(bf16[48,1024]{1,0:T(8,128)(2,1)} %get-tuple-element.16), channel_id=1, source_target_pairs={{4,0},{8,4},{12,8},{16,12},{20,16},{24,20},{28,24},{0,28},{5,1},{9... | collective-permute-start | bytes 294920 | tf_op jit(solution)/shard_map/ppermute | solution.py:318
  9.2 17.7 %collective-permute-start.2 = (bf16[48,1024]{1,0:T(8,128)(2,1)}, bf16[48,1024]{1,0:T(8,128)(2,1)S(1)}, u32[]{:S(2)}, u32[]{:S(2)}) collective-permute-start(bf16[48,1024]{1,0:T(8,128)(2,1)} %get-tuple-element.17), channel_id=1, source_target_pairs={{28,0},{0,4},{4,8},{8,12},{12,16},{16,20},{20,24},{24,28},{29,1},{... | collective-permute-start | bytes 294920 | tf_op jit(solution)/shard_map/ppermute | solution.py:318
  9.8 17.1 %collective-permute-start.3 = (bf16[48,1024]{1,0:T(8,128)(2,1)}, bf16[48,1024]{1,0:T(8,128)(2,1)S(1)}, u32[]{:S(2)}, u32[]{:S(2)}) collective-permute-start(bf16[48,1024]{1,0:T(8,128)(2,1)} %get-tuple-element.18), channel_id=1, source_target_pairs={{24,0},{28,4},{0,8},{4,12},{8,16},{12,20},{16,24},{20,28},{25,1},{... | collective-permute-start | bytes 294920 | tf_op jit(solution)/shard_map/ppermute | solution.py:318
  23.9 13.6 %copy-start.4 = (f32[2,3136]{1,0:T(2,128)S(1)}, f32[2,3136]{1,0:T(2,128)}, u32[]{:S(2)}) copy-start(f32[2,3136]{1,0:T(2,128)} %param.17) | copy-start | bytes 75268
  26.9 0.6 %copy-start = (bf16[48,1024]{1,0:T(8,128)(2,1)}, bf16[48,1024]{1,0:T(8,128)(2,1)S(1)}, u32[]{:S(2)}) copy-start(bf16[48,1024]{1,0:T(8,128)(2,1)S(1)} %collective-permute-done.refs_0_) | copy-start | bytes 294916
  26.9 0.6 %copy-start.1 = (bf16[48,1024]{1,0:T(8,128)(2,1)}, bf16[48,1024]{1,0:T(8,128)(2,1)S(1)}, u32[]{:S(2)}) copy-start(bf16[48,1024]{1,0:T(8,128)(2,1)S(1)} %collective-permute-done.1.refs_1_) | copy-start | bytes 294916
  26.9 0.7 %copy-start.2 = (bf16[48,1024]{1,0:T(8,128)(2,1)}, bf16[48,1024]{1,0:T(8,128)(2,1)S(1)}, u32[]{:S(2)}) copy-start(bf16[48,1024]{1,0:T(8,128)(2,1)S(1)} %collective-permute-done.2.refs_2_) | copy-start | bytes 294916
  26.9 0.7 %copy-start.3 = (bf16[48,1024]{1,0:T(8,128)(2,1)}, bf16[48,1024]{1,0:T(8,128)(2,1)S(1)}, u32[]{:S(2)}) copy-start(bf16[48,1024]{1,0:T(8,128)(2,1)S(1)} %collective-permute-done.3.refs_3_) | copy-start | bytes 294916
  33.3 3.7 %collective-permute-start.6 = (f32[2,3136]{1,0:T(2,128)}, f32[2,3136]{1,0:T(2,128)S(1)}, u32[]{:S(2)}, u32[]{:S(2)}) collective-permute-start(f32[2,3136]{1,0:T(2,128)} %finish.1), channel_id=1, source_target_pairs={{0,3},{1,2},{2,1},{3,0},{4,7},{5,6},{6,5},{7,4},{8,11},{9,10},{10,... | collective-permute-start | bytes 75272 | tf_op jit(solution)/shard_map/ppermute | solution.py:290
  33.5 4.0 %collective-permute-start.5 = (f32[2,3136]{1,0:T(2,128)}, f32[2,3136]{1,0:T(2,128)S(1)}, u32[]{:S(2)}, u32[]{:S(2)}) collective-permute-start(f32[2,3136]{1,0:T(2,128)} %finish.1), channel_id=1, source_target_pairs={{0,2},{1,3},{2,0},{3,1},{4,6},{5,7},{6,4},{7,5},{8,10},{9,11},{10,... | collective-permute-start | bytes 75272 | tf_op jit(solution)/shard_map/ppermute | solution.py:290
  35.0 2.6 %collective-permute-start.4 = (f32[2,3136]{1,0:T(2,128)}, f32[2,3136]{1,0:T(2,128)S(1)}, u32[]{:S(2)}, u32[]{:S(2)}) collective-permute-start(f32[2,3136]{1,0:T(2,128)} %finish.1), channel_id=1, source_target_pairs={{0,1},{1,0},{2,3},{3,2},{4,5},{5,4},{6,7},{7,6},{8,9},{9,8},{10,11... | collective-permute-start | bytes 75272 | tf_op jit(solution)/shard_map/ppermute | solution.py:290

commit v2 on v1

--- a/solution.py
+++ b/solution.py
@@ -1,5 +1,4 @@
 import functools
-import math
 
 import jax
 import jax.numpy as jnp
@@ -10,6 +9,7 @@
 
 REACH = 2
 CAP = 48
+LIMIT = 24 << 20
 LANES = 128
 SUBS = 8
 OFFSETS = tuple(offset for offset in range(-REACH, REACH + 1) if offset != 0)
@@ -78,11 +78,22 @@
     ]
 
 
-def pack_kernel(axis, nbr_ref, table_ref, site_ref, *refs):
-    pack_refs, pad_ref = refs[:-1], refs[-1]
+def pack_kernel(axis, inputs, *refs):
+    sources, refs = refs[:inputs], refs[inputs:]
+    kept, refs = refs[:inputs], refs[inputs:]
+    pack_refs, (pad_ref, sems) = refs[:-2], refs[-2:]
+    copies = [
+        pltpu.make_async_copy(source, ref, sems.at[k])
+        for k, (source, ref) in enumerate(zip(sources, kept))
+    ]
+    for copy in copies:
+        copy.start()
+    nbr_ref, table_ref, site_ref = kept[:3]
     count = nbr_ref.shape[0]
     owned = site_ref.shape[0]
     me = lax.axis_index(axis)
+    copies[0].wait()
+    copies[1].wait()
     atoms = load_lists(nbr_ref, pad_ref, [lax.rem(me + o + count, count) for o in OFFSETS])
     domain, local = resolve(atoms, table_ref, owned)
     width = atoms.shape[1] // len(OFFSETS)
@@ -94,6 +105,8 @@
         matmul(hot, ones_where(local[:, s] == rows), ((1,), (1,))).astype(BF16)
         for hot, s in zip(hots, spans)
     ]
+    for copy in copies[2:]:
+        copy.wait()
     packed = matmul(jnp.concatenate(chosen, axis=0), site_ref[...]).astype(BF16)
     for k, pack_ref in enumerate(pack_refs):
         pack_ref[...] = packed[k * CAP : (k + 1) * CAP]
@@ -109,12 +122,36 @@
     return (iota((LANES, LANES), 0) // 32) == (iota((LANES, LANES), 1) // 32)
 
 
+def strided_row(couple_ref, zone, places):
+    terms, width = couple_ref.shape[1:]
+    lane = iota((terms, LANES), 1)
+    merged = jnp.zeros((terms, LANES), F32)
+    for begin in range(0, width, LANES):
+        size = min(LANES, width - begin)
+        block = couple_ref[zone, :, begin : begin + size].astype(F32)
+        if size < LANES:
+            spare = jnp.zeros((terms, LANES - size), F32)
+            block = jnp.concatenate([block, spare], axis=1)
+        kept = functools.reduce(
+            jnp.logical_or,
+            [lane == at - begin for at in range(0, width, places) if begin <= at < begin + size],
+            lane < 0,
+        )
+        merged = jnp.where(kept, block, merged)
+    order = ones_where(
+        (iota((LANES, LANES), 1) * places) % LANES == iota((LANES, LANES), 0)
+    )
+    return matmul(merged.astype(BF16), order)
+
+
 def prepare_kernel(
     axis,
-    nbr_ref, table_ref, site_ref, first_ref, last_ref, phase_ref, angular_ref,
-    slot_ref, own_ref, chain_ref, spread_ref, start_ref, centre_ref,
-    pad_ref, scaled_ref, grid_ref,
+    nbr_ref, table_ref, site_ref, couple_ref, angular_ref, phase_ref, radial_hbm,
+    slot_ref, own_ref, chain_ref, spread_ref, start_ref, centre_ref, radial_ref,
+    pad_ref, scaled_ref, grid_ref, sem,
 ):
+    fetch = pltpu.make_async_copy(radial_hbm, radial_ref, sem)
+    fetch.start()
     count, zones, places = nbr_ref.shape
     owned = site_ref.shape[0]
     terms = angular_ref.shape[0]
@@ -127,11 +164,12 @@
         [domain == lax.rem(me - o + count, count).astype(F32) for o in OFFSETS]
     )
     scaled_ref[...] = jnp.zeros(scaled_ref.shape, F32)
+    lasts = [strided_row(couple_ref, z, places) for z in range(zones)]
     for z in range(zones):
         for q in range(terms):
             phase = phase_ref[0, q]
-            for half, ref in enumerate((first_ref, last_ref)):
-                row = (phase * ref[z, q : q + 1, :].astype(F32)).astype(BF16)
+            for half, rows in enumerate((couple_ref[z, :, 0:places].astype(F32), lasts[z])):
+                row = (phase * rows[q : q + 1, 0:places]).astype(BF16)
                 at = half * zones * SUBS + z * SUBS + q
                 scaled_ref[at : at + 1, 0:places] = row.astype(F32)
     coefs = []
@@ -213,6 +251,7 @@
             (row % 4 == low_row) & (column == ((row % 32) // 4) * SUBS + row // 32)
         )
         spread_ref[low_row * 32 : (low_row + 1) * 32, :] = matmul(side, move).astype(BF16)
+    fetch.wait()
 
 
 def finish_kernel(
@@ -220,10 +259,8 @@
     *refs,
 ):
     pieces = refs[:piece_refs_count]
-    (slot_ref, own_ref, chain_ref, spread_ref, start_ref, centre_ref, contour_ref, radial_hbm,
-     out_ref, flat_ref, radial_ref, sem) = refs[piece_refs_count:]
-    copy = pltpu.make_async_copy(radial_hbm, radial_ref, sem)
-    copy.start()
+    (slot_ref, own_ref, chain_ref, spread_ref, start_ref, centre_ref, radial_ref, contour_ref,
+     out_ref, flat_ref) = refs[piece_refs_count:]
     zones = out_ref.shape[0]
     near = jnp.concatenate([ref[...] for ref in pieces], axis=0)
     far = matmul(slot_ref[...], near)
@@ -267,8 +304,7 @@
         for g in range(groups):
             flat_ref[z : z + 1, g * LANES : (g + 1) * LANES] = central[g : g + 1]
     central = flat_ref[...].astype(BF16)
-    copy.wait()
-    out_ref[...] = contour_ref[0] * matmul(central, radial_ref[...])[:zones]
+    out_ref[...] = contour_ref[0] * matmul(central, radial_ref[...], ((1,), (1,)))[:zones]
 
 
 def vmem():
@@ -304,55 +340,61 @@
     terms = angular.shape[0]
     atoms = owner_row.shape[0]
     assert owned <= 256 and count <= 256 and places <= LANES and zones == 2
-    assert width == 1024 and terms == 4 and atoms % LANES == 0
+    assert width == 1024 and terms == 4 and atoms % LANES == 0 and places % 2 == 1
     table = owner_row.reshape(atoms // LANES, LANES)
-    packs = pl.pallas_call(
-        functools.partial(pack_kernel, "dom"),
-        out_shape=[jax.ShapeDtypeStruct((CAP, width), BF16)] * len(OFFSETS),
-        in_specs=[vmem()] * 3,
-        out_specs=[vmem()] * len(OFFSETS),
-        scratch_shapes=[pltpu.VMEM((len(OFFSETS) * zones, LANES), jnp.int32)],
+    sources = [neighbours, table, site, coupling, angular]
+    results = pl.pallas_call(
+        functools.partial(pack_kernel, "dom", len(sources)),
+        out_shape=[pltpu.VMEM(x.shape, x.dtype) for x in sources]
+        + [pltpu.VMEM((CAP, width), BF16)] * len(OFFSETS),
+        in_specs=[pl.BlockSpec(memory_space=pltpu.HBM)] * len(sources),
+        out_specs=[vmem()] * (len(sources) + len(OFFSETS)),
+        scratch_shapes=[
+            pltpu.VMEM((len(OFFSETS) * zones, LANES), jnp.int32),
+            pltpu.SemaphoreType.DMA((len(sources),)),
+        ],
+        compiler_params=pltpu.CompilerParams(vmem_limit_bytes=LIMIT),
         name="pack",
-    )(neighbours, table, site)
+    )(*[pltpu.with_memory_space_constraint(x, pltpu.HBM) for x in sources])
+    kept, packs = results[: len(sources)], results[len(sources) :]
     pieces = [
         lax.ppermute(pack, "dom", [((i - offset) % count, i) for i in range(count)])
         for pack, offset in zip(packs, OFFSETS)
     ]
-    first = coupling[:, :, :places]
-    last = coupling.reshape(zones, terms, places, places)[:, :, :, 0]
     size = zones * terms * SUBS
     groups = width // LANES
     prepared = pl.pallas_call(
         functools.partial(prepare_kernel, "dom"),
         out_shape=[
-            jax.ShapeDtypeStruct((2 * size, CAP * len(OFFSETS)), BF16),
-            jax.ShapeDtypeStruct((size, width), F32),
-            jax.ShapeDtypeStruct((zones * terms * LANES, LANES), BF16),
-            jax.ShapeDtypeStruct((LANES, LANES), BF16),
-            jax.ShapeDtypeStruct((zones * groups * SUBS, LANES), F32),
-            jax.ShapeDtypeStruct((zones * groups, LANES), F32),
+            pltpu.VMEM((2 * size, CAP * len(OFFSETS)), BF16),
+            pltpu.VMEM((size, width), F32),
+            pltpu.VMEM((zones * terms * LANES, LANES), BF16),
+            pltpu.VMEM((LANES, LANES), BF16),
+            pltpu.VMEM((zones * groups * SUBS, LANES), F32),
+            pltpu.VMEM((zones * groups, LANES), F32),
+            pltpu.VMEM((radial.shape[2], width), BF16),
         ],
-        in_specs=[vmem()] * 5 + [smem(), vmem()],
-        out_specs=[vmem()] * 6,
+        in_specs=[vmem()] * 5 + [smem(), pl.BlockSpec(memory_space=pltpu.HBM)],
+        out_specs=[vmem()] * 7,
         scratch_shapes=[
             pltpu.VMEM((zones, LANES), jnp.int32),
             pltpu.VMEM((2 * zones * SUBS, LANES), F32),
             pltpu.VMEM((groups, (terms + zones) * LANES), F32),
+            pltpu.SemaphoreType.DMA,
         ],
+        compiler_params=pltpu.CompilerParams(vmem_limit_bytes=LIMIT),
         name="prepare",
-    )(neighbours, table, site, first, last, phases, angular)
+    )(*kept, phases, pltpu.with_memory_space_constraint(radial[0].T, pltpu.HBM))
+    pieces = [pltpu.with_memory_space_constraint(piece, pltpu.VMEM) for piece in pieces]
     part = pl.pallas_call(
         functools.partial(finish_kernel, len(pieces)),
-        out_shape=jax.ShapeDtypeStruct((zones, radial.shape[2]), F32),
-        in_specs=[vmem()] * (len(pieces) + 6) + [smem(), pl.BlockSpec(memory_space=pltpu.HBM)],
+        out_shape=pltpu.VMEM((zones, radial.shape[2]), F32),
+        in_specs=[vmem()] * (len(pieces) + 7) + [smem()],
         out_specs=vmem(),
-        scratch_shapes=[
-            pltpu.VMEM((SUBS, width), F32),
-            pltpu.VMEM(radial.shape[1:], BF16),
-            pltpu.SemaphoreType.DMA,
-        ],
+        scratch_shapes=[pltpu.VMEM((SUBS, width), F32)],
+        compiler_params=pltpu.CompilerParams(vmem_limit_bytes=LIMIT),
         name="finish",
-    )(*pieces, *prepared, contour, radial[0])
+    )(*pieces, *prepared, contour)
     density = sum_over(part, "en")
     return 0.5 * old_potential + 0.5 * density * lax.rsqrt(1.0 + density * density)
 

time: 39.5 us -> 24.9 us (0.63)
  local copies, waits for them, and re-layouts: 13.2 us -> 0.65 us
  Pallas kernels: 11.3 us -> 8.34 us
  waiting for transfers between devices: 2.32 us -> 4.07 us
  other arithmetic: 1.39 us -> 0.65 us
    unnamed x12 -> x4, local copies, waits for them, and re-layouts: 10.9 us -> 0.65 us
    pallas_call x3, Pallas kernels: 11.3 us -> 8.34 us  [the longest x1 3.63 us: shards(): pl.pallas_call(functools.partial(prepare_kernel, 'dom'), out_shape=[pltpu...]
    ppermute x4, waiting for transfers between devices: 0.01 us -> 1.43 us  [shards(): lax.ppermute(pack, 'dom', [((i - offset) % count, i) for i in range(count)])]
    slice x1 -> x0, local copies, waits for them, and re-layouts: 1.27 us -> none  [shards(): first = coupling[:, :, :places]]
    reshape x1 -> x0, local copies, waits for them, and re-layouts: 1.07 us -> none  [shards(): last = coupling.reshape(zones, terms, places, places)[:, :, :, 0]]
    add x1, other arithmetic: 1.39 us -> 0.65 us  [shards(): 0.5 * old_potential + 0.5 * density * lax.rsqrt(1.0 + density * density)]
  transfers between devices with their start and end apart: 7 -> 7, of which waited for: 2 -> 3; matrix products, arithmetic and copies ran while one was open for 32% -> 0% of each run, Pallas kernels for 7% -> 15%
where the time goes in v2:
time: 24.9 us; the launch traced here: 24.7 us
  starting transfers between devices  10.3 us (41%)
  Pallas kernels  8.34 us (33%)
  waiting for transfers between devices  4.07 us (16%)
  between operations  0.7 us (3%)
  local copies, waits for them, and re-layouts  0.65 us (3%)
  other arithmetic  0.65 us (3%)
    ppermute x4, starting transfers between devices, shards(): lax.ppermute(pack, 'dom', [((i - offset) % count, i) for i in range(count)])  8.08 us
    pallas_call x1, Pallas kernels, shards(): pl.pallas_call(functools.partial(prepare_kernel, 'dom'), out_shape=[pltpu...  3.63 us
    pallas_call x1, Pallas kernels, shards(): pl.pallas_call(functools.partial(finish_kernel, len(pieces)), out_shape=p...  2.96 us
    ppermute x3, waiting for transfers between devices, sum_over(): lax.ppermute(value, axis, [(i, i ^ stride * k) for i in range(size)])  2.64 us
    ppermute x3, starting transfers between devices, sum_over(): lax.ppermute(value, axis, [(i, i ^ stride * k) for i in range(size)])  2.17 us
    pallas_call x1, Pallas kernels, shards(): pl.pallas_call(functools.partial(pack_kernel, 'dom', len(sources)), out_s...  1.75 us
    ppermute x4, waiting for transfers between devices, shards(): lax.ppermute(pack, 'dom', [((i - offset) % count, i) for i in range(count)])  1.43 us
    add x1, other arithmetic, shards(): 0.5 * old_potential + 0.5 * density * lax.rsqrt(1.0 + density * density)  0.65 us
  transfers between devices with their start and end apart: 7, of which 3 were waited for; matrix products, arithmetic and copies ran while one was open for 0% of the time, Pallas kernels for 15%

profile of v2, /device:TPU:0, one launch (start us, length us, event | category | flops | bytes accessed | tf_op | source)
XLA Modules:
  0.0 24.7 jit_solution(877746698432240802)
XLA Ops:
  0.0 1.8 %pack.1 = (s32[8,2,65]{2,1,0:T(2,128)S(1)}, s32[16,128]{1,0:T(8,128)S(1)}, bf16[256,1024]{1,0:T(8,128)(2,1)S(1)}, bf16[2,4,4225]{2,1,0:T(4,128)(2,1)S(1)}, bf16[...) custom-call(s32[8,2,65]{2,1,0:T(2,128)} %refs_0_.1, ...), custom_call_target="tpu_custom_call" | custom-call | tf_op jit(solution)/shard_map/pack/pallas_call | solution.py:346
  1.8 5.1 %collective-permute-start = (bf16[48,1024]{1,0:T(8,128)(2,1)S(1)}, bf16[48,1024]{1,0:T(8,128)(2,1)S(1)}, u32[]{:S(2)}, u32[]{:S(2)}) collective-permute-start(bf16[48,1024]{1,0:T(8,128)(2,1)S(1)} %get-tuple-element.21), channel_id=1, source_target_pairs={{8,0},{12,4},{16,8},{20,12},{24,16},{28,20},{0,24},{4,28},{9,1},{1... | collective-permute-start | bytes 294920 | tf_op jit(solution)/shard_map/ppermute | solution.py:361
  6.9 1.4 %collective-permute-start.1 = (bf16[48,1024]{1,0:T(8,128)(2,1)S(1)}, bf16[48,1024]{1,0:T(8,128)(2,1)S(1)}, u32[]{:S(2)}, u32[]{:S(2)}) collective-permute-start(bf16[48,1024]{1,0:T(8,128)(2,1)S(1)} %get-tuple-element.22), channel_id=1, source_target_pairs={{4,0},{8,4},{12,8},{16,12},{20,16},{24,20},{28,24},{0,28},{5,1},{9... | collective-permute-start | bytes 294920 | tf_op jit(solution)/shard_map/ppermute | solution.py:361
  8.3 0.7 %collective-permute-start.2 = (bf16[48,1024]{1,0:T(8,128)(2,1)S(1)}, bf16[48,1024]{1,0:T(8,128)(2,1)S(1)}, u32[]{:S(2)}, u32[]{:S(2)}) collective-permute-start(bf16[48,1024]{1,0:T(8,128)(2,1)S(1)} %get-tuple-element.23), channel_id=1, source_target_pairs={{28,0},{0,4},{4,8},{8,12},{12,16},{16,20},{20,24},{24,28},{29,1},{... | collective-permute-start | bytes 294920 | tf_op jit(solution)/shard_map/ppermute | solution.py:361
  8.9 0.9 %collective-permute-start.3 = (bf16[48,1024]{1,0:T(8,128)(2,1)S(1)}, bf16[48,1024]{1,0:T(8,128)(2,1)S(1)}, u32[]{:S(2)}, u32[]{:S(2)}) collective-permute-start(bf16[48,1024]{1,0:T(8,128)(2,1)S(1)} %get-tuple-element.24), channel_id=1, source_target_pairs={{24,0},{28,4},{0,8},{4,12},{8,16},{12,20},{16,24},{20,28},{25,1},{... | collective-permute-start | bytes 294920 | tf_op jit(solution)/shard_map/ppermute | solution.py:361
  10.5 0.0 copy-start
  10.5 0.6 %copy-done = f32[1,4]{1,0:T(1,128)S(1)} copy-done((f32[1,4]{1,0:T(1,128)S(1)}, f32[1,4]{1,0:T(1,128)}, u32[]{:S(2)}) %copy-start) | copy-done | bytes 40
  11.2 0.0 copy-start.1
  11.2 3.6 %prepare.1 = (bf16[128,192]{1,0:T(8,128)(2,1)S(1)}, f32[64,1024]{1,0:T(8,128)S(1)}, bf16[1024,128]{1,0:T(8,128)(2,1)S(1)}, bf16[128,128]{1,0:T(8,128)(2,1)S(1)},...) custom-call(s32[8,2,65]{2,1,0:T(2,128)S(1)} %get-tuple-element.25.nbr_ref, ...), custom_call_target="tpu_custom_call" | custom-call | tf_op jit(solution)/shard_map/prepare/pallas_call | solution.py:366
  14.8 0.0 collective-permute-done.refs_0_
  14.8 0.0 collective-permute-done.1.refs_1_
  14.8 1.4 %collective-permute-done.2.refs_2_ = bf16[48,1024]{1,0:T(8,128)(2,1)S(1)} collective-permute-done((bf16[48,1024]{1,0:T(8,128)(2,1)S(1)}, bf16[48,1024]{1,0:T(8,128)(2,1)S(1)}, u32[]{:S(2)}, u32[]{:S(2)}) %collective-permute-start.2) | collective-permute-done | bytes 98336 | tf_op jit(solution)/shard_map/ppermute | solution.py:361
  16.2 0.0 collective-permute-done.3.refs_3_
  16.2 3.0 %finish.1 = f32[2,3136]{1,0:T(2,128)S(1)} custom-call(bf16[48,1024]{1,0:T(8,128)(2,1)S(1)} %collective-permute-done.refs_0_, bf16[48,1024]{1,0:T(8,128)(2,1)S(1)} %collective-permute-done.1.refs_1_, bf16[48,1024]{1,0:T(8,128)(2,1)S(1)} %collective-permute-done.2.refs_2_, bf16[48,1024]{1,0:T(8,128)(2,1)S(1)} %collective-permute-done.3.refs_3_, ...), custom_call_target="tpu_custom_call" | custom-call | tf_op jit(solution)/shard_map/finish/pallas_call | solution.py:389
  19.2 1.6 %collective-permute-start.5 = (f32[2,3136]{1,0:T(2,128)S(1)}, f32[2,3136]{1,0:T(2,128)S(1)}, u32[]{:S(2)}, u32[]{:S(2)}) collective-permute-start(f32[2,3136]{1,0:T(2,128)S(1)} %finish.1), channel_id=1, source_target_pairs={{0,2},{1,3},{2,0},{3,1},{4,6},{5,7},{6,4},{7,5},{8,10},{9,11},{10,... | collective-permute-start | bytes 75272 | tf_op jit(solution)/shard_map/ppermute | solution.py:326
  20.8 0.0 collective-permute-start.6
  20.8 0.6 %collective-permute-start.4 = (f32[2,3136]{1,0:T(2,128)S(1)}, f32[2,3136]{1,0:T(2,128)S(1)}, u32[]{:S(2)}, u32[]{:S(2)}) collective-permute-start(f32[2,3136]{1,0:T(2,128)S(1)} %finish.1), channel_id=1, source_target_pairs={{0,1},{1,0},{2,3},{3,2},{4,5},{5,4},{6,7},{7,6},{8,9},{9,8},{10,11... | collective-permute-start | bytes 75272 | tf_op jit(solution)/shard_map/ppermute | solution.py:326
  21.4 1.7 %collective-permute-done.5 = f32[2,3136]{1,0:T(2,128)S(1)} collective-permute-done((f32[2,3136]{1,0:T(2,128)S(1)}, f32[2,3136]{1,0:T(2,128)S(1)}, u32[]{:S(2)}, u32[]{:S(2)}) %collective-permute-start.5) | collective-permute-done | bytes 25120 | tf_op jit(solution)/shard_map/ppermute | solution.py:326
  23.1 0.9 %collective-permute-done.6 = f32[2,3136]{1,0:T(2,128)S(1)} collective-permute-done((f32[2,3136]{1,0:T(2,128)S(1)}, f32[2,3136]{1,0:T(2,128)S(1)}, u32[]{:S(2)}, u32[]{:S(2)}) %collective-permute-start.6) | collective-permute-done | bytes 25120 | tf_op jit(solution)/shard_map/ppermute | solution.py:326
  24.0 0.0 collective-permute-done.4
  24.0 0.0 copy-done.1
  24.0 0.7 %multiply_add_fusion = f32[2,3136]{1,0:T(2,128)} fusion(f32[2,3136]{1,0:T(2,128)S(1)} %collective-permute-done.5, f32[2,3136]{1,0:T(2,128)S(1)} %collective-permute-done.6, f32[2,3136]{1,0:T(2,128)S(1)} %finish.1, f32[2,3136]{1,0:T(2,128)S(1)} %collective-permute-done.4, f32[2,3136]{1,0:T(2,128)S(1)} %copy-done.1), kind=kLoop, calls=%fused_computation | loop fusion | flops 56448 | bytes 150528 | tf_op jit(solution)/shard_map/add | solution.py:399
Async XLA Ops:
  1.8 13.0 %collective-permute-start = (bf16[48,1024]{1,0:T(8,128)(2,1)S(1)}, bf16[48,1024]{1,0:T(8,128)(2,1)S(1)}, u32[]{:S(2)}, u32[]{:S(2)}) collective-permute-start(bf16[48,1024]{1,0:T(8,128)(2,1)S(1)} %get-tuple-element.21), channel_id=1, source_target_pairs={{8,0},{12,4},{16,8},{20,12},{24,16},{28,20},{0,24},{4,28},{9,1},{1... | collective-permute-start | bytes 294920 | tf_op jit(solution)/shard_map/ppermute | solution.py:361
  6.9 7.9 %collective-permute-start.1 = (bf16[48,1024]{1,0:T(8,128)(2,1)S(1)}, bf16[48,1024]{1,0:T(8,128)(2,1)S(1)}, u32[]{:S(2)}, u32[]{:S(2)}) collective-permute-start(bf16[48,1024]{1,0:T(8,128)(2,1)S(1)} %get-tuple-element.22), channel_id=1, source_target_pairs={{4,0},{8,4},{12,8},{16,12},{20,16},{24,20},{28,24},{0,28},{5,1},{9... | collective-permute-start | bytes 294920 | tf_op jit(solution)/shard_map/ppermute | solution.py:361
  8.3 8.0 %collective-permute-start.2 = (bf16[48,1024]{1,0:T(8,128)(2,1)S(1)}, bf16[48,1024]{1,0:T(8,128)(2,1)S(1)}, u32[]{:S(2)}, u32[]{:S(2)}) collective-permute-start(bf16[48,1024]{1,0:T(8,128)(2,1)S(1)} %get-tuple-element.23), channel_id=1, source_target_pairs={{28,0},{0,4},{4,8},{8,12},{12,16},{16,20},{20,24},{24,28},{29,1},{... | collective-permute-start | bytes 294920 | tf_op jit(solution)/shard_map/ppermute | solution.py:361
  8.9 7.3 %collective-permute-start.3 = (bf16[48,1024]{1,0:T(8,128)(2,1)S(1)}, bf16[48,1024]{1,0:T(8,128)(2,1)S(1)}, u32[]{:S(2)}, u32[]{:S(2)}) collective-permute-start(bf16[48,1024]{1,0:T(8,128)(2,1)S(1)} %get-tuple-element.24), channel_id=1, source_target_pairs={{24,0},{28,4},{0,8},{4,12},{8,16},{12,20},{16,24},{20,28},{25,1},{... | collective-permute-start | bytes 294920 | tf_op jit(solution)/shard_map/ppermute | solution.py:361
  10.5 0.7 %copy-start = (f32[1,4]{1,0:T(1,128)S(1)}, f32[1,4]{1,0:T(1,128)}, u32[]{:S(2)}) copy-start(f32[1,4]{1,0:T(1,128)} %phase_ref.1) | copy-start | bytes 52
  11.2 12.9 %copy-start.1 = (f32[2,3136]{1,0:T(2,128)S(1)}, f32[2,3136]{1,0:T(2,128)}, u32[]{:S(2)}) copy-start(f32[2,3136]{1,0:T(2,128)} %param.17) | copy-start | bytes 75268
  19.2 3.9 %collective-permute-start.5 = (f32[2,3136]{1,0:T(2,128)S(1)}, f32[2,3136]{1,0:T(2,128)S(1)}, u32[]{:S(2)}, u32[]{:S(2)}) collective-permute-start(f32[2,3136]{1,0:T(2,128)S(1)} %finish.1), channel_id=1, source_target_pairs={{0,2},{1,3},{2,0},{3,1},{4,6},{5,7},{6,4},{7,5},{8,10},{9,11},{10,... | collective-permute-start | bytes 75272 | tf_op jit(solution)/shard_map/ppermute | solution.py:326
  20.8 3.3 %collective-permute-start.6 = (f32[2,3136]{1,0:T(2,128)S(1)}, f32[2,3136]{1,0:T(2,128)S(1)}, u32[]{:S(2)}, u32[]{:S(2)}) collective-permute-start(f32[2,3136]{1,0:T(2,128)S(1)} %finish.1), channel_id=1, source_target_pairs={{0,3},{1,2},{2,1},{3,0},{4,7},{5,6},{6,5},{7,4},{8,11},{9,10},{10,... | collective-permute-start | bytes 75272 | tf_op jit(solution)/shard_map/ppermute | solution.py:326
  20.8 3.3 %collective-permute-start.4 = (f32[2,3136]{1,0:T(2,128)S(1)}, f32[2,3136]{1,0:T(2,128)S(1)}, u32[]{:S(2)}, u32[]{:S(2)}) collective-permute-start(f32[2,3136]{1,0:T(2,128)S(1)} %finish.1), channel_id=1, source_target_pairs={{0,1},{1,0},{2,3},{3,2},{4,5},{5,4},{6,7},{7,6},{8,9},{9,8},{10,11... | collective-permute-start | bytes 75272 | tf_op jit(solution)/shard_map/ppermute | solution.py:326

commit v3 on v2

--- a/solution.py
+++ b/solution.py
@@ -7,12 +7,14 @@
 from jax.experimental.pallas import tpu as pltpu
 from jax.sharding import PartitionSpec as P
 
+
 REACH = 2
 CAP = 48
 LIMIT = 24 << 20
 LANES = 128
 SUBS = 8
-OFFSETS = tuple(offset for offset in range(-REACH, REACH + 1) if offset != 0)
+SHIFTS = (1, 2, -2, -1)
+PARTS = (4,19)
 F32 = jnp.float32
 BF16 = jnp.bfloat16
 
@@ -79,13 +81,18 @@
 
 
 def pack_kernel(axis, inputs, *refs):
-    sources, refs = refs[:inputs], refs[inputs:]
-    kept, refs = refs[:inputs], refs[inputs:]
+    sources, radial_hbm, refs = refs[:inputs], refs[inputs], refs[inputs + 1 :]
+    kept, radial_ref, refs = refs[:inputs], refs[inputs], refs[inputs + 1 :]
     pack_refs, (pad_ref, sems) = refs[:-2], refs[-2:]
     copies = [
         pltpu.make_async_copy(source, ref, sems.at[k])
         for k, (source, ref) in enumerate(zip(sources, kept))
     ]
+    copies.append(
+        pltpu.make_async_copy(
+            radial_hbm.at[0 : radial_ref.shape[0]], radial_ref, sems.at[inputs]
+        )
+    )
     for copy in copies:
         copy.start()
     nbr_ref, table_ref, site_ref = kept[:3]
@@ -94,22 +101,23 @@
     me = lax.axis_index(axis)
     copies[0].wait()
     copies[1].wait()
-    atoms = load_lists(nbr_ref, pad_ref, [lax.rem(me + o + count, count) for o in OFFSETS])
+    atoms = load_lists(nbr_ref, pad_ref, [lax.rem(me + shift + count, count) for shift in SHIFTS])
     domain, local = resolve(atoms, table_ref, owned)
-    width = atoms.shape[1] // len(OFFSETS)
+    width = atoms.shape[1] // len(SHIFTS)
     mine = domain == me.astype(F32)
-    spans = [slice(k * width, (k + 1) * width) for k in range(len(OFFSETS))]
+    spans = [slice(k * width, (k + 1) * width) for k in range(len(SHIFTS))]
     hots = slot_hot([mine[:, s] for s in spans])
     rows = iota((owned, width), 0).astype(F32)
     chosen = [
         matmul(hot, ones_where(local[:, s] == rows), ((1,), (1,))).astype(BF16)
         for hot, s in zip(hots, spans)
     ]
-    for copy in copies[2:]:
+    for copy in copies[2:-1]:
         copy.wait()
     packed = matmul(jnp.concatenate(chosen, axis=0), site_ref[...]).astype(BF16)
     for k, pack_ref in enumerate(pack_refs):
         pack_ref[...] = packed[k * CAP : (k + 1) * CAP]
+    copies[-1].wait()
 
 
 def fold_matrix():
@@ -145,12 +153,14 @@
 
 
 def prepare_kernel(
-    axis,
+    axis, begin,
     nbr_ref, table_ref, site_ref, couple_ref, angular_ref, phase_ref, radial_hbm,
     slot_ref, own_ref, chain_ref, spread_ref, start_ref, centre_ref, radial_ref,
     pad_ref, scaled_ref, grid_ref, sem,
 ):
-    fetch = pltpu.make_async_copy(radial_hbm, radial_ref, sem)
+    fetch = pltpu.make_async_copy(
+        radial_hbm.at[begin : begin + radial_ref.shape[0]], radial_ref, sem
+    )
     fetch.start()
     count, zones, places = nbr_ref.shape
     owned = site_ref.shape[0]
@@ -161,13 +171,13 @@
     domain, local = resolve(atoms, table_ref, owned)
     width = atoms.shape[1]
     hots = slot_hot(
-        [domain == lax.rem(me - o + count, count).astype(F32) for o in OFFSETS]
+        [domain == lax.rem(me - shift + count, count).astype(F32) for shift in SHIFTS]
     )
     scaled_ref[...] = jnp.zeros(scaled_ref.shape, F32)
     lasts = [strided_row(couple_ref, z, places) for z in range(zones)]
     for z in range(zones):
         for q in range(terms):
-            phase = phase_ref[0, q]
+            phase = phase_ref[0:1, q : q + 1]
             for half, rows in enumerate((couple_ref[z, :, 0:places].astype(F32), lasts[z])):
                 row = (phase * rows[q : q + 1, 0:places]).astype(BF16)
                 at = half * zones * SUBS + z * SUBS + q
@@ -244,23 +254,22 @@
     side = sum(
         jnp.where(lane_term == q, tables[q * 32 : (q + 1) * 32], 0.0) for q in range(terms)
     ).astype(BF16)
-    row = iota((LANES, LANES), 0)
-    column = iota((LANES, LANES), 1) % 64
-    for low_row in range(4):
-        move = ones_where(
-            (row % 4 == low_row) & (column == ((row % 32) // 4) * SUBS + row // 32)
-        )
-        spread_ref[low_row * 32 : (low_row + 1) * 32, :] = matmul(side, move).astype(BF16)
+    row = iota((LANES, 2 * LANES), 0)
+    column = iota((LANES, 2 * LANES), 1)
+    same = (column % SUBS == row // 32) & ((column % 64) // SUBS == (row % 32) // 4)
+    for block in range(4):
+        move = ones_where(same & (row % 4 == (column // 64 + block) % 4))
+        spread_ref[block * 32 : (block + 1) * 32, :] = matmul(side, move).astype(BF16)
     fetch.wait()
 
 
-def finish_kernel(
-    piece_refs_count,
-    *refs,
-):
-    pieces = refs[:piece_refs_count]
-    (slot_ref, own_ref, chain_ref, spread_ref, start_ref, centre_ref, radial_ref, contour_ref,
-     out_ref, flat_ref) = refs[piece_refs_count:]
+def finish_kernel(count, *refs):
+    pieces, refs = refs[:count], refs[count:]
+    slot_ref, own_ref, chain_ref, spread_ref, start_ref, centre_ref, refs = *refs[:6], refs[6:]
+    radial_refs, (contour_ref, radial_hbm, out_ref, flat_ref, tail_ref, sem) = refs[:-6], refs[-6:]
+    begin = radial_hbm.shape[0] - tail_ref.shape[0]
+    fetch = pltpu.make_async_copy(radial_hbm.at[begin : radial_hbm.shape[0]], tail_ref, sem)
+    fetch.start()
     zones = out_ref.shape[0]
     near = jnp.concatenate([ref[...] for ref in pieces], axis=0)
     far = matmul(slot_ref[...], near)
@@ -269,9 +278,8 @@
     per_zone = size // zones
     terms = per_zone // SUBS
     groups = weights.shape[1] // LANES
-    diagonal = block_mask()
-    fold = fold_matrix()
-    flat_ref[...] = jnp.zeros(flat_ref.shape, F32)
+    rows = groups * SUBS
+    turned = []
     for z in range(zones):
         base = z * per_zone
         lhs = jnp.concatenate(
@@ -287,45 +295,57 @@
             ],
             axis=0,
         )
-        rows = groups * SUBS
         both = matmul(
             jnp.concatenate(split(lhs), axis=0),
             chain_ref[z * terms * LANES : (z + 1) * terms * LANES, :],
         )
         sums = both[:rows] + both[rows:] + start_ref[z * rows : (z + 1) * rows, :]
-        field = matmul(spread_ref[...], jnp.concatenate(split(sums), axis=0))
-        field = jnp.where(diagonal, field, 0.0)
-        field = field[0:32] + field[32:64] + field[64:96] + field[96:128]
-        both = matmul(jnp.concatenate(split(field), axis=0), fold)
-        field = (both[:32] + both[32:]).astype(BF16).astype(F32)
-        block = jnp.where(diagonal, jnp.concatenate([field] * 4, axis=0), 0.0).astype(BF16)
-        centre = centre_ref[z * groups : (z + 1) * groups, :]
-        central = centre + matmul(centre.astype(BF16), block)
+        turned.append(
+            jnp.concatenate(
+                [sums] + [pltpu.roll(sums, LANES - 32 * k, 1) for k in range(1, 4)], axis=0
+            )
+        )
+    high, low = split(jnp.concatenate(turned, axis=1))
+    spread = spread_ref[...]
+    field = matmul(spread, high) + matmul(spread, low)
+    diagonal = jnp.concatenate([block_mask()] * zones, axis=1)
+    field = jnp.where(diagonal, field, 0.0).astype(BF16)
+    centre = centre_ref[...]
+    change = matmul(centre.astype(BF16), field)
+    flat_ref[...] = jnp.zeros(flat_ref.shape, F32)
+    for z in range(zones):
+        span = slice(z * groups, (z + 1) * groups)
+        central = centre[span] + change[span, z * LANES : (z + 1) * LANES]
         for g in range(groups):
             flat_ref[z : z + 1, g * LANES : (g + 1) * LANES] = central[g : g + 1]
     central = flat_ref[...].astype(BF16)
-    out_ref[...] = contour_ref[0] * matmul(central, radial_ref[...], ((1,), (1,)))[:zones]
+    scale = contour_ref[0]
+    at = 0
+    for ref in (*radial_refs, tail_ref):
+        if ref is tail_ref:
+            fetch.wait()
+        part = scale * matmul(central, ref[...], ((1,), (1,)))
+        out_ref[:, at : at + ref.shape[0]] = part[:zones].astype(BF16)
+        at += ref.shape[0]
 
 
 def vmem():
     return pl.BlockSpec(memory_space=pltpu.VMEM)
-
-
-def smem():
-    return pl.BlockSpec(memory_space=pltpu.SMEM)
 
 
 def sum_over(value, axis):
     size = lax.axis_size(axis)
     if size & (size - 1):
-        return lax.psum(value, axis)
+        return lax.psum(value.astype(F32), axis)
     stride = 1
     while stride < size:
+        value = value.astype(BF16)
         radix = min(4, size // stride)
-        parts = [value] + [
-            lax.ppermute(value, axis, [(i, i ^ (stride * k)) for i in range(size)])
-            for k in range(1, radix)
-        ]
+        parts = {0: value}
+        for k in (3, 2, 1):
+            if k < radix:
+                parts[k] = lax.ppermute(value, axis, [(i, i ^ (stride * k)) for i in range(size)])
+        parts = [parts[k].astype(F32) for k in range(radix)]
         value = (parts[0] + parts[1]) + (parts[2] + parts[3]) if radix == 4 else parts[0] + parts[1]
         stride *= radix
     return value
@@ -340,41 +360,47 @@
     terms = angular.shape[0]
     atoms = owner_row.shape[0]
     assert owned <= 256 and count <= 256 and places <= LANES and zones == 2
+    assert count > 2 * REACH and sorted(SHIFTS) == [k for k in range(-REACH, REACH + 1) if k]
     assert width == 1024 and terms == 4 and atoms % LANES == 0 and places % 2 == 1
     table = owner_row.reshape(atoms // LANES, LANES)
-    sources = [neighbours, table, site, coupling, angular]
+    sources = [neighbours, table, site, coupling, angular, phases]
+    hbm = pl.BlockSpec(memory_space=pltpu.HBM)
+    params = pltpu.CompilerParams(vmem_limit_bytes=LIMIT)
+    turned = pltpu.with_memory_space_constraint(radial[0].T, pltpu.HBM)
+    parts = [PARTS[0] * LANES, PARTS[1] * LANES]
     results = pl.pallas_call(
         functools.partial(pack_kernel, "dom", len(sources)),
         out_shape=[pltpu.VMEM(x.shape, x.dtype) for x in sources]
-        + [pltpu.VMEM((CAP, width), BF16)] * len(OFFSETS),
-        in_specs=[pl.BlockSpec(memory_space=pltpu.HBM)] * len(sources),
-        out_specs=[vmem()] * (len(sources) + len(OFFSETS)),
+        + [pltpu.VMEM((parts[0], width), BF16)]
+        + [pltpu.VMEM((CAP, width), BF16)] * len(SHIFTS),
+        in_specs=[hbm] * (len(sources) + 1),
+        out_specs=[vmem()] * (len(sources) + 1 + len(SHIFTS)),
         scratch_shapes=[
-            pltpu.VMEM((len(OFFSETS) * zones, LANES), jnp.int32),
-            pltpu.SemaphoreType.DMA((len(sources),)),
+            pltpu.VMEM((len(SHIFTS) * zones, LANES), jnp.int32),
+            pltpu.SemaphoreType.DMA((len(sources) + 1,)),
         ],
-        compiler_params=pltpu.CompilerParams(vmem_limit_bytes=LIMIT),
+        compiler_params=params,
         name="pack",
-    )(*[pltpu.with_memory_space_constraint(x, pltpu.HBM) for x in sources])
-    kept, packs = results[: len(sources)], results[len(sources) :]
+    )(*[pltpu.with_memory_space_constraint(x, pltpu.HBM) for x in sources], turned)
+    kept, head, packs = results[: len(sources)], results[len(sources)], results[len(sources) + 1 :]
     pieces = [
-        lax.ppermute(pack, "dom", [((i - offset) % count, i) for i in range(count)])
-        for pack, offset in zip(packs, OFFSETS)
+        lax.ppermute(pack, "dom", [(i, (i + shift) % count) for i in range(count)])
+        for pack, shift in zip(packs, SHIFTS)
     ]
     size = zones * terms * SUBS
     groups = width // LANES
     prepared = pl.pallas_call(
-        functools.partial(prepare_kernel, "dom"),
+        functools.partial(prepare_kernel, "dom", parts[0]),
         out_shape=[
-            pltpu.VMEM((2 * size, CAP * len(OFFSETS)), BF16),
+            pltpu.VMEM((2 * size, CAP * len(SHIFTS)), BF16),
             pltpu.VMEM((size, width), F32),
             pltpu.VMEM((zones * terms * LANES, LANES), BF16),
-            pltpu.VMEM((LANES, LANES), BF16),
+            pltpu.VMEM((LANES, 2 * LANES), BF16),
             pltpu.VMEM((zones * groups * SUBS, LANES), F32),
             pltpu.VMEM((zones * groups, LANES), F32),
-            pltpu.VMEM((radial.shape[2], width), BF16),
+            pltpu.VMEM((parts[1], width), BF16),
         ],
-        in_specs=[vmem()] * 5 + [smem(), pl.BlockSpec(memory_space=pltpu.HBM)],
+        in_specs=[vmem()] * 6 + [hbm],
         out_specs=[vmem()] * 7,
         scratch_shapes=[
             pltpu.VMEM((zones, LANES), jnp.int32),
@@ -382,19 +408,24 @@
             pltpu.VMEM((groups, (terms + zones) * LANES), F32),
             pltpu.SemaphoreType.DMA,
         ],
-        compiler_params=pltpu.CompilerParams(vmem_limit_bytes=LIMIT),
+        compiler_params=params,
         name="prepare",
-    )(*kept, phases, pltpu.with_memory_space_constraint(radial[0].T, pltpu.HBM))
+    )(*kept, turned)
     pieces = [pltpu.with_memory_space_constraint(piece, pltpu.VMEM) for piece in pieces]
+    entries = radial.shape[2]
     part = pl.pallas_call(
         functools.partial(finish_kernel, len(pieces)),
-        out_shape=pltpu.VMEM((zones, radial.shape[2]), F32),
-        in_specs=[vmem()] * (len(pieces) + 7) + [smem()],
+        out_shape=pltpu.VMEM((zones, entries), BF16),
+        in_specs=[vmem()] * (len(pieces) + 8) + [pl.BlockSpec(memory_space=pltpu.SMEM), hbm],
         out_specs=vmem(),
-        scratch_shapes=[pltpu.VMEM((SUBS, width), F32)],
-        compiler_params=pltpu.CompilerParams(vmem_limit_bytes=LIMIT),
+        scratch_shapes=[
+            pltpu.VMEM((SUBS, width), F32),
+            pltpu.VMEM((entries - sum(parts), width), BF16),
+            pltpu.SemaphoreType.DMA,
+        ],
+        compiler_params=params,
         name="finish",
-    )(*pieces, *prepared, contour)
+    )(*pieces, *prepared[:-1], head, prepared[-1], contour, turned)
     density = sum_over(part, "en")
     return 0.5 * old_potential + 0.5 * density * lax.rsqrt(1.0 + density * density)
 

time: 24.9 us -> 21.9 us (0.88)
  Pallas kernels: 8.34 us -> 7.19 us
  waiting for transfers between devices: 4.07 us -> 3 us
  local copies, waits for them, and re-layouts: 0.65 us -> 0.01 us
    ppermute x4, waiting for transfers between devices: 1.43 us -> 0.01 us  [shards(): lax.ppermute(pack, 'dom', [(i, (i + shift) % count) for i in range(count)])]
    pallas_call x1, Pallas kernels: 3.63 us -> 2.63 us  [shards(): pl.pallas_call(functools.partial(prepare_kernel, 'dom', parts[0]), out_sh...]
    unnamed x4 -> x2, local copies, waits for them, and re-layouts: 0.65 us -> 0.01 us
    ppermute x3, waiting for transfers between devices: 2.64 us -> 2.99 us  [sum_over(): lax.ppermute(value, axis, [(i, i ^ stride * k) for i in range(size)])]
    ppermute x3, starting transfers between devices: 2.17 us -> 1.92 us  [sum_over(): lax.ppermute(value, axis, [(i, i ^ stride * k) for i in range(size)])]
  transfers between devices with their start and end apart: 7 -> 7, of which waited for: 3 -> 2; matrix products, arithmetic and copies ran while one was open for 0% -> 0% of each run, Pallas kernels for 15% -> 12%
where the time goes in v3:
time: 21.9 us; the launch traced here: 21.7 us
  starting transfers between devices  10.1 us (46%)
  Pallas kernels  7.19 us (33%)
  waiting for transfers between devices  3 us (14%)
  between operations  0.73 us (3%)
  other arithmetic  0.66 us (3%)
    ppermute x4, starting transfers between devices, shards(): lax.ppermute(pack, 'dom', [(i, (i + shift) % count) for i in range(count)])  8.15 us
    ppermute x3, waiting for transfers between devices, sum_over(): lax.ppermute(value, axis, [(i, i ^ stride * k) for i in range(size)])  2.99 us
    pallas_call x1, Pallas kernels, shards(): pl.pallas_call(functools.partial(finish_kernel, len(pieces)), out_shape=p...  2.79 us
    pallas_call x1, Pallas kernels, shards(): pl.pallas_call(functools.partial(prepare_kernel, 'dom', parts[0]), out_sh...  2.63 us
    ppermute x3, starting transfers between devices, sum_over(): lax.ppermute(value, axis, [(i, i ^ stride * k) for i in range(size)])  1.92 us
    pallas_call x1, Pallas kernels, shards(): pl.pallas_call(functools.partial(pack_kernel, 'dom', len(sources)), out_s...  1.77 us
    add x1, other arithmetic, shards(): 0.5 * old_potential + 0.5 * density * lax.rsqrt(1.0 + density * density)  0.66 us
  transfers between devices with their start and end apart: 7, of which 2 were waited for; matrix products, arithmetic and copies ran while one was open for 0% of the time, Pallas kernels for 12%

profile of v3, /device:TPU:0, one launch (start us, length us, event | category | flops | bytes accessed | tf_op | source)
XLA Modules:
  0.0 21.7 jit_solution(13584308727905622719)
XLA Ops:
  0.0 1.8 %pack.1 = (s32[8,2,65]{2,1,0:T(2,128)S(1)}, s32[16,128]{1,0:T(8,128)S(1)}, bf16[256,1024]{1,0:T(8,128)(2,1)S(1)}, bf16[2,4,4225]{2,1,0:T(4,128)(2,1)S(1)}, bf16[...) custom-call(s32[8,2,65]{2,1,0:T(2,128)} %refs_0_.1, ...), custom_call_target="tpu_custom_call" | custom-call | tf_op jit(solution)/shard_map/pack/pallas_call | solution.py:371
  1.8 3.0 %collective-permute-start = (bf16[48,1024]{1,0:T(8,128)(2,1)S(1)}, bf16[48,1024]{1,0:T(8,128)(2,1)S(1)}, u32[]{:S(2)}, u32[]{:S(2)}) collective-permute-start(bf16[48,1024]{1,0:T(8,128)(2,1)S(1)} %get-tuple-element.23), channel_id=1, source_target_pairs={{0,4},{4,8},{8,12},{12,16},{16,20},{20,24},{24,28},{28,0},{1,5},{5... | collective-permute-start | bytes 294920 | tf_op jit(solution)/shard_map/ppermute | solution.py:387
  4.8 1.6 %collective-permute-start.1 = (bf16[48,1024]{1,0:T(8,128)(2,1)S(1)}, bf16[48,1024]{1,0:T(8,128)(2,1)S(1)}, u32[]{:S(2)}, u32[]{:S(2)}) collective-permute-start(bf16[48,1024]{1,0:T(8,128)(2,1)S(1)} %get-tuple-element.24), channel_id=1, source_target_pairs={{0,8},{4,12},{8,16},{12,20},{16,24},{20,28},{24,0},{28,4},{1,9},{5... | collective-permute-start | bytes 294920 | tf_op jit(solution)/shard_map/ppermute | solution.py:387
  6.4 2.2 %collective-permute-start.2 = (bf16[48,1024]{1,0:T(8,128)(2,1)S(1)}, bf16[48,1024]{1,0:T(8,128)(2,1)S(1)}, u32[]{:S(2)}, u32[]{:S(2)}) collective-permute-start(bf16[48,1024]{1,0:T(8,128)(2,1)S(1)} %get-tuple-element.25), channel_id=1, source_target_pairs={{0,24},{4,28},{8,0},{12,4},{16,8},{20,12},{24,16},{28,20},{1,25},{... | collective-permute-start | bytes 294920 | tf_op jit(solution)/shard_map/ppermute | solution.py:387
  8.6 1.3 %collective-permute-start.3 = (bf16[48,1024]{1,0:T(8,128)(2,1)S(1)}, bf16[48,1024]{1,0:T(8,128)(2,1)S(1)}, u32[]{:S(2)}, u32[]{:S(2)}) collective-permute-start(bf16[48,1024]{1,0:T(8,128)(2,1)S(1)} %get-tuple-element.26), channel_id=1, source_target_pairs={{0,28},{4,0},{8,4},{12,8},{16,12},{20,16},{24,20},{28,24},{1,29},{... | collective-permute-start | bytes 294920 | tf_op jit(solution)/shard_map/ppermute | solution.py:387
  10.6 2.6 %prepare.1 = (bf16[128,192]{1,0:T(8,128)(2,1)S(1)}, f32[64,1024]{1,0:T(8,128)S(1)}, bf16[1024,128]{1,0:T(8,128)(2,1)S(1)}, bf16[128,256]{1,0:T(8,128)(2,1)S(1)},...) custom-call(s32[8,2,65]{2,1,0:T(2,128)S(1)} %get-tuple-element.27.nbr_ref, ...), custom_call_target="tpu_custom_call" | custom-call | tf_op jit(solution)/shard_map/prepare/pallas_call | solution.py:392
  13.2 0.0 collective-permute-done.refs_0_
  13.2 0.0 collective-permute-done.1.refs_1_
  13.2 0.0 collective-permute-done.2.refs_2_
  13.2 0.0 collective-permute-done.3.refs_3_
  13.3 0.0 copy-start
  13.3 2.8 %finish.1 = bf16[2,3136]{1,0:T(2,128)(2,1)S(1)} custom-call(bf16[48,1024]{1,0:T(8,128)(2,1)S(1)} %collective-permute-done.refs_0_, bf16[48,1024]{1,0:T(8,128)(2,1)S(1)} %collective-permute-done.1.refs_1_, bf16[48,1024]{1,0:T(8,128)(2,1)S(1)} %collective-permute-done.2.refs_2_, bf16[48,1024]{1,0:T(8,128)(2,1)S(1)} %collective-permute-done.3.refs_3_, ...), custom_call_target="tpu_custom_call" | custom-call | tf_op jit(solution)/shard_map/finish/pallas_call | solution.py:416
  16.1 0.1 collective-permute-start.4
  16.2 1.7 %collective-permute-start.5 = (bf16[2,3136]{1,0:T(2,128)(2,1)S(1)}, bf16[2,3136]{1,0:T(2,128)(2,1)S(1)}, u32[]{:S(2)}, u32[]{:S(2)}) collective-permute-start(bf16[2,3136]{1,0:T(2,128)(2,1)S(1)} %finish.1), channel_id=1, source_target_pairs={{0,2},{1,3},{2,0},{3,1},{4,6},{5,7},{6,4},{7,5},{8,10},{9,11},{10,... | collective-permute-start | bytes 37640 | tf_op jit(solution)/shard_map/ppermute | solution.py:347
  17.9 0.1 collective-permute-start.6
  18.0 0.0 collective-permute-done.4
  18.0 1.9 %collective-permute-done.5 = bf16[2,3136]{1,0:T(2,128)(2,1)S(1)} collective-permute-done((bf16[2,3136]{1,0:T(2,128)(2,1)S(1)}, bf16[2,3136]{1,0:T(2,128)(2,1)S(1)}, u32[]{:S(2)}, u32[]{:S(2)}) %collective-permute-start.5) | collective-permute-done | bytes 12576 | tf_op jit(solution)/shard_map/ppermute | solution.py:347
  19.9 1.1 %collective-permute-done.6 = bf16[2,3136]{1,0:T(2,128)(2,1)S(1)} collective-permute-done((bf16[2,3136]{1,0:T(2,128)(2,1)S(1)}, bf16[2,3136]{1,0:T(2,128)(2,1)S(1)}, u32[]{:S(2)}, u32[]{:S(2)}) %collective-permute-start.6) | collective-permute-done | bytes 12576 | tf_op jit(solution)/shard_map/ppermute | solution.py:347
  21.0 0.0 copy-done
  21.0 0.7 %multiply_add_fusion = f32[2,3136]{1,0:T(2,128)} fusion(bf16[2,3136]{1,0:T(2,128)(2,1)S(1)} %collective-permute-done.6, bf16[2,3136]{1,0:T(2,128)(2,1)S(1)} %collective-permute-done.5, bf16[2,3136]{1,0:T(2,128)(2,1)S(1)} %collective-permute-done.4, bf16[2,3136]{1,0:T(2,128)(2,1)S(1)} %finish.1, f32[2,3136]{1,0:T(2,128)S(1)} %copy-done), kind=kLoop, calls=%fused_computation | loop fusion | flops 81536 | bytes 100352 | tf_op jit(solution)/shard_map/add | solution.py:430
Async XLA Ops:
  1.8 11.4 %collective-permute-start = (bf16[48,1024]{1,0:T(8,128)(2,1)S(1)}, bf16[48,1024]{1,0:T(8,128)(2,1)S(1)}, u32[]{:S(2)}, u32[]{:S(2)}) collective-permute-start(bf16[48,1024]{1,0:T(8,128)(2,1)S(1)} %get-tuple-element.23), channel_id=1, source_target_pairs={{0,4},{4,8},{8,12},{12,16},{16,20},{20,24},{24,28},{28,0},{1,5},{5... | collective-permute-start | bytes 294920 | tf_op jit(solution)/shard_map/ppermute | solution.py:387
  4.8 8.4 %collective-permute-start.1 = (bf16[48,1024]{1,0:T(8,128)(2,1)S(1)}, bf16[48,1024]{1,0:T(8,128)(2,1)S(1)}, u32[]{:S(2)}, u32[]{:S(2)}) collective-permute-start(bf16[48,1024]{1,0:T(8,128)(2,1)S(1)} %get-tuple-element.24), channel_id=1, source_target_pairs={{0,8},{4,12},{8,16},{12,20},{16,24},{20,28},{24,0},{28,4},{1,9},{5... | collective-permute-start | bytes 294920 | tf_op jit(solution)/shard_map/ppermute | solution.py:387
  6.4 6.9 %collective-permute-start.2 = (bf16[48,1024]{1,0:T(8,128)(2,1)S(1)}, bf16[48,1024]{1,0:T(8,128)(2,1)S(1)}, u32[]{:S(2)}, u32[]{:S(2)}) collective-permute-start(bf16[48,1024]{1,0:T(8,128)(2,1)S(1)} %get-tuple-element.25), channel_id=1, source_target_pairs={{0,24},{4,28},{8,0},{12,4},{16,8},{20,12},{24,16},{28,20},{1,25},{... | collective-permute-start | bytes 294920 | tf_op jit(solution)/shard_map/ppermute | solution.py:387
  8.6 4.6 %collective-permute-start.3 = (bf16[48,1024]{1,0:T(8,128)(2,1)S(1)}, bf16[48,1024]{1,0:T(8,128)(2,1)S(1)}, u32[]{:S(2)}, u32[]{:S(2)}) collective-permute-start(bf16[48,1024]{1,0:T(8,128)(2,1)S(1)} %get-tuple-element.26), channel_id=1, source_target_pairs={{0,28},{4,0},{8,4},{12,8},{16,12},{20,16},{24,20},{28,24},{1,29},{... | collective-permute-start | bytes 294920 | tf_op jit(solution)/shard_map/ppermute | solution.py:387
  13.3 7.7 %copy-start = (f32[2,3136]{1,0:T(2,128)S(1)}, f32[2,3136]{1,0:T(2,128)}, u32[]{:S(2)}) copy-start(f32[2,3136]{1,0:T(2,128)} %param.17) | copy-start | bytes 75268
  16.1 1.9 %collective-permute-start.4 = (bf16[2,3136]{1,0:T(2,128)(2,1)S(1)}, bf16[2,3136]{1,0:T(2,128)(2,1)S(1)}, u32[]{:S(2)}, u32[]{:S(2)}) collective-permute-start(bf16[2,3136]{1,0:T(2,128)(2,1)S(1)} %finish.1), channel_id=1, source_target_pairs={{0,1},{1,0},{2,3},{3,2},{4,5},{5,4},{6,7},{7,6},{8,9},{9,8},{10,11... | collective-permute-start | bytes 37640 | tf_op jit(solution)/shard_map/ppermute | solution.py:347
  16.2 3.8 %collective-permute-start.5 = (bf16[2,3136]{1,0:T(2,128)(2,1)S(1)}, bf16[2,3136]{1,0:T(2,128)(2,1)S(1)}, u32[]{:S(2)}, u32[]{:S(2)}) collective-permute-start(bf16[2,3136]{1,0:T(2,128)(2,1)S(1)} %finish.1), channel_id=1, source_target_pairs={{0,2},{1,3},{2,0},{3,1},{4,6},{5,7},{6,4},{7,5},{8,10},{9,11},{10,... | collective-permute-start | bytes 37640 | tf_op jit(solution)/shard_map/ppermute | solution.py:347
  17.9 3.1 %collective-permute-start.6 = (bf16[2,3136]{1,0:T(2,128)(2,1)S(1)}, bf16[2,3136]{1,0:T(2,128)(2,1)S(1)}, u32[]{:S(2)}, u32[]{:S(2)}) collective-permute-start(bf16[2,3136]{1,0:T(2,128)(2,1)S(1)} %finish.1), channel_id=1, source_target_pairs={{0,3},{1,2},{2,1},{3,0},{4,7},{5,6},{6,5},{7,4},{8,11},{9,10},{10,... | collective-permute-start | bytes 37640 | tf_op jit(solution)/shard_map/ppermute | solution.py:347

commit v4 on v3

--- a/solution.py
+++ b/solution.py
@@ -14,7 +14,7 @@
 LANES = 128
 SUBS = 8
 SHIFTS = (1, 2, -2, -1)
-PARTS = (4,19)
+HEAD = 6
 F32 = jnp.float32
 BF16 = jnp.bfloat16
 
@@ -48,21 +48,25 @@
 
 def resolve(atoms, table_ref, owned):
     table = table_ref[...]
+    height = table.shape[0]
+    both = jnp.concatenate([table & ~255, table & 255], axis=0).astype(F32)
+    both = jnp.concatenate(
+        [both] + [pltpu.roll(both, LANES - 32 * k, 1) for k in range(1, 4)], axis=0
+    )[:, :32].astype(BF16)
+    width = atoms.shape[1]
+    key = ((atoms >> 5) & 3) * height + (atoms >> 7)
+    hots = []
+    for k in range(4):
+        hot = jnp.where(iota((height, width), 0) + k * height == key, 1.0, 0.0)
+        hots += [hot, hot]
+    picked = matmul(both, jnp.concatenate(hots, axis=0).astype(BF16), ((0,), (0,)))
+    lane_hot = iota((32, width), 0) == (atoms & 31)
+    found = jnp.sum(jnp.where(lane_hot, picked, 0.0), axis=0, keepdims=True).astype(jnp.int32)
     if owned & (owned - 1) == 0:
-        shift = owned.bit_length() - 1
-        domain, local = table >> shift, table & (owned - 1)
+        domain, local = found >> (owned.bit_length() - 1), found & (owned - 1)
     else:
-        domain, local = table // owned, table % owned
-    both = jnp.concatenate([domain, local], axis=1).astype(F32).astype(BF16)
-    width = atoms.shape[1]
-    row_hot = ones_where(iota((table.shape[0], width), 0) == (atoms >> 7))
-    picked = matmul(both, row_hot, ((0,), (0,)))
-    lane_hot = iota((LANES, width), 0) == (atoms & (LANES - 1))
-    found = [
-        jnp.sum(jnp.where(lane_hot, picked[i * LANES : (i + 1) * LANES], 0.0), axis=0, keepdims=True)
-        for i in range(2)
-    ]
-    return jnp.where(atoms < 0, -1.0, found[0]), found[1]
+        domain, local = found // owned, found % owned
+    return jnp.where(atoms < 0, -1, domain), local
 
 
 def slot_hot(masks):
@@ -104,10 +108,10 @@
     atoms = load_lists(nbr_ref, pad_ref, [lax.rem(me + shift + count, count) for shift in SHIFTS])
     domain, local = resolve(atoms, table_ref, owned)
     width = atoms.shape[1] // len(SHIFTS)
-    mine = domain == me.astype(F32)
+    mine = domain == me
     spans = [slice(k * width, (k + 1) * width) for k in range(len(SHIFTS))]
     hots = slot_hot([mine[:, s] for s in spans])
-    rows = iota((owned, width), 0).astype(F32)
+    rows = iota((owned, width), 0)
     chosen = [
         matmul(hot, ones_where(local[:, s] == rows), ((1,), (1,))).astype(BF16)
         for hot, s in zip(hots, spans)
@@ -154,8 +158,8 @@
 
 def prepare_kernel(
     axis, begin,
-    nbr_ref, table_ref, site_ref, couple_ref, angular_ref, phase_ref, radial_hbm,
-    slot_ref, own_ref, chain_ref, spread_ref, start_ref, centre_ref, radial_ref,
+    nbr_ref, table_ref, site_ref, couple_ref, angular_ref, phase_ref, head_ref, radial_hbm,
+    slot_ref, own_ref, chain_ref, spread_ref, start_ref, centre_ref, turned_ref, radial_ref,
     pad_ref, scaled_ref, grid_ref, sem,
 ):
     fetch = pltpu.make_async_copy(
@@ -171,7 +175,7 @@
     domain, local = resolve(atoms, table_ref, owned)
     width = atoms.shape[1]
     hots = slot_hot(
-        [domain == lax.rem(me - shift + count, count).astype(F32) for shift in SHIFTS]
+        [domain == lax.rem(me - shift + count, count) for shift in SHIFTS]
     )
     scaled_ref[...] = jnp.zeros(scaled_ref.shape, F32)
     lasts = [strided_row(couple_ref, z, places) for z in range(zones)]
@@ -201,7 +205,7 @@
         iota((2 * SUBS, width), 1) == iota((2 * SUBS, width), 0) * LANES
     )
     own_hot = ones_where(
-        (local == iota((owned, width), 0).astype(F32)) & (domain == me.astype(F32))
+        (local == iota((owned, width), 0)) & (domain == me)
     )
     own_coefs = matmul(jnp.concatenate([both, centres], axis=0), own_hot, ((1,), (1,)))
     own = matmul(own_coefs.astype(BF16), site_ref[...])
@@ -254,22 +258,34 @@
     side = sum(
         jnp.where(lane_term == q, tables[q * 32 : (q + 1) * 32], 0.0) for q in range(terms)
     ).astype(BF16)
+    order = ones_where(
+        iota((32, 32), 1) == (iota((32, 32), 0) % groups) * 4 + iota((32, 32), 0) // groups
+    )
+    mixed = []
+    for z in range(zones):
+        block = tiled[(terms + z) * 32 : (terms + z + 1) * 32].astype(BF16)
+        sorted_rows = matmul(order, block).astype(BF16)
+        mixed += split(matmul(sorted_rows[:, :32], side))
     row = iota((LANES, 2 * LANES), 0)
     column = iota((LANES, 2 * LANES), 1)
     same = (column % SUBS == row // 32) & ((column % 64) // SUBS == (row % 32) // 4)
     for block in range(4):
         move = ones_where(same & (row % 4 == (column // 64 + block) % 4))
-        spread_ref[block * 32 : (block + 1) * 32, :] = matmul(side, move).astype(BF16)
+        rows = jnp.concatenate(
+            [x[block * groups : (block + 1) * groups].astype(F32) for x in mixed], axis=0
+        ).astype(BF16)
+        moved = matmul(rows, move)
+        for k in range(2 * zones):
+            at = k * 4 * groups + block * groups
+            spread_ref[at : at + groups, :] = moved[k * groups : (k + 1) * groups]
+    turned_ref[...] = head_ref[...].T
     fetch.wait()
 
 
 def finish_kernel(count, *refs):
     pieces, refs = refs[:count], refs[count:]
     slot_ref, own_ref, chain_ref, spread_ref, start_ref, centre_ref, refs = *refs[:6], refs[6:]
-    radial_refs, (contour_ref, radial_hbm, out_ref, flat_ref, tail_ref, sem) = refs[:-6], refs[-6:]
-    begin = radial_hbm.shape[0] - tail_ref.shape[0]
-    fetch = pltpu.make_async_copy(radial_hbm.at[begin : radial_hbm.shape[0]], tail_ref, sem)
-    fetch.start()
+    radial_refs, (contour_ref, out_ref, flat_ref) = refs[:-3], refs[-3:]
     zones = out_ref.shape[0]
     near = jnp.concatenate([ref[...] for ref in pieces], axis=0)
     far = matmul(slot_ref[...], near)
@@ -279,7 +295,7 @@
     terms = per_zone // SUBS
     groups = weights.shape[1] // LANES
     rows = groups * SUBS
-    turned = []
+    flat_ref[...] = jnp.zeros(flat_ref.shape, F32)
     for z in range(zones):
         base = z * per_zone
         lhs = jnp.concatenate(
@@ -300,33 +316,27 @@
             chain_ref[z * terms * LANES : (z + 1) * terms * LANES, :],
         )
         sums = both[:rows] + both[rows:] + start_ref[z * rows : (z + 1) * rows, :]
-        turned.append(
-            jnp.concatenate(
-                [sums] + [pltpu.roll(sums, LANES - 32 * k, 1) for k in range(1, 4)], axis=0
-            )
-        )
-    high, low = split(jnp.concatenate(turned, axis=1))
-    spread = spread_ref[...]
-    field = matmul(spread, high) + matmul(spread, low)
-    diagonal = jnp.concatenate([block_mask()] * zones, axis=1)
-    field = jnp.where(diagonal, field, 0.0).astype(BF16)
-    centre = centre_ref[...]
-    change = matmul(centre.astype(BF16), field)
-    flat_ref[...] = jnp.zeros(flat_ref.shape, F32)
-    for z in range(zones):
-        span = slice(z * groups, (z + 1) * groups)
-        central = centre[span] + change[span, z * LANES : (z + 1) * LANES]
+        turned = jnp.concatenate(
+            [sums] + [pltpu.roll(sums, LANES - 32 * k, 1) for k in range(1, 4)], axis=0
+        )
+        spread = spread_ref[2 * z * 4 * groups : 2 * (z + 1) * 4 * groups, :].astype(BF16)
+        change = matmul(spread, jnp.concatenate(split(turned), axis=1))
+        change = change[:, :LANES] + change[:, LANES:]
+        change = change[: 4 * groups] + change[4 * groups :]
+        own_lanes = iota(change.shape, 0) // groups == iota(change.shape, 1) // 32
+        change = jnp.where(own_lanes, change, 0.0)
+        central = centre_ref[z * groups : (z + 1) * groups, :]
+        for block in range(4):
+            central = central + change[block * groups : (block + 1) * groups]
         for g in range(groups):
             flat_ref[z : z + 1, g * LANES : (g + 1) * LANES] = central[g : g + 1]
     central = flat_ref[...].astype(BF16)
     scale = contour_ref[0]
     at = 0
-    for ref in (*radial_refs, tail_ref):
-        if ref is tail_ref:
-            fetch.wait()
-        part = scale * matmul(central, ref[...], ((1,), (1,)))
-        out_ref[:, at : at + ref.shape[0]] = part[:zones].astype(BF16)
-        at += ref.shape[0]
+    for ref, side in zip(radial_refs, (0, 1)):
+        part = scale * matmul(central, ref[...], ((1,), (side,)))
+        out_ref[:, at : at + part.shape[1]] = part[:zones].astype(BF16)
+        at += part.shape[1]
 
 
 def vmem():
@@ -355,11 +365,11 @@
     single_site, coupling, angular, phases, contour, radial, neighbours, owner_row, old_potential
 ):
     site = single_site[0]
-    owned, width = site.shape
+    _, width = site.shape
     count, zones, places = neighbours.shape
     terms = angular.shape[0]
     atoms = owner_row.shape[0]
-    assert owned <= 256 and count <= 256 and places <= LANES and zones == 2
+    assert atoms <= 65536 and places <= LANES and zones == 2
     assert count > 2 * REACH and sorted(SHIFTS) == [k for k in range(-REACH, REACH + 1) if k]
     assert width == 1024 and terms == 4 and atoms % LANES == 0 and places % 2 == 1
     table = owner_row.reshape(atoms // LANES, LANES)
@@ -367,7 +377,7 @@
     hbm = pl.BlockSpec(memory_space=pltpu.HBM)
     params = pltpu.CompilerParams(vmem_limit_bytes=LIMIT)
     turned = pltpu.with_memory_space_constraint(radial[0].T, pltpu.HBM)
-    parts = [PARTS[0] * LANES, PARTS[1] * LANES]
+    parts = [HEAD * LANES, radial.shape[2] - HEAD * LANES]
     results = pl.pallas_call(
         functools.partial(pack_kernel, "dom", len(sources)),
         out_shape=[pltpu.VMEM(x.shape, x.dtype) for x in sources]
@@ -395,13 +405,14 @@
             pltpu.VMEM((2 * size, CAP * len(SHIFTS)), BF16),
             pltpu.VMEM((size, width), F32),
             pltpu.VMEM((zones * terms * LANES, LANES), BF16),
-            pltpu.VMEM((LANES, 2 * LANES), BF16),
+            pltpu.VMEM((2 * zones * 4 * groups, 2 * LANES), F32),
             pltpu.VMEM((zones * groups * SUBS, LANES), F32),
             pltpu.VMEM((zones * groups, LANES), F32),
+            pltpu.VMEM((width, parts[0]), BF16),
             pltpu.VMEM((parts[1], width), BF16),
         ],
-        in_specs=[vmem()] * 6 + [hbm],
-        out_specs=[vmem()] * 7,
+        in_specs=[vmem()] * 7 + [hbm],
+        out_specs=[vmem()] * 8,
         scratch_shapes=[
             pltpu.VMEM((zones, LANES), jnp.int32),
             pltpu.VMEM((2 * zones * SUBS, LANES), F32),
@@ -410,22 +421,20 @@
         ],
         compiler_params=params,
         name="prepare",
-    )(*kept, turned)
+    )(*kept, head, turned)
     pieces = [pltpu.with_memory_space_constraint(piece, pltpu.VMEM) for piece in pieces]
     entries = radial.shape[2]
     part = pl.pallas_call(
         functools.partial(finish_kernel, len(pieces)),
         out_shape=pltpu.VMEM((zones, entries), BF16),
-        in_specs=[vmem()] * (len(pieces) + 8) + [pl.BlockSpec(memory_space=pltpu.SMEM), hbm],
+        in_specs=[vmem()] * (len(pieces) + 8) + [pl.BlockSpec(memory_space=pltpu.SMEM)],
         out_specs=vmem(),
         scratch_shapes=[
             pltpu.VMEM((SUBS, width), F32),
-            pltpu.VMEM((entries - sum(parts), width), BF16),
-            pltpu.SemaphoreType.DMA,
         ],
         compiler_params=params,
         name="finish",
-    )(*pieces, *prepared[:-1], head, prepared[-1], contour, turned)
+    )(*pieces, *prepared, contour)
     density = sum_over(part, "en")
     return 0.5 * old_potential + 0.5 * density * lax.rsqrt(1.0 + density * density)
 

time: 21.9 us -> 20.9 us (0.954)
  the two profiles are of different devices: /device:TPU:0 before, /device:TPU:3 now
where the time goes in v4:
time: 20.9 us; the launch traced here: 20.7 us
  starting transfers between devices  7.53 us (36%)
  Pallas kernels  6.59 us (32%)
  waiting for transfers between devices  5.2 us (25%)
  between operations  0.69 us (3%)
  other arithmetic  0.67 us (3%)
    ppermute x4, starting transfers between devices, shards(): lax.ppermute(pack, 'dom', [(i, (i + shift) % count) for i in range(count)])  4.84 us
    ppermute x4, waiting for transfers between devices, shards(): lax.ppermute(pack, 'dom', [(i, (i + shift) % count) for i in range(count)])  2.92 us
    ppermute x3, starting transfers between devices, sum_over(): lax.ppermute(value, axis, [(i, i ^ stride * k) for i in range(size)])  2.68 us
    pallas_call x1, Pallas kernels, shards(): pl.pallas_call(functools.partial(finish_kernel, len(pieces)), out_shape=p...  2.47 us
    pallas_call x1, Pallas kernels, shards(): pl.pallas_call(functools.partial(prepare_kernel, 'dom', parts[0]), out_sh...  2.4 us
    ppermute x3, waiting for transfers between devices, sum_over(): lax.ppermute(value, axis, [(i, i ^ stride * k) for i in range(size)])  2.28 us
    pallas_call x1, Pallas kernels, shards(): pl.pallas_call(functools.partial(pack_kernel, 'dom', len(sources)), out_s...  1.72 us
    add x1, other arithmetic, shards(): 0.5 * old_potential + 0.5 * density * lax.rsqrt(1.0 + density * density)  0.67 us
  transfers between devices with their start and end apart: 7, of which 4 were waited for; matrix products, arithmetic and copies ran while one was open for 0% of the time, Pallas kernels for 12%

profile of v4, /device:TPU:3, one launch (start us, length us, event | category | flops | bytes accessed | tf_op | source)
XLA Modules:
  0.0 20.7 jit_solution(4255086694752532947)
XLA Ops:
  0.0 1.7 %pack.1 = (s32[8,2,65]{2,1,0:T(2,128)S(1)}, s32[16,128]{1,0:T(8,128)S(1)}, bf16[256,1024]{1,0:T(8,128)(2,1)S(1)}, bf16[2,4,4225]{2,1,0:T(4,128)(2,1)S(1)}, bf16[...) custom-call(s32[8,2,65]{2,1,0:T(2,128)} %refs_0_.1, ...), custom_call_target="tpu_custom_call" | custom-call | tf_op jit(solution)/shard_map/pack/pallas_call | solution.py:381
  1.7 1.3 %collective-permute-start = (bf16[48,1024]{1,0:T(8,128)(2,1)S(1)}, bf16[48,1024]{1,0:T(8,128)(2,1)S(1)}, u32[]{:S(2)}, u32[]{:S(2)}) collective-permute-start(bf16[48,1024]{1,0:T(8,128)(2,1)S(1)} %get-tuple-element.24), channel_id=1, source_target_pairs={{0,4},{4,8},{8,12},{12,16},{16,20},{20,24},{24,28},{28,0},{1,5},{5... | collective-permute-start | bytes 294920 | tf_op jit(solution)/shard_map/ppermute | solution.py:397
  3.0 1.3 %collective-permute-start.1 = (bf16[48,1024]{1,0:T(8,128)(2,1)S(1)}, bf16[48,1024]{1,0:T(8,128)(2,1)S(1)}, u32[]{:S(2)}, u32[]{:S(2)}) collective-permute-start(bf16[48,1024]{1,0:T(8,128)(2,1)S(1)} %get-tuple-element.25), channel_id=1, source_target_pairs={{0,8},{4,12},{8,16},{12,20},{16,24},{20,28},{24,0},{28,4},{1,9},{5... | collective-permute-start | bytes 294920 | tf_op jit(solution)/shard_map/ppermute | solution.py:397
  4.3 2.0 %collective-permute-start.2 = (bf16[48,1024]{1,0:T(8,128)(2,1)S(1)}, bf16[48,1024]{1,0:T(8,128)(2,1)S(1)}, u32[]{:S(2)}, u32[]{:S(2)}) collective-permute-start(bf16[48,1024]{1,0:T(8,128)(2,1)S(1)} %get-tuple-element.26), channel_id=1, source_target_pairs={{0,24},{4,28},{8,0},{12,4},{16,8},{20,12},{24,16},{28,20},{1,25},{... | collective-permute-start | bytes 294920 | tf_op jit(solution)/shard_map/ppermute | solution.py:397
  6.3 0.3 %collective-permute-start.3 = (bf16[48,1024]{1,0:T(8,128)(2,1)S(1)}, bf16[48,1024]{1,0:T(8,128)(2,1)S(1)}, u32[]{:S(2)}, u32[]{:S(2)}) collective-permute-start(bf16[48,1024]{1,0:T(8,128)(2,1)S(1)} %get-tuple-element.27), channel_id=1, source_target_pairs={{0,28},{4,0},{8,4},{12,8},{16,12},{20,16},{24,20},{28,24},{1,29},{... | collective-permute-start | bytes 294920 | tf_op jit(solution)/shard_map/ppermute | solution.py:397
  7.2 2.4 %prepare.1 = (bf16[128,192]{1,0:T(8,128)(2,1)S(1)}, f32[64,1024]{1,0:T(8,128)S(1)}, bf16[1024,128]{1,0:T(8,128)(2,1)S(1)}, f32[128,256]{1,0:T(8,128)S(1)}, f32[1...) custom-call(s32[8,2,65]{2,1,0:T(2,128)S(1)} %get-tuple-element.28.nbr, ...), custom_call_target="tpu_custom_call" | custom-call | tf_op jit(solution)/shard_map/prepare/pallas_call | solution.py:402
  9.6 0.0 copy-start
  9.6 0.0 collective-permute-done.refs_0_
  9.7 0.1 collective-permute-done.1.refs_1_
  9.7 2.8 %collective-permute-done.2.refs_2_ = bf16[48,1024]{1,0:T(8,128)(2,1)S(1)} collective-permute-done((bf16[48,1024]{1,0:T(8,128)(2,1)S(1)}, bf16[48,1024]{1,0:T(8,128)(2,1)S(1)}, u32[]{:S(2)}, u32[]{:S(2)}) %collective-permute-start.2) | collective-permute-done | bytes 98336 | tf_op jit(solution)/shard_map/ppermute | solution.py:397
  12.6 0.0 collective-permute-done.3.refs_3_
  12.6 2.5 %finish.1 = bf16[2,3136]{1,0:T(2,128)(2,1)S(1)} custom-call(bf16[48,1024]{1,0:T(8,128)(2,1)S(1)} %collective-permute-done.refs_0_, bf16[48,1024]{1,0:T(8,128)(2,1)S(1)} %collective-permute-done.1.refs_1_, bf16[48,1024]{1,0:T(8,128)(2,1)S(1)} %collective-permute-done.2.refs_2_, bf16[48,1024]{1,0:T(8,128)(2,1)S(1)} %collective-permute-done.3.refs_3_, ...), custom_call_target="tpu_custom_call" | custom-call | tf_op jit(solution)/shard_map/finish/pallas_call | solution.py:427
  15.0 2.3 %collective-permute-start.6 = (bf16[2,3136]{1,0:T(2,128)(2,1)S(1)}, bf16[2,3136]{1,0:T(2,128)(2,1)S(1)}, u32[]{:S(2)}, u32[]{:S(2)}) collective-permute-start(bf16[2,3136]{1,0:T(2,128)(2,1)S(1)} %finish.1), channel_id=1, source_target_pairs={{0,3},{1,2},{2,1},{3,0},{4,7},{5,6},{6,5},{7,4},{8,11},{9,10},{10,... | collective-permute-start | bytes 37640 | tf_op jit(solution)/shard_map/ppermute | solution.py:357
  17.3 0.2 %collective-permute-start.5 = (bf16[2,3136]{1,0:T(2,128)(2,1)S(1)}, bf16[2,3136]{1,0:T(2,128)(2,1)S(1)}, u32[]{:S(2)}, u32[]{:S(2)}) collective-permute-start(bf16[2,3136]{1,0:T(2,128)(2,1)S(1)} %finish.1), channel_id=1, source_target_pairs={{0,2},{1,3},{2,0},{3,1},{4,6},{5,7},{6,4},{7,5},{8,10},{9,11},{10,... | collective-permute-start | bytes 37640 | tf_op jit(solution)/shard_map/ppermute | solution.py:357
  17.5 0.2 collective-permute-start.4
  17.7 1.2 %collective-permute-done.6 = bf16[2,3136]{1,0:T(2,128)(2,1)S(1)} collective-permute-done((bf16[2,3136]{1,0:T(2,128)(2,1)S(1)}, bf16[2,3136]{1,0:T(2,128)(2,1)S(1)}, u32[]{:S(2)}, u32[]{:S(2)}) %collective-permute-start.6) | collective-permute-done | bytes 12576 | tf_op jit(solution)/shard_map/ppermute | solution.py:357
  19.0 1.0 %collective-permute-done.5 = bf16[2,3136]{1,0:T(2,128)(2,1)S(1)} collective-permute-done((bf16[2,3136]{1,0:T(2,128)(2,1)S(1)}, bf16[2,3136]{1,0:T(2,128)(2,1)S(1)}, u32[]{:S(2)}, u32[]{:S(2)}) %collective-permute-start.5) | collective-permute-done | bytes 12576 | tf_op jit(solution)/shard_map/ppermute | solution.py:357
  20.0 0.0 collective-permute-done.4
  20.0 0.0 copy-done
  20.0 0.7 %multiply_add_fusion = f32[2,3136]{1,0:T(2,128)} fusion(bf16[2,3136]{1,0:T(2,128)(2,1)S(1)} %collective-permute-done.6, bf16[2,3136]{1,0:T(2,128)(2,1)S(1)} %collective-permute-done.5, bf16[2,3136]{1,0:T(2,128)(2,1)S(1)} %collective-permute-done.4, bf16[2,3136]{1,0:T(2,128)(2,1)S(1)} %finish.1, f32[2,3136]{1,0:T(2,128)S(1)} %copy-done), kind=kLoop, calls=%fused_computation | loop fusion | flops 81536 | bytes 100352 | tf_op jit(solution)/shard_map/add | solution.py:439
Async XLA Ops:
  1.7 7.9 %collective-permute-start = (bf16[48,1024]{1,0:T(8,128)(2,1)S(1)}, bf16[48,1024]{1,0:T(8,128)(2,1)S(1)}, u32[]{:S(2)}, u32[]{:S(2)}) collective-permute-start(bf16[48,1024]{1,0:T(8,128)(2,1)S(1)} %get-tuple-element.24), channel_id=1, source_target_pairs={{0,4},{4,8},{8,12},{12,16},{16,20},{20,24},{24,28},{28,0},{1,5},{5... | collective-permute-start | bytes 294920 | tf_op jit(solution)/shard_map/ppermute | solution.py:397
  3.0 6.7 %collective-permute-start.1 = (bf16[48,1024]{1,0:T(8,128)(2,1)S(1)}, bf16[48,1024]{1,0:T(8,128)(2,1)S(1)}, u32[]{:S(2)}, u32[]{:S(2)}) collective-permute-start(bf16[48,1024]{1,0:T(8,128)(2,1)S(1)} %get-tuple-element.25), channel_id=1, source_target_pairs={{0,8},{4,12},{8,16},{12,20},{16,24},{20,28},{24,0},{28,4},{1,9},{5... | collective-permute-start | bytes 294920 | tf_op jit(solution)/shard_map/ppermute | solution.py:397
  4.3 8.2 %collective-permute-start.2 = (bf16[48,1024]{1,0:T(8,128)(2,1)S(1)}, bf16[48,1024]{1,0:T(8,128)(2,1)S(1)}, u32[]{:S(2)}, u32[]{:S(2)}) collective-permute-start(bf16[48,1024]{1,0:T(8,128)(2,1)S(1)} %get-tuple-element.26), channel_id=1, source_target_pairs={{0,24},{4,28},{8,0},{12,4},{16,8},{20,12},{24,16},{28,20},{1,25},{... | collective-permute-start | bytes 294920 | tf_op jit(solution)/shard_map/ppermute | solution.py:397
  6.3 6.3 %collective-permute-start.3 = (bf16[48,1024]{1,0:T(8,128)(2,1)S(1)}, bf16[48,1024]{1,0:T(8,128)(2,1)S(1)}, u32[]{:S(2)}, u32[]{:S(2)}) collective-permute-start(bf16[48,1024]{1,0:T(8,128)(2,1)S(1)} %get-tuple-element.27), channel_id=1, source_target_pairs={{0,28},{4,0},{8,4},{12,8},{16,12},{20,16},{24,20},{28,24},{1,29},{... | collective-permute-start | bytes 294920 | tf_op jit(solution)/shard_map/ppermute | solution.py:397
  9.6 10.4 %copy-start = (f32[2,3136]{1,0:T(2,128)S(1)}, f32[2,3136]{1,0:T(2,128)}, u32[]{:S(2)}) copy-start(f32[2,3136]{1,0:T(2,128)} %param.17) | copy-start | bytes 75268
  15.0 3.9 %collective-permute-start.6 = (bf16[2,3136]{1,0:T(2,128)(2,1)S(1)}, bf16[2,3136]{1,0:T(2,128)(2,1)S(1)}, u32[]{:S(2)}, u32[]{:S(2)}) collective-permute-start(bf16[2,3136]{1,0:T(2,128)(2,1)S(1)} %finish.1), channel_id=1, source_target_pairs={{0,3},{1,2},{2,1},{3,0},{4,7},{5,6},{6,5},{7,4},{8,11},{9,10},{10,... | collective-permute-start | bytes 37640 | tf_op jit(solution)/shard_map/ppermute | solution.py:357
  17.3 2.7 %collective-permute-start.5 = (bf16[2,3136]{1,0:T(2,128)(2,1)S(1)}, bf16[2,3136]{1,0:T(2,128)(2,1)S(1)}, u32[]{:S(2)}, u32[]{:S(2)}) collective-permute-start(bf16[2,3136]{1,0:T(2,128)(2,1)S(1)} %finish.1), channel_id=1, source_target_pairs={{0,2},{1,3},{2,0},{3,1},{4,6},{5,7},{6,4},{7,5},{8,10},{9,11},{10,... | collective-permute-start | bytes 37640 | tf_op jit(solution)/shard_map/ppermute | solution.py:357
  17.5 2.5 %collective-permute-start.4 = (bf16[2,3136]{1,0:T(2,128)(2,1)S(1)}, bf16[2,3136]{1,0:T(2,128)(2,1)S(1)}, u32[]{:S(2)}, u32[]{:S(2)}) collective-permute-start(bf16[2,3136]{1,0:T(2,128)(2,1)S(1)} %finish.1), channel_id=1, source_target_pairs={{0,1},{1,0},{2,3},{3,2},{4,5},{5,4},{6,7},{7,6},{8,9},{9,8},{10,11... | collective-permute-start | bytes 37640 | tf_op jit(solution)/shard_map/ppermute | solution.py:357

commit v5 on v4

--- a/solution.py
+++ b/solution.py
@@ -14,7 +14,8 @@
 LANES = 128
 SUBS = 8
 SHIFTS = (1, 2, -2, -1)
-HEAD = 6
+HEAD = 24
+FLOPS = 5000000000
 F32 = jnp.float32
 BF16 = jnp.bfloat16
 
@@ -85,18 +86,13 @@
 
 
 def pack_kernel(axis, inputs, *refs):
-    sources, radial_hbm, refs = refs[:inputs], refs[inputs], refs[inputs + 1 :]
-    kept, radial_ref, refs = refs[:inputs], refs[inputs], refs[inputs + 1 :]
+    sources, refs = refs[:inputs], refs[inputs:]
+    kept, refs = refs[:inputs], refs[inputs:]
     pack_refs, (pad_ref, sems) = refs[:-2], refs[-2:]
     copies = [
         pltpu.make_async_copy(source, ref, sems.at[k])
         for k, (source, ref) in enumerate(zip(sources, kept))
     ]
-    copies.append(
-        pltpu.make_async_copy(
-            radial_hbm.at[0 : radial_ref.shape[0]], radial_ref, sems.at[inputs]
-        )
-    )
     for copy in copies:
         copy.start()
     nbr_ref, table_ref, site_ref = kept[:3]
@@ -116,12 +112,12 @@
         matmul(hot, ones_where(local[:, s] == rows), ((1,), (1,))).astype(BF16)
         for hot, s in zip(hots, spans)
     ]
-    for copy in copies[2:-1]:
-        copy.wait()
+    copies[2].wait()
     packed = matmul(jnp.concatenate(chosen, axis=0), site_ref[...]).astype(BF16)
     for k, pack_ref in enumerate(pack_refs):
         pack_ref[...] = packed[k * CAP : (k + 1) * CAP]
-    copies[-1].wait()
+    for copy in copies[3:]:
+        copy.wait()
 
 
 def fold_matrix():
@@ -158,14 +154,10 @@
 
 def prepare_kernel(
     axis, begin,
-    nbr_ref, table_ref, site_ref, couple_ref, angular_ref, phase_ref, head_ref, radial_hbm,
-    slot_ref, own_ref, chain_ref, spread_ref, start_ref, centre_ref, turned_ref, radial_ref,
-    pad_ref, scaled_ref, grid_ref, sem,
+    nbr_ref, table_ref, site_ref, couple_ref, angular_ref, phase_ref, radial_ref,
+    slot_ref, own_ref, chain_ref, spread_ref, start_ref, centre_ref, turned_ref,
+    pad_ref, scaled_ref, grid_ref,
 ):
-    fetch = pltpu.make_async_copy(
-        radial_hbm.at[begin : begin + radial_ref.shape[0]], radial_ref, sem
-    )
-    fetch.start()
     count, zones, places = nbr_ref.shape
     owned = site_ref.shape[0]
     terms = angular_ref.shape[0]
@@ -278,8 +270,7 @@
         for k in range(2 * zones):
             at = k * 4 * groups + block * groups
             spread_ref[at : at + groups, :] = moved[k * groups : (k + 1) * groups]
-    turned_ref[...] = head_ref[...].T
-    fetch.wait()
+    turned_ref[...] = radial_ref[:begin, :].T
 
 
 def finish_kernel(count, *refs):
@@ -333,8 +324,9 @@
     central = flat_ref[...].astype(BF16)
     scale = contour_ref[0]
     at = 0
-    for ref, side in zip(radial_refs, (0, 1)):
-        part = scale * matmul(central, ref[...], ((1,), (side,)))
+    turned_ref, radial_ref = radial_refs
+    for matrix, side in ((turned_ref[...], 0), (radial_ref[turned_ref.shape[1] :, :], 1)):
+        part = scale * matmul(central, matrix, ((1,), (side,)))
         out_ref[:, at : at + part.shape[1]] = part[:zones].astype(BF16)
         at += part.shape[1]
 
@@ -376,23 +368,23 @@
     sources = [neighbours, table, site, coupling, angular, phases]
     hbm = pl.BlockSpec(memory_space=pltpu.HBM)
     params = pltpu.CompilerParams(vmem_limit_bytes=LIMIT)
-    turned = pltpu.with_memory_space_constraint(radial[0].T, pltpu.HBM)
+    turned = radial[0].T
     parts = [HEAD * LANES, radial.shape[2] - HEAD * LANES]
     results = pl.pallas_call(
         functools.partial(pack_kernel, "dom", len(sources)),
         out_shape=[pltpu.VMEM(x.shape, x.dtype) for x in sources]
-        + [pltpu.VMEM((parts[0], width), BF16)]
         + [pltpu.VMEM((CAP, width), BF16)] * len(SHIFTS),
-        in_specs=[hbm] * (len(sources) + 1),
-        out_specs=[vmem()] * (len(sources) + 1 + len(SHIFTS)),
+        in_specs=[hbm] * len(sources),
+        out_specs=[vmem()] * (len(sources) + len(SHIFTS)),
         scratch_shapes=[
             pltpu.VMEM((len(SHIFTS) * zones, LANES), jnp.int32),
-            pltpu.SemaphoreType.DMA((len(sources) + 1,)),
+            pltpu.SemaphoreType.DMA((len(sources),)),
         ],
         compiler_params=params,
+        cost_estimate=pl.CostEstimate(flops=FLOPS, bytes_accessed=0, transcendentals=0),
         name="pack",
-    )(*[pltpu.with_memory_space_constraint(x, pltpu.HBM) for x in sources], turned)
-    kept, head, packs = results[: len(sources)], results[len(sources)], results[len(sources) + 1 :]
+    )(*[pltpu.with_memory_space_constraint(x, pltpu.HBM) for x in sources])
+    kept, packs = results[: len(sources)], results[len(sources) :]
     pieces = [
         lax.ppermute(pack, "dom", [(i, (i + shift) % count) for i in range(count)])
         for pack, shift in zip(packs, SHIFTS)
@@ -409,19 +401,17 @@
             pltpu.VMEM((zones * groups * SUBS, LANES), F32),
             pltpu.VMEM((zones * groups, LANES), F32),
             pltpu.VMEM((width, parts[0]), BF16),
-            pltpu.VMEM((parts[1], width), BF16),
         ],
-        in_specs=[vmem()] * 7 + [hbm],
-        out_specs=[vmem()] * 8,
+        in_specs=[vmem()] * 7,
+        out_specs=[vmem()] * 7,
         scratch_shapes=[
             pltpu.VMEM((zones, LANES), jnp.int32),
             pltpu.VMEM((2 * zones * SUBS, LANES), F32),
             pltpu.VMEM((groups, (terms + zones) * LANES), F32),
-            pltpu.SemaphoreType.DMA,
         ],
         compiler_params=params,
         name="prepare",
-    )(*kept, head, turned)
+    )(*kept, turned)
     pieces = [pltpu.with_memory_space_constraint(piece, pltpu.VMEM) for piece in pieces]
     entries = radial.shape[2]
     part = pl.pallas_call(
@@ -434,7 +424,7 @@
         ],
         compiler_params=params,
         name="finish",
-    )(*pieces, *prepared, contour)
+    )(*pieces, *prepared, turned, contour)
     density = sum_over(part, "en")
     return 0.5 * old_potential + 0.5 * density * lax.rsqrt(1.0 + density * density)
 

time: 20.9 us -> 20.3 us (0.971)
  Pallas kernels: 6.59 us -> 5.88 us
    pallas_call x1, Pallas kernels: 2.47 us -> 1.82 us  [shards(): pl.pallas_call(functools.partial(finish_kernel, len(pieces)), out_shape=p...]
  transfers between devices with their start and end apart: 7 -> 7, of which waited for: 4 -> 4; matrix products, arithmetic and copies ran while one was open for 0% -> 0% of each run, Pallas kernels for 12% -> 11%
where the time goes in v5:
time: 20.3 us; the launch traced here: 20.1 us
  starting transfers between devices  7.57 us (37%)
  Pallas kernels  5.88 us (29%)
  waiting for transfers between devices  5.34 us (26%)
  between operations  0.69 us (3%)
  other arithmetic  0.67 us (3%)
    ppermute x4, starting transfers between devices, shards(): lax.ppermute(pack, 'dom', [(i, (i + shift) % count) for i in range(count)])  4.84 us
    ppermute x4, waiting for transfers between devices, shards(): lax.ppermute(pack, 'dom', [(i, (i + shift) % count) for i in range(count)])  3.09 us
    ppermute x3, starting transfers between devices, sum_over(): lax.ppermute(value, axis, [(i, i ^ stride * k) for i in range(size)])  2.72 us
    ppermute x3, waiting for transfers between devices, sum_over(): lax.ppermute(value, axis, [(i, i ^ stride * k) for i in range(size)])  2.25 us
    pallas_call x1, Pallas kernels, shards(): pl.pallas_call(functools.partial(prepare_kernel, 'dom', parts[0]), out_sh...  2.24 us
    pallas_call x1, Pallas kernels, shards(): pl.pallas_call(functools.partial(finish_kernel, len(pieces)), out_shape=p...  1.82 us
    pallas_call x1, Pallas kernels, shards(): pl.pallas_call(functools.partial(pack_kernel, 'dom', len(sources)), out_s...  1.82 us
    add x1, other arithmetic, shards(): 0.5 * old_potential + 0.5 * density * lax.rsqrt(1.0 + density * density)  0.67 us
  transfers between devices with their start and end apart: 7, of which 4 were waited for; matrix products, arithmetic and copies ran while one was open for 0% of the time, Pallas kernels for 11%

profile of v5, /device:TPU:3, one launch (start us, length us, event | category | flops | bytes accessed | tf_op | source)
XLA Modules:
  0.0 20.1 jit_solution(1502533236691986808)
XLA Ops:
  0.0 0.0 copy-start
  0.0 1.8 %pack.1 = (s32[8,2,65]{2,1,0:T(2,128)S(1)}, s32[16,128]{1,0:T(8,128)S(1)}, bf16[256,1024]{1,0:T(8,128)(2,1)S(1)}, bf16[2,4,4225]{2,1,0:T(4,128)(2,1)S(1)}, bf16[...) custom-call(s32[8,2,65]{2,1,0:T(2,128)} %refs_0_.1, ...), custom_call_target="tpu_custom_call" | custom-call | flops 5000000000 | tf_op jit(solution)/shard_map/pack/pallas_call | solution.py:373
  1.8 1.3 %collective-permute-start = (bf16[48,1024]{1,0:T(8,128)(2,1)S(1)}, bf16[48,1024]{1,0:T(8,128)(2,1)S(1)}, u32[]{:S(2)}, u32[]{:S(2)}) collective-permute-start(bf16[48,1024]{1,0:T(8,128)(2,1)S(1)} %get-tuple-element.22), channel_id=1, source_target_pairs={{0,4},{4,8},{8,12},{12,16},{16,20},{20,24},{24,28},{28,0},{1,5},{5... | collective-permute-start | bytes 294920 | tf_op jit(solution)/shard_map/ppermute | solution.py:389
  3.1 1.3 %collective-permute-start.1 = (bf16[48,1024]{1,0:T(8,128)(2,1)S(1)}, bf16[48,1024]{1,0:T(8,128)(2,1)S(1)}, u32[]{:S(2)}, u32[]{:S(2)}) collective-permute-start(bf16[48,1024]{1,0:T(8,128)(2,1)S(1)} %get-tuple-element.23), channel_id=1, source_target_pairs={{0,8},{4,12},{8,16},{12,20},{16,24},{20,28},{24,0},{28,4},{1,9},{5... | collective-permute-start | bytes 294920 | tf_op jit(solution)/shard_map/ppermute | solution.py:389
  4.4 2.0 %collective-permute-start.2 = (bf16[48,1024]{1,0:T(8,128)(2,1)S(1)}, bf16[48,1024]{1,0:T(8,128)(2,1)S(1)}, u32[]{:S(2)}, u32[]{:S(2)}) collective-permute-start(bf16[48,1024]{1,0:T(8,128)(2,1)S(1)} %get-tuple-element.24), channel_id=1, source_target_pairs={{0,24},{4,28},{8,0},{12,4},{16,8},{20,12},{24,16},{28,20},{1,25},{... | collective-permute-start | bytes 294920 | tf_op jit(solution)/shard_map/ppermute | solution.py:389
  6.4 0.3 %collective-permute-start.3 = (bf16[48,1024]{1,0:T(8,128)(2,1)S(1)}, bf16[48,1024]{1,0:T(8,128)(2,1)S(1)}, u32[]{:S(2)}, u32[]{:S(2)}) collective-permute-start(bf16[48,1024]{1,0:T(8,128)(2,1)S(1)} %get-tuple-element.25), channel_id=1, source_target_pairs={{0,28},{4,0},{8,4},{12,8},{16,12},{20,16},{24,20},{28,24},{1,29},{... | collective-permute-start | bytes 294920 | tf_op jit(solution)/shard_map/ppermute | solution.py:389
  7.3 0.0 copy-done
  7.3 2.2 %prepare.1 = (bf16[128,192]{1,0:T(8,128)(2,1)S(1)}, f32[64,1024]{1,0:T(8,128)S(1)}, bf16[1024,128]{1,0:T(8,128)(2,1)S(1)}, f32[128,256]{1,0:T(8,128)S(1)}, f32[1...) custom-call(s32[8,2,65]{2,1,0:T(2,128)S(1)} %get-tuple-element.26.nbr_ref, ...), custom_call_target="tpu_custom_call" | custom-call | tf_op jit(solution)/shard_map/prepare/pallas_call | solution.py:394
  9.6 0.0 collective-permute-done.refs_0_
  9.6 0.2 %collective-permute-done.1.refs_1_ = bf16[48,1024]{1,0:T(8,128)(2,1)S(1)} collective-permute-done((bf16[48,1024]{1,0:T(8,128)(2,1)S(1)}, bf16[48,1024]{1,0:T(8,128)(2,1)S(1)}, u32[]{:S(2)}, u32[]{:S(2)}) %collective-permute-start.1) | collective-permute-done | bytes 98336 | tf_op jit(solution)/shard_map/ppermute | solution.py:389
  9.8 2.8 %collective-permute-done.2.refs_2_ = bf16[48,1024]{1,0:T(8,128)(2,1)S(1)} collective-permute-done((bf16[48,1024]{1,0:T(8,128)(2,1)S(1)}, bf16[48,1024]{1,0:T(8,128)(2,1)S(1)}, u32[]{:S(2)}, u32[]{:S(2)}) %collective-permute-start.2) | collective-permute-done | bytes 98336 | tf_op jit(solution)/shard_map/ppermute | solution.py:389
  12.7 0.0 collective-permute-done.3.refs_3_
  12.7 0.0 copy-start.1
  12.7 1.8 %finish.1 = bf16[2,3136]{1,0:T(2,128)(2,1)S(1)} custom-call(bf16[48,1024]{1,0:T(8,128)(2,1)S(1)} %collective-permute-done.refs_0_, bf16[48,1024]{1,0:T(8,128)(2,1)S(1)} %collective-permute-done.1.refs_1_, bf16[48,1024]{1,0:T(8,128)(2,1)S(1)} %collective-permute-done.2.refs_2_, bf16[48,1024]{1,0:T(8,128)(2,1)S(1)} %collective-permute-done.3.refs_3_, ...), custom_call_target="tpu_custom_call" | custom-call | tf_op jit(solution)/shard_map/finish/pallas_call | solution.py:417
  14.5 2.3 %collective-permute-start.6 = (bf16[2,3136]{1,0:T(2,128)(2,1)S(1)}, bf16[2,3136]{1,0:T(2,128)(2,1)S(1)}, u32[]{:S(2)}, u32[]{:S(2)}) collective-permute-start(bf16[2,3136]{1,0:T(2,128)(2,1)S(1)} %finish.1), channel_id=1, source_target_pairs={{0,3},{1,2},{2,1},{3,0},{4,7},{5,6},{6,5},{7,4},{8,11},{9,10},{10,... | collective-permute-start | bytes 37640 | tf_op jit(solution)/shard_map/ppermute | solution.py:349
  16.8 0.2 %collective-permute-start.5 = (bf16[2,3136]{1,0:T(2,128)(2,1)S(1)}, bf16[2,3136]{1,0:T(2,128)(2,1)S(1)}, u32[]{:S(2)}, u32[]{:S(2)}) collective-permute-start(bf16[2,3136]{1,0:T(2,128)(2,1)S(1)} %finish.1), channel_id=1, source_target_pairs={{0,2},{1,3},{2,0},{3,1},{4,6},{5,7},{6,4},{7,5},{8,10},{9,11},{10,... | collective-permute-start | bytes 37640 | tf_op jit(solution)/shard_map/ppermute | solution.py:349
  17.0 0.2 %collective-permute-start.4 = (bf16[2,3136]{1,0:T(2,128)(2,1)S(1)}, bf16[2,3136]{1,0:T(2,128)(2,1)S(1)}, u32[]{:S(2)}, u32[]{:S(2)}) collective-permute-start(bf16[2,3136]{1,0:T(2,128)(2,1)S(1)} %finish.1), channel_id=1, source_target_pairs={{0,1},{1,0},{2,3},{3,2},{4,5},{5,4},{6,7},{7,6},{8,9},{9,8},{10,11... | collective-permute-start | bytes 37640 | tf_op jit(solution)/shard_map/ppermute | solution.py:349
  17.2 1.2 %collective-permute-done.6 = bf16[2,3136]{1,0:T(2,128)(2,1)S(1)} collective-permute-done((bf16[2,3136]{1,0:T(2,128)(2,1)S(1)}, bf16[2,3136]{1,0:T(2,128)(2,1)S(1)}, u32[]{:S(2)}, u32[]{:S(2)}) %collective-permute-start.6) | collective-permute-done | bytes 12576 | tf_op jit(solution)/shard_map/ppermute | solution.py:349
  18.4 1.0 %collective-permute-done.5 = bf16[2,3136]{1,0:T(2,128)(2,1)S(1)} collective-permute-done((bf16[2,3136]{1,0:T(2,128)(2,1)S(1)}, bf16[2,3136]{1,0:T(2,128)(2,1)S(1)}, u32[]{:S(2)}, u32[]{:S(2)}) %collective-permute-start.5) | collective-permute-done | bytes 12576 | tf_op jit(solution)/shard_map/ppermute | solution.py:349
  19.5 0.0 collective-permute-done.4
  19.5 0.0 copy-done.1
  19.5 0.7 %multiply_add_fusion = f32[2,3136]{1,0:T(2,128)} fusion(bf16[2,3136]{1,0:T(2,128)(2,1)S(1)} %collective-permute-done.6, bf16[2,3136]{1,0:T(2,128)(2,1)S(1)} %collective-permute-done.5, bf16[2,3136]{1,0:T(2,128)(2,1)S(1)} %collective-permute-done.4, bf16[2,3136]{1,0:T(2,128)(2,1)S(1)} %finish.1, f32[2,3136]{1,0:T(2,128)S(1)} %copy-done.1), kind=kLoop, calls=%fused_computation | loop fusion | flops 81536 | bytes 100352 | tf_op jit(solution)/shard_map/add | solution.py:429
Async XLA Ops:
  0.0 7.3 %copy-start = (bf16[1,1024,3136]{1,2,0:T(8,128)(2,1)S(1)}, bf16[1,1024,3136]{1,2,0:T(8,128)(2,1)}, u32[]{:S(2)}) copy-start(bf16[1,1024,3136]{1,2,0:T(8,128)(2,1)} %param.14) | copy-start | bytes 19267588
  1.8 7.8 %collective-permute-start = (bf16[48,1024]{1,0:T(8,128)(2,1)S(1)}, bf16[48,1024]{1,0:T(8,128)(2,1)S(1)}, u32[]{:S(2)}, u32[]{:S(2)}) collective-permute-start(bf16[48,1024]{1,0:T(8,128)(2,1)S(1)} %get-tuple-element.22), channel_id=1, source_target_pairs={{0,4},{4,8},{8,12},{12,16},{16,20},{20,24},{24,28},{28,0},{1,5},{5... | collective-permute-start | bytes 294920 | tf_op jit(solution)/shard_map/ppermute | solution.py:389
  3.1 6.7 %collective-permute-start.1 = (bf16[48,1024]{1,0:T(8,128)(2,1)S(1)}, bf16[48,1024]{1,0:T(8,128)(2,1)S(1)}, u32[]{:S(2)}, u32[]{:S(2)}) collective-permute-start(bf16[48,1024]{1,0:T(8,128)(2,1)S(1)} %get-tuple-element.23), channel_id=1, source_target_pairs={{0,8},{4,12},{8,16},{12,20},{16,24},{20,28},{24,0},{28,4},{1,9},{5... | collective-permute-start | bytes 294920 | tf_op jit(solution)/shard_map/ppermute | solution.py:389
  4.4 8.2 %collective-permute-start.2 = (bf16[48,1024]{1,0:T(8,128)(2,1)S(1)}, bf16[48,1024]{1,0:T(8,128)(2,1)S(1)}, u32[]{:S(2)}, u32[]{:S(2)}) collective-permute-start(bf16[48,1024]{1,0:T(8,128)(2,1)S(1)} %get-tuple-element.24), channel_id=1, source_target_pairs={{0,24},{4,28},{8,0},{12,4},{16,8},{20,12},{24,16},{28,20},{1,25},{... | collective-permute-start | bytes 294920 | tf_op jit(solution)/shard_map/ppermute | solution.py:389
  6.4 6.3 %collective-permute-start.3 = (bf16[48,1024]{1,0:T(8,128)(2,1)S(1)}, bf16[48,1024]{1,0:T(8,128)(2,1)S(1)}, u32[]{:S(2)}, u32[]{:S(2)}) collective-permute-start(bf16[48,1024]{1,0:T(8,128)(2,1)S(1)} %get-tuple-element.25), channel_id=1, source_target_pairs={{0,28},{4,0},{8,4},{12,8},{16,12},{20,16},{24,20},{28,24},{1,29},{... | collective-permute-start | bytes 294920 | tf_op jit(solution)/shard_map/ppermute | solution.py:389
  12.7 6.8 %copy-start.1 = (f32[2,3136]{1,0:T(2,128)S(1)}, f32[2,3136]{1,0:T(2,128)}, u32[]{:S(2)}) copy-start(f32[2,3136]{1,0:T(2,128)} %param.17) | copy-start | bytes 75268
  14.5 3.9 %collective-permute-start.6 = (bf16[2,3136]{1,0:T(2,128)(2,1)S(1)}, bf16[2,3136]{1,0:T(2,128)(2,1)S(1)}, u32[]{:S(2)}, u32[]{:S(2)}) collective-permute-start(bf16[2,3136]{1,0:T(2,128)(2,1)S(1)} %finish.1), channel_id=1, source_target_pairs={{0,3},{1,2},{2,1},{3,0},{4,7},{5,6},{6,5},{7,4},{8,11},{9,10},{10,... | collective-permute-start | bytes 37640 | tf_op jit(solution)/shard_map/ppermute | solution.py:349
  16.8 2.7 %collective-permute-start.5 = (bf16[2,3136]{1,0:T(2,128)(2,1)S(1)}, bf16[2,3136]{1,0:T(2,128)(2,1)S(1)}, u32[]{:S(2)}, u32[]{:S(2)}) collective-permute-start(bf16[2,3136]{1,0:T(2,128)(2,1)S(1)} %finish.1), channel_id=1, source_target_pairs={{0,2},{1,3},{2,0},{3,1},{4,6},{5,7},{6,4},{7,5},{8,10},{9,11},{10,... | collective-permute-start | bytes 37640 | tf_op jit(solution)/shard_map/ppermute | solution.py:349
  17.0 2.5 %collective-permute-start.4 = (bf16[2,3136]{1,0:T(2,128)(2,1)S(1)}, bf16[2,3136]{1,0:T(2,128)(2,1)S(1)}, u32[]{:S(2)}, u32[]{:S(2)}) collective-permute-start(bf16[2,3136]{1,0:T(2,128)(2,1)S(1)} %finish.1), channel_id=1, source_target_pairs={{0,1},{1,0},{2,3},{3,2},{4,5},{5,4},{6,7},{7,6},{8,9},{9,8},{10,11... | collective-permute-start | bytes 37640 | tf_op jit(solution)/shard_map/ppermute | solution.py:349

commit v6 on v5

--- a/solution.py
+++ b/solution.py
@@ -14,7 +14,6 @@
 LANES = 128
 SUBS = 8
 SHIFTS = (1, 2, -2, -1)
-HEAD = 24
 FLOPS = 5000000000
 F32 = jnp.float32
 BF16 = jnp.bfloat16
@@ -153,7 +152,7 @@
 
 
 def prepare_kernel(
-    axis, begin,
+    axis,
     nbr_ref, table_ref, site_ref, couple_ref, angular_ref, phase_ref, radial_ref,
     slot_ref, own_ref, chain_ref, spread_ref, start_ref, centre_ref, turned_ref,
     pad_ref, scaled_ref, grid_ref,
@@ -270,13 +269,13 @@
         for k in range(2 * zones):
             at = k * 4 * groups + block * groups
             spread_ref[at : at + groups, :] = moved[k * groups : (k + 1) * groups]
-    turned_ref[...] = radial_ref[:begin, :].T
+    turned_ref[...] = radial_ref[...].T
 
 
 def finish_kernel(count, *refs):
     pieces, refs = refs[:count], refs[count:]
     slot_ref, own_ref, chain_ref, spread_ref, start_ref, centre_ref, refs = *refs[:6], refs[6:]
-    radial_refs, (contour_ref, out_ref, flat_ref) = refs[:-3], refs[-3:]
+    turned_ref, contour_ref, out_ref, flat_ref = refs
     zones = out_ref.shape[0]
     near = jnp.concatenate([ref[...] for ref in pieces], axis=0)
     far = matmul(slot_ref[...], near)
@@ -323,12 +322,7 @@
             flat_ref[z : z + 1, g * LANES : (g + 1) * LANES] = central[g : g + 1]
     central = flat_ref[...].astype(BF16)
     scale = contour_ref[0]
-    at = 0
-    turned_ref, radial_ref = radial_refs
-    for matrix, side in ((turned_ref[...], 0), (radial_ref[turned_ref.shape[1] :, :], 1)):
-        part = scale * matmul(central, matrix, ((1,), (side,)))
-        out_ref[:, at : at + part.shape[1]] = part[:zones].astype(BF16)
-        at += part.shape[1]
+    out_ref[...] = (scale * matmul(central, turned_ref[...])[:zones]).astype(BF16)
 
 
 def vmem():
@@ -369,7 +363,6 @@
     hbm = pl.BlockSpec(memory_space=pltpu.HBM)
     params = pltpu.CompilerParams(vmem_limit_bytes=LIMIT)
     turned = radial[0].T
-    parts = [HEAD * LANES, radial.shape[2] - HEAD * LANES]
     results = pl.pallas_call(
         functools.partial(pack_kernel, "dom", len(sources)),
         out_shape=[pltpu.VMEM(x.shape, x.dtype) for x in sources]
@@ -392,7 +385,7 @@
     size = zones * terms * SUBS
     groups = width // LANES
     prepared = pl.pallas_call(
-        functools.partial(prepare_kernel, "dom", parts[0]),
+        functools.partial(prepare_kernel, "dom"),
         out_shape=[
             pltpu.VMEM((2 * size, CAP * len(SHIFTS)), BF16),
             pltpu.VMEM((size, width), F32),
@@ -400,7 +393,7 @@
             pltpu.VMEM((2 * zones * 4 * groups, 2 * LANES), F32),
             pltpu.VMEM((zones * groups * SUBS, LANES), F32),
             pltpu.VMEM((zones * groups, LANES), F32),
-            pltpu.VMEM((width, parts[0]), BF16),
+            pltpu.VMEM((width, radial.shape[2]), BF16),
         ],
         in_specs=[vmem()] * 7,
         out_specs=[vmem()] * 7,
@@ -417,14 +410,14 @@
     part = pl.pallas_call(
         functools.partial(finish_kernel, len(pieces)),
         out_shape=pltpu.VMEM((zones, entries), BF16),
-        in_specs=[vmem()] * (len(pieces) + 8) + [pl.BlockSpec(memory_space=pltpu.SMEM)],
+        in_specs=[vmem()] * (len(pieces) + 7) + [pl.BlockSpec(memory_space=pltpu.SMEM)],
         out_specs=vmem(),
         scratch_shapes=[
             pltpu.VMEM((SUBS, width), F32),
         ],
         compiler_params=params,
         name="finish",
-    )(*pieces, *prepared, turned, contour)
+    )(*pieces, *prepared, contour)
     density = sum_over(part, "en")
     return 0.5 * old_potential + 0.5 * density * lax.rsqrt(1.0 + density * density)
 

time: 20.3 us -> 20.3 us (level)
  no operation moved by 1% of the time
where the time goes in v6:
time: 20.3 us; the launch traced here: 20.1 us
  starting transfers between devices  7.61 us (37%)
  Pallas kernels  5.89 us (29%)
  waiting for transfers between devices  5.28 us (26%)
  between operations  0.7 us (3%)
  other arithmetic  0.67 us (3%)
    ppermute x4, starting transfers between devices, shards(): lax.ppermute(pack, 'dom', [(i, (i + shift) % count) for i in range(count)])  4.84 us
    ppermute x4, waiting for transfers between devices, shards(): lax.ppermute(pack, 'dom', [(i, (i + shift) % count) for i in range(count)])  3.04 us
    ppermute x3, starting transfers between devices, sum_over(): lax.ppermute(value, axis, [(i, i ^ stride * k) for i in range(size)])  2.76 us
    pallas_call x1, Pallas kernels, shards(): pl.pallas_call(functools.partial(prepare_kernel, 'dom'), out_shape=[pltpu...  2.27 us
    ppermute x3, waiting for transfers between devices, sum_over(): lax.ppermute(value, axis, [(i, i ^ stride * k) for i in range(size)])  2.23 us
    pallas_call x1, Pallas kernels, shards(): pl.pallas_call(functools.partial(pack_kernel, 'dom', len(sources)), out_s...  1.82 us
    pallas_call x1, Pallas kernels, shards(): pl.pallas_call(functools.partial(finish_kernel, len(pieces)), out_shape=p...  1.8 us
    add x1, other arithmetic, shards(): 0.5 * old_potential + 0.5 * density * lax.rsqrt(1.0 + density * density)  0.67 us
  transfers between devices with their start and end apart: 7, of which 4 were waited for; matrix products, arithmetic and copies ran while one was open for 0% of the time, Pallas kernels for 11%

profile of v6, /device:TPU:3, one launch (start us, length us, event | category | flops | bytes accessed | tf_op | source)
XLA Modules:
  0.0 20.1 jit_solution(722476055063288390)
XLA Ops:
  0.0 0.0 copy-start
  0.0 1.8 %pack.1 = (s32[8,2,65]{2,1,0:T(2,128)S(1)}, s32[16,128]{1,0:T(8,128)S(1)}, bf16[256,1024]{1,0:T(8,128)(2,1)S(1)}, bf16[2,4,4225]{2,1,0:T(4,128)(2,1)S(1)}, bf16[...) custom-call(s32[8,2,65]{2,1,0:T(2,128)} %refs_0_.1, ...), custom_call_target="tpu_custom_call" | custom-call | flops 5000000000 | tf_op jit(solution)/shard_map/pack/pallas_call | solution.py:366
  1.8 1.3 %collective-permute-start = (bf16[48,1024]{1,0:T(8,128)(2,1)S(1)}, bf16[48,1024]{1,0:T(8,128)(2,1)S(1)}, u32[]{:S(2)}, u32[]{:S(2)}) collective-permute-start(bf16[48,1024]{1,0:T(8,128)(2,1)S(1)} %get-tuple-element.22), channel_id=1, source_target_pairs={{0,4},{4,8},{8,12},{12,16},{16,20},{20,24},{24,28},{28,0},{1,5},{5... | collective-permute-start | bytes 294920 | tf_op jit(solution)/shard_map/ppermute | solution.py:382
  3.1 1.3 %collective-permute-start.1 = (bf16[48,1024]{1,0:T(8,128)(2,1)S(1)}, bf16[48,1024]{1,0:T(8,128)(2,1)S(1)}, u32[]{:S(2)}, u32[]{:S(2)}) collective-permute-start(bf16[48,1024]{1,0:T(8,128)(2,1)S(1)} %get-tuple-element.23), channel_id=1, source_target_pairs={{0,8},{4,12},{8,16},{12,20},{16,24},{20,28},{24,0},{28,4},{1,9},{5... | collective-permute-start | bytes 294920 | tf_op jit(solution)/shard_map/ppermute | solution.py:382
  4.4 2.0 %collective-permute-start.2 = (bf16[48,1024]{1,0:T(8,128)(2,1)S(1)}, bf16[48,1024]{1,0:T(8,128)(2,1)S(1)}, u32[]{:S(2)}, u32[]{:S(2)}) collective-permute-start(bf16[48,1024]{1,0:T(8,128)(2,1)S(1)} %get-tuple-element.24), channel_id=1, source_target_pairs={{0,24},{4,28},{8,0},{12,4},{16,8},{20,12},{24,16},{28,20},{1,25},{... | collective-permute-start | bytes 294920 | tf_op jit(solution)/shard_map/ppermute | solution.py:382
  6.4 0.3 %collective-permute-start.3 = (bf16[48,1024]{1,0:T(8,128)(2,1)S(1)}, bf16[48,1024]{1,0:T(8,128)(2,1)S(1)}, u32[]{:S(2)}, u32[]{:S(2)}) collective-permute-start(bf16[48,1024]{1,0:T(8,128)(2,1)S(1)} %get-tuple-element.25), channel_id=1, source_target_pairs={{0,28},{4,0},{8,4},{12,8},{16,12},{20,16},{24,20},{28,24},{1,29},{... | collective-permute-start | bytes 294920 | tf_op jit(solution)/shard_map/ppermute | solution.py:382
  7.3 0.0 copy-done
  7.3 0.0 copy-start.1
  7.3 2.3 %prepare.1 = (bf16[128,192]{1,0:T(8,128)(2,1)S(1)}, f32[64,1024]{1,0:T(8,128)S(1)}, bf16[1024,128]{1,0:T(8,128)(2,1)S(1)}, f32[128,256]{1,0:T(8,128)S(1)}, f32[1...) custom-call(s32[8,2,65]{2,1,0:T(2,128)S(1)} %get-tuple-element.26.nbr_ref, ...), custom_call_target="tpu_custom_call" | custom-call | tf_op jit(solution)/shard_map/prepare/pallas_call | solution.py:387
  9.6 0.0 collective-permute-done.refs_0_
  9.6 0.2 collective-permute-done.1.refs_1_
  9.8 2.8 %collective-permute-done.2.refs_2_ = bf16[48,1024]{1,0:T(8,128)(2,1)S(1)} collective-permute-done((bf16[48,1024]{1,0:T(8,128)(2,1)S(1)}, bf16[48,1024]{1,0:T(8,128)(2,1)S(1)}, u32[]{:S(2)}, u32[]{:S(2)}) %collective-permute-start.2) | collective-permute-done | bytes 98336 | tf_op jit(solution)/shard_map/ppermute | solution.py:382
  12.7 0.0 collective-permute-done.3.refs_3_
  12.7 1.8 %finish.1 = bf16[2,3136]{1,0:T(2,128)(2,1)S(1)} custom-call(bf16[48,1024]{1,0:T(8,128)(2,1)S(1)} %collective-permute-done.refs_0_, bf16[48,1024]{1,0:T(8,128)(2,1)S(1)} %collective-permute-done.1.refs_1_, bf16[48,1024]{1,0:T(8,128)(2,1)S(1)} %collective-permute-done.2.refs_2_, bf16[48,1024]{1,0:T(8,128)(2,1)S(1)} %collective-permute-done.3.refs_3_, ...), custom_call_target="tpu_custom_call" | custom-call | tf_op jit(solution)/shard_map/finish/pallas_call | solution.py:410
  14.5 2.3 %collective-permute-start.6 = (bf16[2,3136]{1,0:T(2,128)(2,1)S(1)}, bf16[2,3136]{1,0:T(2,128)(2,1)S(1)}, u32[]{:S(2)}, u32[]{:S(2)}) collective-permute-start(bf16[2,3136]{1,0:T(2,128)(2,1)S(1)} %finish.1), channel_id=1, source_target_pairs={{0,3},{1,2},{2,1},{3,0},{4,7},{5,6},{6,5},{7,4},{8,11},{9,10},{10,... | collective-permute-start | bytes 37640 | tf_op jit(solution)/shard_map/ppermute | solution.py:343
  16.8 0.2 %collective-permute-start.5 = (bf16[2,3136]{1,0:T(2,128)(2,1)S(1)}, bf16[2,3136]{1,0:T(2,128)(2,1)S(1)}, u32[]{:S(2)}, u32[]{:S(2)}) collective-permute-start(bf16[2,3136]{1,0:T(2,128)(2,1)S(1)} %finish.1), channel_id=1, source_target_pairs={{0,2},{1,3},{2,0},{3,1},{4,6},{5,7},{6,4},{7,5},{8,10},{9,11},{10,... | collective-permute-start | bytes 37640 | tf_op jit(solution)/shard_map/ppermute | solution.py:343
  17.0 0.2 %collective-permute-start.4 = (bf16[2,3136]{1,0:T(2,128)(2,1)S(1)}, bf16[2,3136]{1,0:T(2,128)(2,1)S(1)}, u32[]{:S(2)}, u32[]{:S(2)}) collective-permute-start(bf16[2,3136]{1,0:T(2,128)(2,1)S(1)} %finish.1), channel_id=1, source_target_pairs={{0,1},{1,0},{2,3},{3,2},{4,5},{5,4},{6,7},{7,6},{8,9},{9,8},{10,11... | collective-permute-start | bytes 37640 | tf_op jit(solution)/shard_map/ppermute | solution.py:343
  17.2 1.2 %collective-permute-done.6 = bf16[2,3136]{1,0:T(2,128)(2,1)S(1)} collective-permute-done((bf16[2,3136]{1,0:T(2,128)(2,1)S(1)}, bf16[2,3136]{1,0:T(2,128)(2,1)S(1)}, u32[]{:S(2)}, u32[]{:S(2)}) %collective-permute-start.6) | collective-permute-done | bytes 12576 | tf_op jit(solution)/shard_map/ppermute | solution.py:343
  18.4 1.0 %collective-permute-done.5 = bf16[2,3136]{1,0:T(2,128)(2,1)S(1)} collective-permute-done((bf16[2,3136]{1,0:T(2,128)(2,1)S(1)}, bf16[2,3136]{1,0:T(2,128)(2,1)S(1)}, u32[]{:S(2)}, u32[]{:S(2)}) %collective-permute-start.5) | collective-permute-done | bytes 12576 | tf_op jit(solution)/shard_map/ppermute | solution.py:343
  19.5 0.0 collective-permute-done.4
  19.5 0.0 copy-done.1
  19.5 0.7 %multiply_add_fusion = f32[2,3136]{1,0:T(2,128)} fusion(bf16[2,3136]{1,0:T(2,128)(2,1)S(1)} %collective-permute-done.6, bf16[2,3136]{1,0:T(2,128)(2,1)S(1)} %collective-permute-done.5, bf16[2,3136]{1,0:T(2,128)(2,1)S(1)} %collective-permute-done.4, bf16[2,3136]{1,0:T(2,128)(2,1)S(1)} %finish.1, f32[2,3136]{1,0:T(2,128)S(1)} %copy-done.1), kind=kLoop, calls=%fused_computation | loop fusion | flops 81536 | bytes 100352 | tf_op jit(solution)/shard_map/add | solution.py:422
Async XLA Ops:
  0.0 7.3 %copy-start = (bf16[1,1024,3136]{1,2,0:T(8,128)(2,1)S(1)}, bf16[1,1024,3136]{1,2,0:T(8,128)(2,1)}, u32[]{:S(2)}) copy-start(bf16[1,1024,3136]{1,2,0:T(8,128)(2,1)} %param.14) | copy-start | bytes 19267588
  1.8 7.8 %collective-permute-start = (bf16[48,1024]{1,0:T(8,128)(2,1)S(1)}, bf16[48,1024]{1,0:T(8,128)(2,1)S(1)}, u32[]{:S(2)}, u32[]{:S(2)}) collective-permute-start(bf16[48,1024]{1,0:T(8,128)(2,1)S(1)} %get-tuple-element.22), channel_id=1, source_target_pairs={{0,4},{4,8},{8,12},{12,16},{16,20},{20,24},{24,28},{28,0},{1,5},{5... | collective-permute-start | bytes 294920 | tf_op jit(solution)/shard_map/ppermute | solution.py:382
  3.1 6.7 %collective-permute-start.1 = (bf16[48,1024]{1,0:T(8,128)(2,1)S(1)}, bf16[48,1024]{1,0:T(8,128)(2,1)S(1)}, u32[]{:S(2)}, u32[]{:S(2)}) collective-permute-start(bf16[48,1024]{1,0:T(8,128)(2,1)S(1)} %get-tuple-element.23), channel_id=1, source_target_pairs={{0,8},{4,12},{8,16},{12,20},{16,24},{20,28},{24,0},{28,4},{1,9},{5... | collective-permute-start | bytes 294920 | tf_op jit(solution)/shard_map/ppermute | solution.py:382
  4.4 8.2 %collective-permute-start.2 = (bf16[48,1024]{1,0:T(8,128)(2,1)S(1)}, bf16[48,1024]{1,0:T(8,128)(2,1)S(1)}, u32[]{:S(2)}, u32[]{:S(2)}) collective-permute-start(bf16[48,1024]{1,0:T(8,128)(2,1)S(1)} %get-tuple-element.24), channel_id=1, source_target_pairs={{0,24},{4,28},{8,0},{12,4},{16,8},{20,12},{24,16},{28,20},{1,25},{... | collective-permute-start | bytes 294920 | tf_op jit(solution)/shard_map/ppermute | solution.py:382
  6.4 6.3 %collective-permute-start.3 = (bf16[48,1024]{1,0:T(8,128)(2,1)S(1)}, bf16[48,1024]{1,0:T(8,128)(2,1)S(1)}, u32[]{:S(2)}, u32[]{:S(2)}) collective-permute-start(bf16[48,1024]{1,0:T(8,128)(2,1)S(1)} %get-tuple-element.25), channel_id=1, source_target_pairs={{0,28},{4,0},{8,4},{12,8},{16,12},{20,16},{24,20},{28,24},{1,29},{... | collective-permute-start | bytes 294920 | tf_op jit(solution)/shard_map/ppermute | solution.py:382
  7.3 12.1 %copy-start.1 = (f32[2,3136]{1,0:T(2,128)S(1)}, f32[2,3136]{1,0:T(2,128)}, u32[]{:S(2)}) copy-start(f32[2,3136]{1,0:T(2,128)} %param.17) | copy-start | bytes 75268
  14.5 4.0 %collective-permute-start.6 = (bf16[2,3136]{1,0:T(2,128)(2,1)S(1)}, bf16[2,3136]{1,0:T(2,128)(2,1)S(1)}, u32[]{:S(2)}, u32[]{:S(2)}) collective-permute-start(bf16[2,3136]{1,0:T(2,128)(2,1)S(1)} %finish.1), channel_id=1, source_target_pairs={{0,3},{1,2},{2,1},{3,0},{4,7},{5,6},{6,5},{7,4},{8,11},{9,10},{10,... | collective-permute-start | bytes 37640 | tf_op jit(solution)/shard_map/ppermute | solution.py:343
  16.8 2.7 %collective-permute-start.5 = (bf16[2,3136]{1,0:T(2,128)(2,1)S(1)}, bf16[2,3136]{1,0:T(2,128)(2,1)S(1)}, u32[]{:S(2)}, u32[]{:S(2)}) collective-permute-start(bf16[2,3136]{1,0:T(2,128)(2,1)S(1)} %finish.1), channel_id=1, source_target_pairs={{0,2},{1,3},{2,0},{3,1},{4,6},{5,7},{6,4},{7,5},{8,10},{9,11},{10,... | collective-permute-start | bytes 37640 | tf_op jit(solution)/shard_map/ppermute | solution.py:343
  17.0 2.5 %collective-permute-start.4 = (bf16[2,3136]{1,0:T(2,128)(2,1)S(1)}, bf16[2,3136]{1,0:T(2,128)(2,1)S(1)}, u32[]{:S(2)}, u32[]{:S(2)}) collective-permute-start(bf16[2,3136]{1,0:T(2,128)(2,1)S(1)} %finish.1), channel_id=1, source_target_pairs={{0,1},{1,0},{2,3},{3,2},{4,5},{5,4},{6,7},{7,6},{8,9},{9,8},{10,11... | collective-permute-start | bytes 37640 | tf_op jit(solution)/shard_map/ppermute | solution.py:343

commit v7 on v6

--- a/solution.py
+++ b/solution.py
@@ -106,9 +106,13 @@
     mine = domain == me
     spans = [slice(k * width, (k + 1) * width) for k in range(len(SHIFTS))]
     hots = slot_hot([mine[:, s] for s in spans])
-    rows = iota((owned, width), 0)
+    rows = iota((owned, width), 0).astype(F32).astype(BF16)
     chosen = [
-        matmul(hot, ones_where(local[:, s] == rows), ((1,), (1,))).astype(BF16)
+        matmul(
+            hot,
+            jnp.where(local[:, s].astype(F32).astype(BF16) == rows, BF16(1), BF16(0)),
+            ((1,), (1,)),
+        ).astype(BF16)
         for hot, s in zip(hots, spans)
     ]
     copies[2].wait()
@@ -351,11 +355,11 @@
     single_site, coupling, angular, phases, contour, radial, neighbours, owner_row, old_potential
 ):
     site = single_site[0]
-    _, width = site.shape
+    owned, width = site.shape
     count, zones, places = neighbours.shape
     terms = angular.shape[0]
     atoms = owner_row.shape[0]
-    assert atoms <= 65536 and places <= LANES and zones == 2
+    assert owned <= 256 and atoms <= 65536 and places <= LANES and zones == 2
     assert count > 2 * REACH and sorted(SHIFTS) == [k for k in range(-REACH, REACH + 1) if k]
     assert width == 1024 and terms == 4 and atoms % LANES == 0 and places % 2 == 1
     table = owner_row.reshape(atoms // LANES, LANES)

time: 20.3 us -> 20.3 us (level)
  no operation moved by 1% of the time
where the time goes in v7:
time: 20.3 us; the launch traced here: 20.1 us
  starting transfers between devices  7.6 us (37%)
  Pallas kernels  5.89 us (29%)
  waiting for transfers between devices  5.28 us (26%)
  between operations  0.7 us (3%)
  other arithmetic  0.67 us (3%)
    ppermute x4, starting transfers between devices, shards(): lax.ppermute(pack, 'dom', [(i, (i + shift) % count) for i in range(count)])  4.84 us
    ppermute x4, waiting for transfers between devices, shards(): lax.ppermute(pack, 'dom', [(i, (i + shift) % count) for i in range(count)])  3.04 us
    ppermute x3, starting transfers between devices, sum_over(): lax.ppermute(value, axis, [(i, i ^ stride * k) for i in range(size)])  2.76 us
    pallas_call x1, Pallas kernels, shards(): pl.pallas_call(functools.partial(prepare_kernel, 'dom'), out_shape=[pltpu...  2.27 us
    ppermute x3, waiting for transfers between devices, sum_over(): lax.ppermute(value, axis, [(i, i ^ stride * k) for i in range(size)])  2.24 us
    pallas_call x1, Pallas kernels, shards(): pl.pallas_call(functools.partial(pack_kernel, 'dom', len(sources)), out_s...  1.81 us
    pallas_call x1, Pallas kernels, shards(): pl.pallas_call(functools.partial(finish_kernel, len(pieces)), out_shape=p...  1.81 us
    add x1, other arithmetic, shards(): 0.5 * old_potential + 0.5 * density * lax.rsqrt(1.0 + density * density)  0.67 us
  transfers between devices with their start and end apart: 7, of which 4 were waited for; matrix products, arithmetic and copies ran while one was open for 0% of the time, Pallas kernels for 11%

profile of v7, /device:TPU:3, one launch (start us, length us, event | category | flops | bytes accessed | tf_op | source)
XLA Modules:
  0.0 20.1 jit_solution(529939740931642883)
XLA Ops:
  0.0 0.0 copy-start
  0.0 1.8 %pack.1 = (s32[8,2,65]{2,1,0:T(2,128)S(1)}, s32[16,128]{1,0:T(8,128)S(1)}, bf16[256,1024]{1,0:T(8,128)(2,1)S(1)}, bf16[2,4,4225]{2,1,0:T(4,128)(2,1)S(1)}, bf16[...) custom-call(s32[8,2,65]{2,1,0:T(2,128)} %refs_0_.1, ...), custom_call_target="tpu_custom_call" | custom-call | flops 5000000000 | tf_op jit(solution)/shard_map/pack/pallas_call | solution.py:370
  1.8 1.3 %collective-permute-start = (bf16[48,1024]{1,0:T(8,128)(2,1)S(1)}, bf16[48,1024]{1,0:T(8,128)(2,1)S(1)}, u32[]{:S(2)}, u32[]{:S(2)}) collective-permute-start(bf16[48,1024]{1,0:T(8,128)(2,1)S(1)} %get-tuple-element.22), channel_id=1, source_target_pairs={{0,4},{4,8},{8,12},{12,16},{16,20},{20,24},{24,28},{28,0},{1,5},{5... | collective-permute-start | bytes 294920 | tf_op jit(solution)/shard_map/ppermute | solution.py:386
  3.1 1.3 %collective-permute-start.1 = (bf16[48,1024]{1,0:T(8,128)(2,1)S(1)}, bf16[48,1024]{1,0:T(8,128)(2,1)S(1)}, u32[]{:S(2)}, u32[]{:S(2)}) collective-permute-start(bf16[48,1024]{1,0:T(8,128)(2,1)S(1)} %get-tuple-element.23), channel_id=1, source_target_pairs={{0,8},{4,12},{8,16},{12,20},{16,24},{20,28},{24,0},{28,4},{1,9},{5... | collective-permute-start | bytes 294920 | tf_op jit(solution)/shard_map/ppermute | solution.py:386
  4.4 2.0 %collective-permute-start.2 = (bf16[48,1024]{1,0:T(8,128)(2,1)S(1)}, bf16[48,1024]{1,0:T(8,128)(2,1)S(1)}, u32[]{:S(2)}, u32[]{:S(2)}) collective-permute-start(bf16[48,1024]{1,0:T(8,128)(2,1)S(1)} %get-tuple-element.24), channel_id=1, source_target_pairs={{0,24},{4,28},{8,0},{12,4},{16,8},{20,12},{24,16},{28,20},{1,25},{... | collective-permute-start | bytes 294920 | tf_op jit(solution)/shard_map/ppermute | solution.py:386
  6.4 0.3 %collective-permute-start.3 = (bf16[48,1024]{1,0:T(8,128)(2,1)S(1)}, bf16[48,1024]{1,0:T(8,128)(2,1)S(1)}, u32[]{:S(2)}, u32[]{:S(2)}) collective-permute-start(bf16[48,1024]{1,0:T(8,128)(2,1)S(1)} %get-tuple-element.25), channel_id=1, source_target_pairs={{0,28},{4,0},{8,4},{12,8},{16,12},{20,16},{24,20},{28,24},{1,29},{... | collective-permute-start | bytes 294920 | tf_op jit(solution)/shard_map/ppermute | solution.py:386
  7.3 0.0 copy-done
  7.3 0.0 copy-start.1
  7.3 2.3 %prepare.1 = (bf16[128,192]{1,0:T(8,128)(2,1)S(1)}, f32[64,1024]{1,0:T(8,128)S(1)}, bf16[1024,128]{1,0:T(8,128)(2,1)S(1)}, f32[128,256]{1,0:T(8,128)S(1)}, f32[1...) custom-call(s32[8,2,65]{2,1,0:T(2,128)S(1)} %get-tuple-element.26.nbr_ref, ...), custom_call_target="tpu_custom_call" | custom-call | tf_op jit(solution)/shard_map/prepare/pallas_call | solution.py:391
  9.6 0.0 collective-permute-done.refs_0_
  9.6 0.2 collective-permute-done.1.refs_1_
  9.8 2.8 %collective-permute-done.2.refs_2_ = bf16[48,1024]{1,0:T(8,128)(2,1)S(1)} collective-permute-done((bf16[48,1024]{1,0:T(8,128)(2,1)S(1)}, bf16[48,1024]{1,0:T(8,128)(2,1)S(1)}, u32[]{:S(2)}, u32[]{:S(2)}) %collective-permute-start.2) | collective-permute-done | bytes 98336 | tf_op jit(solution)/shard_map/ppermute | solution.py:386
  12.7 0.0 collective-permute-done.3.refs_3_
  12.7 1.8 %finish.1 = bf16[2,3136]{1,0:T(2,128)(2,1)S(1)} custom-call(bf16[48,1024]{1,0:T(8,128)(2,1)S(1)} %collective-permute-done.refs_0_, bf16[48,1024]{1,0:T(8,128)(2,1)S(1)} %collective-permute-done.1.refs_1_, bf16[48,1024]{1,0:T(8,128)(2,1)S(1)} %collective-permute-done.2.refs_2_, bf16[48,1024]{1,0:T(8,128)(2,1)S(1)} %collective-permute-done.3.refs_3_, ...), custom_call_target="tpu_custom_call" | custom-call | tf_op jit(solution)/shard_map/finish/pallas_call | solution.py:414
  14.5 2.3 %collective-permute-start.6 = (bf16[2,3136]{1,0:T(2,128)(2,1)S(1)}, bf16[2,3136]{1,0:T(2,128)(2,1)S(1)}, u32[]{:S(2)}, u32[]{:S(2)}) collective-permute-start(bf16[2,3136]{1,0:T(2,128)(2,1)S(1)} %finish.1), channel_id=1, source_target_pairs={{0,3},{1,2},{2,1},{3,0},{4,7},{5,6},{6,5},{7,4},{8,11},{9,10},{10,... | collective-permute-start | bytes 37640 | tf_op jit(solution)/shard_map/ppermute | solution.py:347
  16.8 0.2 %collective-permute-start.5 = (bf16[2,3136]{1,0:T(2,128)(2,1)S(1)}, bf16[2,3136]{1,0:T(2,128)(2,1)S(1)}, u32[]{:S(2)}, u32[]{:S(2)}) collective-permute-start(bf16[2,3136]{1,0:T(2,128)(2,1)S(1)} %finish.1), channel_id=1, source_target_pairs={{0,2},{1,3},{2,0},{3,1},{4,6},{5,7},{6,4},{7,5},{8,10},{9,11},{10,... | collective-permute-start | bytes 37640 | tf_op jit(solution)/shard_map/ppermute | solution.py:347
  17.0 0.2 %collective-permute-start.4 = (bf16[2,3136]{1,0:T(2,128)(2,1)S(1)}, bf16[2,3136]{1,0:T(2,128)(2,1)S(1)}, u32[]{:S(2)}, u32[]{:S(2)}) collective-permute-start(bf16[2,3136]{1,0:T(2,128)(2,1)S(1)} %finish.1), channel_id=1, source_target_pairs={{0,1},{1,0},{2,3},{3,2},{4,5},{5,4},{6,7},{7,6},{8,9},{9,8},{10,11... | collective-permute-start | bytes 37640 | tf_op jit(solution)/shard_map/ppermute | solution.py:347
  17.2 1.2 %collective-permute-done.6 = bf16[2,3136]{1,0:T(2,128)(2,1)S(1)} collective-permute-done((bf16[2,3136]{1,0:T(2,128)(2,1)S(1)}, bf16[2,3136]{1,0:T(2,128)(2,1)S(1)}, u32[]{:S(2)}, u32[]{:S(2)}) %collective-permute-start.6) | collective-permute-done | bytes 12576 | tf_op jit(solution)/shard_map/ppermute | solution.py:347
  18.4 1.0 %collective-permute-done.5 = bf16[2,3136]{1,0:T(2,128)(2,1)S(1)} collective-permute-done((bf16[2,3136]{1,0:T(2,128)(2,1)S(1)}, bf16[2,3136]{1,0:T(2,128)(2,1)S(1)}, u32[]{:S(2)}, u32[]{:S(2)}) %collective-permute-start.5) | collective-permute-done | bytes 12576 | tf_op jit(solution)/shard_map/ppermute | solution.py:347
  19.5 0.0 collective-permute-done.4
  19.5 0.0 copy-done.1
  19.5 0.7 %multiply_add_fusion = f32[2,3136]{1,0:T(2,128)} fusion(bf16[2,3136]{1,0:T(2,128)(2,1)S(1)} %collective-permute-done.6, bf16[2,3136]{1,0:T(2,128)(2,1)S(1)} %collective-permute-done.5, bf16[2,3136]{1,0:T(2,128)(2,1)S(1)} %collective-permute-done.4, bf16[2,3136]{1,0:T(2,128)(2,1)S(1)} %finish.1, f32[2,3136]{1,0:T(2,128)S(1)} %copy-done.1), kind=kLoop, calls=%fused_computation | loop fusion | flops 81536 | bytes 100352 | tf_op jit(solution)/shard_map/add | solution.py:426
Async XLA Ops:
  0.0 7.3 %copy-start = (bf16[1,1024,3136]{1,2,0:T(8,128)(2,1)S(1)}, bf16[1,1024,3136]{1,2,0:T(8,128)(2,1)}, u32[]{:S(2)}) copy-start(bf16[1,1024,3136]{1,2,0:T(8,128)(2,1)} %param.14) | copy-start | bytes 19267588
  1.8 7.8 %collective-permute-start = (bf16[48,1024]{1,0:T(8,128)(2,1)S(1)}, bf16[48,1024]{1,0:T(8,128)(2,1)S(1)}, u32[]{:S(2)}, u32[]{:S(2)}) collective-permute-start(bf16[48,1024]{1,0:T(8,128)(2,1)S(1)} %get-tuple-element.22), channel_id=1, source_target_pairs={{0,4},{4,8},{8,12},{12,16},{16,20},{20,24},{24,28},{28,0},{1,5},{5... | collective-permute-start | bytes 294920 | tf_op jit(solution)/shard_map/ppermute | solution.py:386
  3.1 6.7 %collective-permute-start.1 = (bf16[48,1024]{1,0:T(8,128)(2,1)S(1)}, bf16[48,1024]{1,0:T(8,128)(2,1)S(1)}, u32[]{:S(2)}, u32[]{:S(2)}) collective-permute-start(bf16[48,1024]{1,0:T(8,128)(2,1)S(1)} %get-tuple-element.23), channel_id=1, source_target_pairs={{0,8},{4,12},{8,16},{12,20},{16,24},{20,28},{24,0},{28,4},{1,9},{5... | collective-permute-start | bytes 294920 | tf_op jit(solution)/shard_map/ppermute | solution.py:386
  4.4 8.2 %collective-permute-start.2 = (bf16[48,1024]{1,0:T(8,128)(2,1)S(1)}, bf16[48,1024]{1,0:T(8,128)(2,1)S(1)}, u32[]{:S(2)}, u32[]{:S(2)}) collective-permute-start(bf16[48,1024]{1,0:T(8,128)(2,1)S(1)} %get-tuple-element.24), channel_id=1, source_target_pairs={{0,24},{4,28},{8,0},{12,4},{16,8},{20,12},{24,16},{28,20},{1,25},{... | collective-permute-start | bytes 294920 | tf_op jit(solution)/shard_map/ppermute | solution.py:386
  6.4 6.3 %collective-permute-start.3 = (bf16[48,1024]{1,0:T(8,128)(2,1)S(1)}, bf16[48,1024]{1,0:T(8,128)(2,1)S(1)}, u32[]{:S(2)}, u32[]{:S(2)}) collective-permute-start(bf16[48,1024]{1,0:T(8,128)(2,1)S(1)} %get-tuple-element.25), channel_id=1, source_target_pairs={{0,28},{4,0},{8,4},{12,8},{16,12},{20,16},{24,20},{28,24},{1,29},{... | collective-permute-start | bytes 294920 | tf_op jit(solution)/shard_map/ppermute | solution.py:386
  7.3 12.2 %copy-start.1 = (f32[2,3136]{1,0:T(2,128)S(1)}, f32[2,3136]{1,0:T(2,128)}, u32[]{:S(2)}) copy-start(f32[2,3136]{1,0:T(2,128)} %param.17) | copy-start | bytes 75268
  14.5 4.0 %collective-permute-start.6 = (bf16[2,3136]{1,0:T(2,128)(2,1)S(1)}, bf16[2,3136]{1,0:T(2,128)(2,1)S(1)}, u32[]{:S(2)}, u32[]{:S(2)}) collective-permute-start(bf16[2,3136]{1,0:T(2,128)(2,1)S(1)} %finish.1), channel_id=1, source_target_pairs={{0,3},{1,2},{2,1},{3,0},{4,7},{5,6},{6,5},{7,4},{8,11},{9,10},{10,... | collective-permute-start | bytes 37640 | tf_op jit(solution)/shard_map/ppermute | solution.py:347
  16.8 2.7 %collective-permute-start.5 = (bf16[2,3136]{1,0:T(2,128)(2,1)S(1)}, bf16[2,3136]{1,0:T(2,128)(2,1)S(1)}, u32[]{:S(2)}, u32[]{:S(2)}) collective-permute-start(bf16[2,3136]{1,0:T(2,128)(2,1)S(1)} %finish.1), channel_id=1, source_target_pairs={{0,2},{1,3},{2,0},{3,1},{4,6},{5,7},{6,4},{7,5},{8,10},{9,11},{10,... | collective-permute-start | bytes 37640 | tf_op jit(solution)/shard_map/ppermute | solution.py:347
  17.0 2.5 %collective-permute-start.4 = (bf16[2,3136]{1,0:T(2,128)(2,1)S(1)}, bf16[2,3136]{1,0:T(2,128)(2,1)S(1)}, u32[]{:S(2)}, u32[]{:S(2)}) collective-permute-start(bf16[2,3136]{1,0:T(2,128)(2,1)S(1)} %finish.1), channel_id=1, source_target_pairs={{0,1},{1,0},{2,3},{3,2},{4,5},{5,4},{6,7},{7,6},{8,9},{9,8},{10,11... | collective-permute-start | bytes 37640 | tf_op jit(solution)/shard_map/ppermute | solution.py:347
